TPU v7x, 128 devices: a whole 4x4x4 slice. The times are simulated.
128 devices in a mesh: dp: 128 (over z, y, x, core).
Axes of the slice: x: 4, y: 4, z: 4, core: 2. Of those that a mesh axis runs over, the one named last changes fastest.
Arguments:
- x_rows: bfloat16 [131072, 512], P('dp')
- dy_rows: bfloat16 [131072, 512], P('dp')
- w_one: bfloat16 [512, 8192], replicated
- w_two: bfloat16 [8192, 512], replicated
- w_three: bfloat16 [512, 2048], replicated
- w_four: bfloat16 [2048, 512], replicated
- master_one: float32 [512, 8192], P('dp')
- master_two: float32 [8192, 512], P('dp')
- master_three: float32 [512, 2048], P('dp')
- master_four: float32 [2048, 512], P('dp')
- m_one: float32 [512, 8192], P('dp')
- m_two: float32 [8192, 512], P('dp')
- m_three: float32 [512, 2048], P('dp')
- m_four: float32 [2048, 512], P('dp')
- v_one: float32 [512, 8192], P('dp')
- v_two: float32 [8192, 512], P('dp')
- v_three: float32 [512, 2048], P('dp')
- v_four: float32 [2048, 512], P('dp')
- learn_rate: float32 [], replicated
- clip_max: float32 [], replicated
Outputs:
- output 1: bfloat16 [512, 8192], replicated
- output 2: bfloat16 [8192, 512], replicated
- output 3: bfloat16 [512, 2048], replicated
- output 4: bfloat16 [2048, 512], replicated
- output 5: float32 [512, 8192], P('dp')
- output 6: float32 [8192, 512], P('dp')
- output 7: float32 [512, 2048], P('dp')
- output 8: float32 [2048, 512], P('dp')
- output 9: float32 [512, 8192], P('dp')
- output 10: float32 [8192, 512], P('dp')
- output 11: float32 [512, 2048], P('dp')
- output 12: float32 [2048, 512], P('dp')
- output 13: float32 [512, 8192], P('dp')
- output 14: float32 [8192, 512], P('dp')
- output 15: float32 [512, 2048], P('dp')
- output 16: float32 [2048, 512], P('dp')
- output 17: float32 [], replicated
All inputs are finite; a program needn't handle non-finite values.
Results may differ from a plain program's by a relative error of at most 0.0112006.
Values are sent between devices in bfloat16 or wider.
A program may use at most 1 GiB of HBM per device.

v0:
```python
import jax
import jax.numpy as jnp
from jax import lax
from jax.sharding import PartitionSpec as P

ADAM_STEP = 10
BETA_ONE = 0.9
BETA_TWO = 0.95
ADAM_EPS = 1e-8
NORM_EPS = 1e-6
BIAS_ONE = 1.0 - BETA_ONE ** ADAM_STEP
BIAS_TWO = 1.0 - BETA_TWO ** ADAM_STEP
INV_SQRT2 = 0.7071067811865476
INV_SQRT2PI = 0.3989422804014327


def gelu_value(pre_act):
    pre_wide = pre_act.astype(jnp.float32)
    return 0.5 * pre_wide * (1.0 + lax.erf(pre_wide * INV_SQRT2))


def gelu_slope(pre_act):
    pre_wide = pre_act.astype(jnp.float32)
    return 0.5 * (1.0 + lax.erf(pre_wide * INV_SQRT2)) + pre_wide * INV_SQRT2PI * jnp.exp(-0.5 * pre_wide * pre_wide)


def local_grads(x_rows, dy_rows, w_one, w_two, w_three, w_four):
    z_one = jnp.dot(x_rows, w_one, preferred_element_type=jnp.float32).astype(jnp.bfloat16)
    a_one = gelu_value(z_one).astype(jnp.bfloat16)
    h_two = jnp.dot(a_one, w_two, preferred_element_type=jnp.float32).astype(jnp.bfloat16)
    z_three = jnp.dot(h_two, w_three, preferred_element_type=jnp.float32).astype(jnp.bfloat16)
    a_three = gelu_value(z_three).astype(jnp.bfloat16)
    g_four = jnp.einsum('rf,rd->fd', a_three, dy_rows, preferred_element_type=jnp.float32)
    da_three = jnp.einsum('rd,fd->rf', dy_rows, w_four, preferred_element_type=jnp.float32).astype(jnp.bfloat16)
    dz_three = (da_three.astype(jnp.float32) * gelu_slope(z_three)).astype(jnp.bfloat16)
    g_three = jnp.einsum('rd,rf->df', h_two, dz_three, preferred_element_type=jnp.float32)
    dh_two = jnp.einsum('rf,df->rd', dz_three, w_three, preferred_element_type=jnp.float32).astype(jnp.bfloat16)
    g_two = jnp.einsum('rw,rd->wd', a_one, dh_two, preferred_element_type=jnp.float32)
    da_one = jnp.einsum('rd,wd->rw', dh_two, w_two, preferred_element_type=jnp.float32).astype(jnp.bfloat16)
    dz_one = (da_one.astype(jnp.float32) * gelu_slope(z_one)).astype(jnp.bfloat16)
    g_one = jnp.einsum('rd,rw->dw', x_rows, dz_one, preferred_element_type=jnp.float32)
    return g_one, g_two, g_three, g_four


def adam_rows(grad_mat, master_mat, mom_mat, var_mat, clip_scale, learn_rate):
    scaled = clip_scale * grad_mat
    mom_new = BETA_ONE * mom_mat + (1.0 - BETA_ONE) * scaled
    var_new = BETA_TWO * var_mat + (1.0 - BETA_TWO) * scaled * scaled
    master_new = master_mat - learn_rate * (mom_new / BIAS_ONE) / (jnp.sqrt(var_new / BIAS_TWO) + ADAM_EPS)
    return master_new, mom_new, var_new


def solution(mesh):
    dp_size = mesh.shape['dp']
    row_spec = P('dp', None)
    rep_spec = P()

    def per_device(x_rows, dy_rows, w_one, w_two, w_three, w_four, master_one, master_two, master_three, master_four, m_one, m_two, m_three, m_four, v_one, v_two, v_three, v_four, learn_rate, clip_max):
        grads = local_grads(x_rows, dy_rows, w_one, w_two, w_three, w_four)
        shards = [lax.psum_scatter(grad_mat, 'dp', scatter_dimension=0, tiled=True) / dp_size for grad_mat in grads]
        local_sq = sum(jnp.sum(shard_mat * shard_mat) for shard_mat in shards)
        grad_norm = jnp.sqrt(lax.psum(local_sq, 'dp'))
        clip_scale = jnp.minimum(1.0, clip_max / (grad_norm + NORM_EPS))
        results = [adam_rows(shard_mat, master_mat, mom_mat, var_mat, clip_scale, learn_rate) for shard_mat, master_mat, mom_mat, var_mat in zip(shards, (master_one, master_two, master_three, master_four), (m_one, m_two, m_three, m_four), (v_one, v_two, v_three, v_four))]
        new_weights = tuple(lax.all_gather(result[0].astype(jnp.bfloat16), 'dp', axis=0, tiled=True) for result in results)
        return new_weights + tuple(result[0] for result in results) + tuple(result[1] for result in results) + tuple(result[2] for result in results) + (grad_norm,)

    in_specs = (row_spec, row_spec) + (rep_spec,) * 4 + (row_spec,) * 12 + (rep_spec, rep_spec)
    out_specs = (rep_spec,) * 4 + (row_spec,) * 12 + (rep_spec,)
    return jax.shard_map(per_device, mesh=mesh, in_specs=in_specs, out_specs=out_specs, check_vma=False)
```

profile of v0, /device:TPU:1, one launch (start us, length us, event | category | flops | bytes accessed | tf_op | source)
XLA Modules:
  0.0 1961.7 jit_solution(14100784518407644965)
XLA Ops:
  7.3 21.3 %fusion.3 = (f32[1024,8192]{1,0:T(8,128)}, bf16[1024,8192]{1,0:T(8,128)(2,1)}) fusion(bf16[1024,512]{1,0:T(8,128)(2,1)} %param.20, bf16[512,8192]{1,0:T(8,128)(2,1)} %param.22), kind=kOutput, calls=%fused_computation.8 | convolution fusion | flops 8623489024 | bytes 59768832 | tf_op jit(solution)/shard_map/dot_general | solution.py:28
  28.6 21.0 %convolution_convert_fusion.2 = bf16[1024,512]{1,0:T(8,128)(2,1)S(1)} fusion(bf16[8192,512]{1,0:T(8,128)(2,1)} %param.23, f32[1024,8192]{1,0:T(8,128)} %get-tuple-element.88, bf16[1024,8192]{1,0:T(8,128)(2,1)} %get-tuple-element.89), kind=kOutput, calls=%fused_computation.36 | convolution fusion | flops 8624013312 | bytes 59768832 | tf_op jit(solution)/shard_map/dot_general | solution.py:30
  49.7 2.3 convolution_convert_fusion.1
  52.0 2.0 copy-done.17
  54.0 4.2 fusion.25
  58.5 6.8 fusion.21
  65.3 4.4 fusion.46
  69.7 2.4 convolution_convert_fusion.3
  72.1 32.7 %fusion.11 = f32[512,8192]{0,1:T(8,128)} fusion(bf16[1024,512]{1,0:T(8,128)(2,1)} %param.20, bf16[1024,8192]{1,0:T(8,128)(2,1)} %get-tuple-element.89, f32[1024,8192]{1,0:T(8,128)} %get-tuple-element.88, bf16[1024,512]{1,0:T(8,128)(2,1)S(1)} %convolution_convert_fusion.3, bf16[8192,512]{1,0:T(8,128)(2,1)} %param.23), kind=kOutput, calls=%fused_computation.21 | convolution fusion | flops 17272143872 | bytes 77594624 | tf_op jit(solution)/shard_map/rd,rw->dw/dot_general | solution.py:41
  105.1 24.7 %fusion.36 = f32[8192,512]{1,0:T(8,128)} fusion(bf16[1024,512]{1,0:T(8,128)(2,1)S(1)} %convolution_convert_fusion.3, f32[1024,8192]{1,0:T(8,128)} %get-tuple-element.88, bf16[1024,8192]{1,0:T(8,128)(2,1)} %get-tuple-element.89), kind=kOutput, calls=%fused_computation.64 | convolution fusion | flops 8623489024 | bytes 68157440 | tf_op jit(solution)/shard_map/rw,rd->wd/dot_general | solution.py:38
  131.4 573.1 %reduce-scatter.6.cloned.1.call-done = f32[16,512]{1,0:T(8,128)} async-done(((f32[2048,512]{1,0:T(8,128)}), f32[16,512]{1,0:T(8,128)}) %reduce-scatter.6.cloned.1.call-update) | async-done | bytes 32784 | tf_op jit(solution)/shard_map/reduce_scatter | solution.py:60
  706.0 227.4 %all-reduce.5.cloned.1.call-done = (f32[512,8192]{0,1:T(8,128)}, f32[512,2048]{1,0:T(8,128)}) async-done(((f32[512,8192]{0,1:T(8,128)}, f32[512,2048]{1,0:T(8,128)}), (f32[512,8192]{0,1:T(8,128)}, f32[512,2048]{1,0:T(8,128)})) %all-reduce.5.cloned.1.call-update) | async-done | bytes 20971536
  934.9 5.9 multiply_reduce_fusion
  940.8 658.5 %reduce-scatter.4.cloned.1.call-done = f32[64,512]{1,0:T(8,128)} async-done(((f32[8192,512]{1,0:T(8,128)}), f32[64,512]{1,0:T(8,128)}) %reduce-scatter.4.cloned.1.call-update) | async-done | bytes 131088 | tf_op jit(solution)/shard_map/reduce_scatter | solution.py:60
  1603.5 69.3 %psum.7 = f32[]{:T(128)} all-reduce(f32[]{:T(128)S(6)} %add.90), channel_id=1, replica_groups=mesh['dp'=128] {'dp'}, use_global_device_ids=true, to_apply=%region_8.0 | all-reduce | flops 1 | bytes 8 | tf_op jit(solution)/shard_map/psum | solution.py:62
  1676.0 2.8 copy.63
  1679.9 1.7 fusion.43
  1681.6 55.8 %all-gather.13.cloned.1.call-done = bf16[128,4,2048]{2,1,0:T(4,128)(2,1)} async-done(((bf16[1,4,2048]{2,1,0:T(4,128)(2,1)}), bf16[128,4,2048]{2,1,0:T(4,128)(2,1)}) %all-gather.13.cloned.1.call-update) | async-done | bytes 2097168 | tf_op jit(solution)/shard_map/all_gather | solution.py:65
  1737.4 3.9 reshape.37
  1741.3 62.4 %all-gather.9.cloned.1.call-done = bf16[2048,512]{1,0:T(8,128)(2,1)} async-done(((bf16[16,512]{1,0:T(8,128)(2,1)}), bf16[2048,512]{1,0:T(8,128)(2,1)}) %all-gather.9.cloned.1.call-update) | async-done | bytes 2097168 | tf_op jit(solution)/shard_map/all_gather | solution.py:65
  1803.7 70.4 %all-gather.11.cloned.1.call-done = bf16[128,4,8192]{2,1,0:T(4,128)(2,1)} async-done(((bf16[1,4,8192]{2,1,0:T(4,128)(2,1)}), bf16[128,4,8192]{2,1,0:T(4,128)(2,1)}) %all-gather.11.cloned.1.call-update) | async-done | bytes 8388624 | tf_op jit(solution)/shard_map/all_gather | solution.py:65
  1874.1 12.4 reshape.35
  1886.6 58.3 %all-gather.7.cloned.1.call-done = bf16[8192,512]{1,0:T(8,128)(2,1)} async-done(((bf16[64,512]{1,0:T(8,128)(2,1)}), bf16[8192,512]{1,0:T(8,128)(2,1)}) %all-gather.7.cloned.1.call-update) | async-done | bytes 8388624 | tf_op jit(solution)/shard_map/all_gather | solution.py:65
  1944.9 7.5 copy.72
  (56 shorter events, 9.8 us)
Async XLA Ops:
  7.2 42.4 %copy-start = (bf16[512,2048]{1,0:T(8,128)(2,1)S(1)}, bf16[512,2048]{1,0:T(8,128)(2,1)}, u32[]{:S(2)}) copy-start(bf16[512,2048]{1,0:T(8,128)(2,1)} %param.24) | copy-start | bytes 6291460
  7.2 697.4 %reduce-scatter.6.cloned.1.call-start = ((), (), s32[]{:S(2)}) async-start(), calls=%async_computation.3 | async-start | bytes 4227072 | tf_op jit(solution)/shard_map/reduce_scatter | solution.py:60
  49.6 4.4 copy-start.16
  58.3 875.2 %all-reduce.5.cloned.1.call-start = ((), (), s32[]{:S(2)}) async-start(), calls=%async_computation.8 | async-start | bytes 41943040
  104.8 1494.5 %reduce-scatter.4.cloned.1.call-start = ((), (), s32[]{:S(2)}) async-start(), calls=%async_computation.2 | async-start | bytes 16908288 | tf_op jit(solution)/shard_map/reduce_scatter | solution.py:60
  129.8 1543.8 %copy-start.10 = (f32[4,2048]{1,0:T(4,128)S(1)}, f32[4,2048]{1,0:T(4,128)}, u32[]{:S(2)}) copy-start(f32[4,2048]{1,0:T(4,128)} %param.28) | copy-start | bytes 98308
  129.8 1543.8 %copy-start.11 = (f32[4,2048]{1,0:T(4,128)S(1)}, f32[4,2048]{1,0:T(4,128)}, u32[]{:S(2)}) copy-start(f32[4,2048]{1,0:T(4,128)} %param.32) | copy-start | bytes 98308
  129.8 1543.8 %copy-start.12 = (f32[4,2048]{1,0:T(4,128)S(1)}, f32[4,2048]{1,0:T(4,128)}, u32[]{:S(2)}) copy-start(f32[4,2048]{1,0:T(4,128)} %param.36) | copy-start | bytes 98308
  129.8 1545.4 %copy-start.13 = (f32[16,512]{1,0:T(8,128)S(1)}, f32[16,512]{1,0:T(8,128)}, u32[]{:S(2)}) copy-start(f32[16,512]{1,0:T(8,128)} %param.29) | copy-start | bytes 98308
  129.8 1545.4 %copy-start.14 = (f32[16,512]{1,0:T(8,128)S(1)}, f32[16,512]{1,0:T(8,128)}, u32[]{:S(2)}) copy-start(f32[16,512]{1,0:T(8,128)} %param.33) | copy-start | bytes 98308
  129.8 1545.4 %copy-start.15 = (f32[16,512]{1,0:T(8,128)S(1)}, f32[16,512]{1,0:T(8,128)}, u32[]{:S(2)}) copy-start(f32[16,512]{1,0:T(8,128)} %param.37) | copy-start | bytes 98308
  129.8 1549.0 %copy-start.3 = (f32[4,8192]{1,0:T(4,128)S(1)}, f32[4,8192]{1,0:T(4,128)}, u32[]{:S(2)}) copy-start(f32[4,8192]{1,0:T(4,128)} %param.26) | copy-start | bytes 393220
  129.9 1549.0 %copy-start.4 = (f32[4,8192]{1,0:T(4,128)S(1)}, f32[4,8192]{1,0:T(4,128)}, u32[]{:S(2)}) copy-start(f32[4,8192]{1,0:T(4,128)} %param.30) | copy-start | bytes 393220
  129.9 1549.0 %copy-start.5 = (f32[4,8192]{1,0:T(4,128)S(1)}, f32[4,8192]{1,0:T(4,128)}, u32[]{:S(2)}) copy-start(f32[4,8192]{1,0:T(4,128)} %param.34) | copy-start | bytes 393220
  129.9 1550.0 %copy-start.6 = (f32[64,512]{1,0:T(8,128)S(1)}, f32[64,512]{1,0:T(8,128)}, u32[]{:S(2)}) copy-start(f32[64,512]{1,0:T(8,128)} %param.27) | copy-start | bytes 393220
  129.9 1550.0 %copy-start.7 = (f32[64,512]{1,0:T(8,128)S(1)}, f32[64,512]{1,0:T(8,128)}, u32[]{:S(2)}) copy-start(f32[64,512]{1,0:T(8,128)} %param.31) | copy-start | bytes 393220
  129.9 1550.0 %copy-start.8 = (f32[64,512]{1,0:T(8,128)S(1)}, f32[64,512]{1,0:T(8,128)}, u32[]{:S(2)}) copy-start(f32[64,512]{1,0:T(8,128)} %param.35) | copy-start | bytes 393220
  129.9 1607.5 %all-gather.13.cloned.1.call-start = ((), (), s32[]{:S(2)}) async-start(), calls=%async_computation.7 | async-start | bytes 2113536 | tf_op jit(solution)/shard_map/all_gather | solution.py:65
  704.6 970.7 %copy-start.9 = (f32[16,512]{1,0:T(8,128)S(1)}, f32[16,512]{1,0:T(8,128)}, u32[]{:S(2)}) copy-start(f32[16,512]{1,0:T(8,128)} %reduce-scatter.6.cloned.1.call-done) | copy-start | bytes 98308
  1675.1 128.6 %all-gather.9.cloned.1.call-start = ((), (), s32[]{:S(2)}) async-start(), calls=%async_computation.5 | async-start | bytes 2113536 | tf_op jit(solution)/shard_map/all_gather | solution.py:65
  1675.9 198.2 %all-gather.11.cloned.1.call-start = ((), (), s32[]{:S(2)}) async-start(), calls=%async_computation.6 | async-start | bytes 8454144 | tf_op jit(solution)/shard_map/all_gather | solution.py:65
  1679.8 265.1 %all-gather.7.cloned.1.call-start = ((), (), s32[]{:S(2)}) async-start(), calls=%async_computation.4 | async-start | bytes 8454144 | tf_op jit(solution)/shard_map/all_gather | solution.py:65
  1944.9 8.8 copy-start.1
  1944.9 7.5 copy-start.2
  (1 other events, 2.0 us)
Sparse Core Ops, SparseCore 0:
  58.4 646.1 reduce-scatter.5
  710.9 222.5 all-reduce.4
  935.8 663.4 reduce-scatter.3
  1675.3 62.0 all-gather.12
  1740.9 62.7 all-gather.8
  1807.1 66.9 all-gather.10
  1877.7 67.1 all-gather.6
where the time goes:
time: 1960 us
  waiting for transfers between devices  1710 us (87%)
  matrix products  120 us (6%)
  blocking collectives  69.3 us (4%)
  local copies, waits for them, and re-layouts  30.2 us (2%)
  between operations  20.3 us (1%)
    reduce_scatter x2, waiting for transfers between devices, per_device(): lax.psum_scatter(grad_mat, 'dp', scatter_dimension=0, tiled=True) / dp_size  1230 us
    all_gather x4, waiting for transfers between devices, per_device(): lax.all_gather(result[0].astype(jnp.bfloat16), 'dp', axis=0, tiled=True)  247 us
    unnamed x8, waiting for transfers between devices  228 us
    psum x1, blocking collectives, per_device(): grad_norm = jnp.sqrt(lax.psum(local_sq, 'dp'))  69.3 us
  transfers between devices with their start and end apart: 7, of which 7 were waited for; matrix products, arithmetic and copies ran while one was open for 5% of the time, Pallas kernels for 0%

commit v1 on v0

v1 whole, which is shorter than its diff:
```python
import functools

import jax
import jax.numpy as jnp
from jax import lax
from jax.experimental import pallas as pl
from jax.experimental.pallas import tpu as pltpu
from jax.sharding import PartitionSpec as P

ADAM_STEP = 10
BETA_ONE = 0.9
BETA_TWO = 0.95
ADAM_EPS = 1e-8
NORM_EPS = 1e-6
BIAS_ONE = 1.0 - BETA_ONE ** ADAM_STEP
BIAS_TWO = 1.0 - BETA_TWO ** ADAM_STEP
INV_SQRT2 = 0.7071067811865476
INV_SQRT2PI = 0.3989422804014327

WIDTH = 512
SIDE = 4
ROWS = 8
UNITS_OF = {3: 2, 4: 2, 2: 8, 1: 8}
SLOTS = 4
MESH_ID = pl.DeviceIdType.MESH
VMEM_BYTES = 62 * 1024 * 1024


def unit_list():
    return [(mat, piece) for mat in (3, 4, 2, 1) for piece in range(UNITS_OF[mat])]


def first_unit(mat):
    return unit_list().index((mat, 0))


def gelu_value(pre_act):
    pre_wide = pre_act.astype(jnp.float32)
    return 0.5 * pre_wide * (1.0 + lax.erf(pre_wide * INV_SQRT2))


def gelu_slope(pre_act):
    pre_wide = pre_act.astype(jnp.float32)
    return 0.5 * (1.0 + lax.erf(pre_wide * INV_SQRT2)) + pre_wide * INV_SQRT2PI * jnp.exp(-0.5 * pre_wide * pre_wide)


def local_grads(x_rows, dy_rows, w_one, w_two, w_three, w_four):
    z_one = jnp.dot(x_rows, w_one, preferred_element_type=jnp.float32).astype(jnp.bfloat16)
    a_one = gelu_value(z_one).astype(jnp.bfloat16)
    h_two = jnp.dot(a_one, w_two, preferred_element_type=jnp.float32).astype(jnp.bfloat16)
    z_three = jnp.dot(h_two, w_three, preferred_element_type=jnp.float32).astype(jnp.bfloat16)
    a_three = gelu_value(z_three).astype(jnp.bfloat16)
    g_four = jnp.einsum('rf,rd->fd', a_three, dy_rows, preferred_element_type=jnp.float32)
    da_three = jnp.einsum('rd,fd->rf', dy_rows, w_four, preferred_element_type=jnp.float32).astype(jnp.bfloat16)
    dz_three = (da_three.astype(jnp.float32) * gelu_slope(z_three)).astype(jnp.bfloat16)
    g_three = jnp.einsum('rd,rf->df', h_two, dz_three, preferred_element_type=jnp.float32)
    dh_two = jnp.einsum('rf,df->rd', dz_three, w_three, preferred_element_type=jnp.float32).astype(jnp.bfloat16)
    g_two = jnp.einsum('rw,rd->wd', a_one, dh_two, preferred_element_type=jnp.float32)
    da_one = jnp.einsum('rd,wd->rw', dh_two, w_two, preferred_element_type=jnp.float32).astype(jnp.bfloat16)
    dz_one = (da_one.astype(jnp.float32) * gelu_slope(z_one)).astype(jnp.bfloat16)
    g_one = jnp.einsum('rd,rw->dw', x_rows, dz_one, preferred_element_type=jnp.float32)
    return g_one, g_two, g_three, g_four


class Place:
    def __init__(self):
        me = lax.axis_index('dp')
        self.core = lax.rem(me, 2)
        self.coords = [lax.div(me, 2 * SIDE * SIDE), lax.rem(lax.div(me, 2 * SIDE), SIDE), lax.rem(lax.div(me, 2), SIDE)]

    def step(self, axis, by):
        return lax.rem(self.coords[axis] + by, SIDE)

    def device(self, moves=None, other_core=False):
        pos = list(self.coords)
        for axis, by in (moves or {}).items():
            pos[axis] = self.step(axis, by)
        core = 1 - self.core if other_core else self.core
        return (((pos[0] * SIDE + pos[1]) * SIDE + pos[2]) * 2 + core,)

    def neighbours(self):
        found = [self.device(other_core=True)]
        for axis in range(3):
            found += [self.device({axis: 1}), self.device({axis: SIDE - 1})]
        return found


def enter(peers):
    barrier = pltpu.get_barrier_semaphore()
    for peer in peers:
        pl.semaphore_signal(barrier, inc=1, device_id=peer, device_id_type=MESH_ID)
    pl.semaphore_wait(barrier, len(peers))


def send(src, dst, send_sem, recv_sem, peer):
    pltpu.make_async_remote_copy(src_ref=src, dst_ref=dst, send_sem=send_sem, recv_sem=recv_sem, device_id=peer, device_id_type=MESH_ID).start()


def await_bytes(ref, sem):
    pltpu.make_async_copy(ref, ref, sem).wait()


def spot(lead, dims, fixed, cols):
    return tuple(lead) + tuple(fixed.get(axis, slice(None)) for axis in dims) + (slice(None), cols)


LEFT = pl.ds(0, WIDTH // 2)
RIGHT = pl.ds(WIDTH // 2, WIDTH // 2)
ALL = slice(None)


class RingSum:
    def __init__(self, place, dims, axis, relay, final, relay_sem, final_sem, send_sem):
        self.place, self.dims, self.axis = place, dims, axis
        self.relay, self.final = relay, final
        self.relay_sem, self.final_sem, self.send_sem = relay_sem, final_sem, send_sem
        self.own = place.coords[axis]
        self.up, self.down, self.far = place.step(axis, 1), place.step(axis, SIDE - 1), place.step(axis, 2)
        self.up_dev, self.down_dev = place.device({axis: 1}), place.device({axis: SIDE - 1})
        self.rest = [dim for dim in dims if dim != axis]

    def start(self, src, lead, unit):
        s = self
        send(src.at[spot(lead, s.dims, {s.axis: s.far}, LEFT)], s.relay.at[unit, 0], s.send_sem.at[unit], s.relay_sem.at[unit], s.up_dev)
        send(src.at[spot(lead, s.dims, {s.axis: s.far}, RIGHT)], s.relay.at[unit, 1], s.send_sem.at[unit], s.relay_sem.at[unit], s.down_dev)
        send(src.at[spot(lead, s.dims, {s.axis: s.up}, RIGHT)], s.final.at[spot((unit, 0), s.rest, {}, RIGHT)], s.send_sem.at[unit], s.final_sem.at[unit], s.up_dev)
        send(src.at[spot(lead, s.dims, {s.axis: s.down}, LEFT)], s.final.at[spot((unit, 1), s.rest, {}, LEFT)], s.send_sem.at[unit], s.final_sem.at[unit], s.down_dev)

    def pass_on(self, src, lead, unit):
        s = self
        await_bytes(s.relay.at[unit], s.relay_sem.at[unit])
        up_spot = spot(lead, s.dims, {s.axis: s.up}, LEFT)
        src[up_spot] = src[up_spot] + s.relay[unit, 0]
        send(src.at[up_spot], s.final.at[spot((unit, 0), s.rest, {}, LEFT)], s.send_sem.at[unit], s.final_sem.at[unit], s.up_dev)
        down_spot = spot(lead, s.dims, {s.axis: s.down}, RIGHT)
        src[down_spot] = src[down_spot] + s.relay[unit, 1]
        send(src.at[down_spot], s.final.at[spot((unit, 1), s.rest, {}, RIGHT)], s.send_sem.at[unit], s.final_sem.at[unit], s.down_dev)

    def finish(self, src, lead, unit):
        s = self
        await_bytes(s.final.at[unit], s.final_sem.at[unit])
        return src[spot(lead, s.dims, {s.axis: s.own}, ALL)] + s.final[unit, 0] + s.final[unit, 1]

    def drain(self, unit):
        await_bytes(self.relay.at[unit], self.send_sem.at[unit])
        await_bytes(self.final.at[unit], self.send_sem.at[unit])


def reduce_kernel(g_one, g_two, g_three, g_four, shard, swapped, norm_tile, own, part, relay1, final1, relay2, final2, relay3, final3, mid, low, norm_own, norm_a, norm_b, norm_c, load_sem, part_send, part_recv, ring_sems, swap_sems, norm_sems):
    place = Place()
    units = unit_list()
    chunks = -(-len(units) // 3)
    counts = [len(range(order, len(units), 3)) for order in range(3)]
    partner = place.device(other_core=True)
    group_x = [(place.device({2: by}, other_core=swap)) for by in range(SIDE) for swap in (False, True) if by or swap]
    group_y = [place.device({1: by}) for by in range(1, SIDE)]
    group_z = [place.device({0: by}) for by in range(1, SIDE)]
    enter(group_x + group_y + group_z)

    def source(mat, piece, core):
        if mat in (1, 3):
            ref = g_one if mat == 1 else g_three
            start = core * (UNITS_OF[mat] * WIDTH) + piece * WIDTH
            return ref.at[:, :, :, :, pl.ds(pl.multiple_of(start, WIDTH), WIDTH)]
        ref = g_two if mat == 2 else g_four
        return ref.at[:, :, :, core, pl.ds(piece * ROWS, ROWS), :]

    rings = []
    for order in range(3):
        a, b = order, (order + 1) % 3
        c = (order + 2) % 3
        first = RingSum(place, [0, 1, 2], a, relay1, final1, ring_sems.at[0, 0], ring_sems.at[0, 1], ring_sems.at[0, 2])
        second = RingSum(place, first.rest, b, relay2, final2, ring_sems.at[1, 0], ring_sems.at[1, 1], ring_sems.at[1, 2])
        third = RingSum(place, second.rest, c, relay3, final3, ring_sems.at[2, 0], ring_sems.at[2, 1], ring_sems.at[2, 2])
        rings.append((first, second, third))

    def load(chunk):
        for order in range(3):
            unit = 3 * chunk + order
            if unit >= len(units):
                continue
            mat, piece = units[unit]
            send(source(mat, piece, 1 - place.core), part.at[unit], part_send.at[unit], part_recv.at[unit], partner)
            if chunk >= SLOTS:
                rings[order][0].drain(unit - 3 * SLOTS)
            pltpu.make_async_copy(source(mat, piece, place.core), own.at[order, chunk % SLOTS], load_sem.at[unit]).start()

    def stage_b(order, chunk, unit):
        lead = (order, lax.rem(chunk, SLOTS))
        await_bytes(own.at[lead], load_sem.at[unit])
        await_bytes(part.at[unit], part_recv.at[unit])
        own[lead] = own[lead] + part[unit]
        rings[order][0].start(own, lead, unit)

    def stage_c(order, chunk, unit):
        rings[order][0].pass_on(own, (order, lax.rem(chunk, SLOTS)), unit)

    def stage_d(order, chunk, unit):
        mid[unit] = rings[order][0].finish(own, (order, lax.rem(chunk, SLOTS)), unit)
        rings[order][1].start(mid, (unit,), unit)

    def stage_e(order, chunk, unit):
        rings[order][1].pass_on(mid, (unit,), unit)

    def stage_f(order, chunk, unit):
        low[unit] = rings[order][1].finish(mid, (unit,), unit)
        rings[order][2].start(low, (unit,), unit)

    def stage_g(order, chunk, unit):
        rings[order][2].pass_on(low, (unit,), unit)

    def stage_h(order, chunk, unit):
        shard[unit] = rings[order][2].finish(low, (unit,), unit) * (1.0 / (2 * SIDE ** 3))

    stages = (stage_b, stage_c, stage_d, stage_e, stage_f, stage_g, stage_h)

    def turn(now, carry):
        for chunk in range(chunks):
            @pl.when(now == chunk)
            def _(chunk=chunk):
                load(chunk)
        for lag, stage in enumerate(stages):
            chunk = now - lag - 1
            for order in range(3):
                @pl.when((chunk >= 0) & (chunk < counts[order]))
                def _(stage=stage, order=order, chunk=chunk):
                    stage(order, chunk, 3 * chunk + order)
        return carry

    lax.fori_loop(0, chunks + len(stages), turn, 0)

    n_three = UNITS_OF[3]
    n_one = UNITS_OF[1]
    base_one = first_unit(1)
    send(shard.at[pl.ds(0, n_three)], swapped.at[pl.ds(0, n_three)], swap_sems.at[0], swap_sems.at[1], partner)
    send(shard.at[pl.ds(base_one, n_one)], swapped.at[pl.ds(n_three, n_one)], swap_sems.at[0], swap_sems.at[1], partner)

    def fold(unit, total):
        value = shard[unit]
        return total + value * value

    squares = lax.fori_loop(0, len(units), fold, jnp.zeros((ROWS, WIDTH), jnp.float32))
    total = squares[:, 0:128]
    for col in range(1, WIDTH // 128):
        total = total + squares[:, col * 128:(col + 1) * 128]
    levels = ((norm_a, group_x, place.coords[2] * 2 + place.core), (norm_b, group_y, place.coords[1]), (norm_c, group_z, place.coords[0]))
    for level, (board, group, seat) in enumerate(levels):
        norm_own[level] = total
        board[seat] = total
        for peer in group:
            send(norm_own.at[level], board.at[seat], norm_sems.at[0, level], norm_sems.at[1, level], peer)
        await_bytes(board.at[pl.ds(0, len(group))], norm_sems.at[1, level])
        total = board[0]
        for row in range(1, len(group) + 1):
            total = total + board[row]
    norm_tile[...] = total

    await_bytes(swapped, swap_sems.at[0])
    await_bytes(swapped, swap_sems.at[1])
    for level, (board, group, seat) in enumerate(levels):
        await_bytes(board.at[pl.ds(0, len(group))], norm_sems.at[0, level])
    for order in range(3):
        def tidy(chunk, carry, order=order):
            unit = 3 * chunk + order
            await_bytes(part.at[unit], part_send.at[unit])
            rings[order][1].drain(unit)
            rings[order][2].drain(unit)

            @pl.when(chunk >= counts[order] - SLOTS)
            def _():
                rings[order][0].drain(unit)
            return carry

        lax.fori_loop(0, counts[order], tidy, 0)


def reduce_grads(g_one, g_two, g_three, g_four):
    n = len(unit_list())
    cube = (SIDE, SIDE, SIDE)
    args = (
        g_one.reshape(cube + (ROWS, 2 * UNITS_OF[1] * WIDTH)),
        g_two.reshape(cube + (2, UNITS_OF[2] * ROWS, WIDTH)),
        g_three.reshape(cube + (ROWS, 2 * UNITS_OF[3] * WIDTH)),
        g_four.reshape(cube + (2, UNITS_OF[4] * ROWS, WIDTH)),
    )
    f32 = jnp.float32
    dma = pltpu.SemaphoreType.DMA
    scratch = [
        pltpu.VMEM((3, SLOTS) + cube + (ROWS, WIDTH), f32),
        pltpu.VMEM((n,) + cube + (ROWS, WIDTH), f32),
        pltpu.VMEM((n, 2, SIDE, SIDE, ROWS, WIDTH // 2), f32),
        pltpu.VMEM((n, 2, SIDE, SIDE, ROWS, WIDTH), f32),
        pltpu.VMEM((n, 2, SIDE, ROWS, WIDTH // 2), f32),
        pltpu.VMEM((n, 2, SIDE, ROWS, WIDTH), f32),
        pltpu.VMEM((n, 2, ROWS, WIDTH // 2), f32),
        pltpu.VMEM((n, 2, ROWS, WIDTH), f32),
        pltpu.VMEM((n, SIDE, SIDE, ROWS, WIDTH), f32),
        pltpu.VMEM((n, SIDE, ROWS, WIDTH), f32),
        pltpu.VMEM((3, ROWS, 128), f32),
        pltpu.VMEM((2 * SIDE, ROWS, 128), f32),
        pltpu.VMEM((SIDE, ROWS, 128), f32),
        pltpu.VMEM((SIDE, ROWS, 128), f32),
        dma((n,)), dma((n,)), dma((n,)), dma((3, 3, n)), dma((2,)), dma((2, 3)),
    ]
    any_spec = pl.BlockSpec(memory_space=pl.ANY)
    vmem_spec = pl.BlockSpec(memory_space=pltpu.VMEM)
    return pl.pallas_call(
        reduce_kernel,
        out_shape=(
            jax.ShapeDtypeStruct((n, ROWS, WIDTH), f32),
            jax.ShapeDtypeStruct((UNITS_OF[3] + UNITS_OF[1], ROWS, WIDTH), f32),
            jax.ShapeDtypeStruct((ROWS, 128), f32),
        ),
        in_specs=[any_spec] * 4,
        out_specs=(vmem_spec,) * 3,
        scratch_shapes=scratch,
        compiler_params=pltpu.CompilerParams(collective_id=0, has_side_effects=True, vmem_limit_bytes=VMEM_BYTES),
        name='reduce_grads',
    )(*args)


def adam_kernel(lr_ref, clip_ref, norm_tile, shard, swapped, *refs):
    masters, moms, variances = refs[0:4], refs[4:8], refs[8:12]
    new_masters, new_moms, new_vars = refs[12:16], refs[16:20], refs[20:24]
    two_rows, four_rows, norm_ref = refs[24:27]
    core = lax.rem(lax.axis_index('dp'), 2)
    grad_norm = jnp.sqrt(jnp.sum(jnp.sum(norm_tile[...], axis=1, keepdims=True), axis=0, keepdims=True))
    norm_ref[...] = grad_norm
    clip_scale = jnp.minimum(1.0, clip_ref[...] / (grad_norm + NORM_EPS))
    learn_rate = lr_ref[...]

    def update(mat, where, grad):
        scaled = clip_scale * grad
        mom_new = BETA_ONE * moms[mat][where] + (1.0 - BETA_ONE) * scaled
        var_new = BETA_TWO * variances[mat][where] + (1.0 - BETA_TWO) * scaled * scaled
        master_new = masters[mat][where] - learn_rate * (mom_new / BIAS_ONE) / (jnp.sqrt(var_new / BIAS_TWO) + ADAM_EPS)
        new_moms[mat][where] = mom_new
        new_vars[mat][where] = var_new
        new_masters[mat][where] = master_new
        return master_new

    for mat, rows_out in ((2, two_rows), (4, four_rows)):
        for piece in range(UNITS_OF[mat]):
            where = (slice(piece * ROWS, (piece + 1) * ROWS), slice(None))
            rows_out[piece] = update(mat - 1, where, shard[first_unit(mat) + piece]).astype(jnp.bfloat16)
    for mat, base in ((3, 0), (1, UNITS_OF[3])):
        for half in range(2):
            for piece in range(UNITS_OF[mat]):
                col = (half * UNITS_OF[mat] + piece) * WIDTH
                where = (slice(None), slice(col, col + WIDTH))
                block = jnp.where(core == half, shard[first_unit(mat) + piece], swapped[base + piece])
                update(mat - 1, where, jnp.where(core == 0, block[0:ROWS // 2], block[ROWS // 2:ROWS]))


def adam_update(learn_rate, clip_max, norm_tile, shard, swapped, masters, moms, variances):
    state = list(masters) + list(moms) + list(variances)
    f32, bf16 = jnp.float32, jnp.bfloat16
    vmem_spec = pl.BlockSpec(memory_space=pltpu.VMEM)
    out_shape = [jax.ShapeDtypeStruct(part.shape, f32) for part in state]
    out_shape += [
        jax.ShapeDtypeStruct((UNITS_OF[2], ROWS, WIDTH), bf16),
        jax.ShapeDtypeStruct((UNITS_OF[4], ROWS, WIDTH), bf16),
        jax.ShapeDtypeStruct((1, 1), f32),
    ]
    args = [learn_rate.reshape(1, 1), clip_max.reshape(1, 1), norm_tile, shard, swapped] + state
    return pl.pallas_call(
        adam_kernel,
        out_shape=out_shape,
        in_specs=[vmem_spec] * len(args),
        out_specs=[vmem_spec] * len(out_shape),
        name='adam_update',
    )(*args)


class RingSpread:
    def __init__(self, place, axis, known, board, near_sem, far_sem, send_sem):
        self.place, self.axis, self.known, self.board = place, axis, known, board
        self.near_sem, self.far_sem, self.send_sem = near_sem, far_sem, send_sem
        self.up_dev, self.down_dev = place.device({axis: 1}), place.device({axis: SIDE - 1})

    def block(self, unit, by, cols):
        fixed = {dim: self.place.coords[dim] for dim in range(3) if dim not in self.known}
        fixed[self.axis] = self.place.step(self.axis, by)
        return self.board.at[spot((unit,), [0, 1, 2], fixed, cols)]

    def blocks(self, unit, count):
        return self.board.at[(unit,) + (0,) * (2 - len(self.known)) + (pl.ds(0, count),)]

    def start(self, unit):
        s = self
        mine = s.block(unit, 0, ALL)
        send(mine, mine, s.send_sem.at[unit], s.near_sem.at[unit], s.up_dev)
        send(mine, mine, s.send_sem.at[unit], s.near_sem.at[unit], s.down_dev)

    def pass_on(self, unit):
        s = self
        await_bytes(s.blocks(unit, 2), s.near_sem.at[unit])
        from_down, from_up = s.block(unit, SIDE - 1, LEFT), s.block(unit, 1, RIGHT)
        send(from_down, from_down, s.send_sem.at[unit], s.far_sem.at[unit], s.up_dev)
        send(from_up, from_up, s.send_sem.at[unit], s.far_sem.at[unit], s.down_dev)

    def finish(self, unit):
        await_bytes(self.block(unit, 0, ALL), self.far_sem.at[unit])

    def drain(self, unit):
        await_bytes(self.blocks(unit, 3), self.send_sem.at[unit])


def gather_kernel(one_rows, three_rows, two_rows, four_rows, board, other, swap_one, swap_three, ring_sems, pair_sems, swap_sems):
    place = Place()
    units = unit_list()
    chunks = -(-len(units) // 3)
    counts = [len(range(order, len(units), 3)) for order in range(3)]
    partner = place.device(other_core=True)
    here = tuple(place.coords)
    enter(place.neighbours())
    splits = ((1, one_rows, swap_one), (3, three_rows, swap_three))
    for index, (mat, rows, landing) in enumerate(splits):
        span = UNITS_OF[mat] * WIDTH
        theirs = rows.at[:, pl.ds(pl.multiple_of((1 - place.core) * span, WIDTH), span)]
        send(theirs, landing, swap_sems.at[0, index], swap_sems.at[1, index], partner)
    for mat, rows in ((2, two_rows), (4, four_rows)):
        for piece in range(UNITS_OF[mat]):
            board[(first_unit(mat) + piece,) + here] = rows[piece]
    for index, (mat, rows, landing) in enumerate(splits):
        await_bytes(landing, swap_sems.at[1, index])
        for piece in range(UNITS_OF[mat]):
            start = place.core * (UNITS_OF[mat] * WIDTH) + piece * WIDTH
            mine = rows[:, pl.ds(pl.multiple_of(start, WIDTH), WIDTH)]
            theirs = landing[:, piece * WIDTH:(piece + 1) * WIDTH]
            top = jnp.where(place.core == 0, mine, theirs)
            bottom = jnp.where(place.core == 0, theirs, mine)
            board[(first_unit(mat) + piece,) + here] = jnp.concatenate([top, bottom], axis=0).astype(board.dtype)

    rings = []
    for order in range(3):
        axes = (order + 2) % 3, (order + 1) % 3, order
        rings.append([RingSpread(place, axis, axes[:level], board, ring_sems.at[level, 0], ring_sems.at[level, 1], ring_sems.at[level, 2]) for level, axis in enumerate(axes)])

    def every(action):
        def turn(chunk, carry):
            for order in range(3):
                @pl.when(chunk < counts[order])
                def _(order=order):
                    action(order, 3 * chunk + order)
            return carry

        lax.fori_loop(0, chunks, turn, 0)

    def begin(order, unit):
        rings[order][0].start(unit)

    every(begin)
    for level in range(3):
        def pass_on(order, unit, level=level):
            rings[order][level].pass_on(unit)

        def onward(order, unit, level=level):
            rings[order][level].finish(unit)
            if level < 2:
                rings[order][level + 1].start(unit)
            else:
                send(board.at[unit], other.at[unit], pair_sems.at[0, unit], pair_sems.at[1, unit], partner)

        every(pass_on)
        every(onward)

    def tidy(order, unit):
        await_bytes(other.at[unit], pair_sems.at[1, unit])
        await_bytes(board.at[unit], pair_sems.at[0, unit])
        for level in range(3):
            rings[order][level].drain(unit)

    every(tidy)
    for index, (mat, rows, landing) in enumerate(splits):
        await_bytes(landing, swap_sems.at[0, index])


def gather_rows(one_rows, three_rows, two_rows, four_rows):
    n = len(unit_list())
    cube = (SIDE, SIDE, SIDE)
    bf16, f32 = jnp.bfloat16, jnp.float32
    dma = pltpu.SemaphoreType.DMA
    vmem_spec = pl.BlockSpec(memory_space=pltpu.VMEM)
    full = jax.ShapeDtypeStruct((n,) + cube + (ROWS, WIDTH), bf16)
    return pl.pallas_call(
        gather_kernel,
        out_shape=(full, full),
        in_specs=[vmem_spec] * 4,
        out_specs=(vmem_spec, vmem_spec),
        scratch_shapes=[
            pltpu.VMEM((ROWS // 2, UNITS_OF[1] * WIDTH), f32),
            pltpu.VMEM((ROWS // 2, UNITS_OF[3] * WIDTH), f32),
            dma((3, 3, n)), dma((2, n)), dma((2, 2)),
        ],
        compiler_params=pltpu.CompilerParams(collective_id=1, has_side_effects=True, vmem_limit_bytes=32 * 1024 * 1024),
        name='gather_rows',
    )(one_rows, three_rows, two_rows, four_rows)


def place_kernel(board, other, w_one, w_two, w_three, w_four, sems):
    core = lax.rem(lax.axis_index('dp'), 2)
    outs = {1: w_one, 2: w_two, 3: w_three, 4: w_four}
    copies = []
    for unit, (mat, piece) in enumerate(unit_list()):
        for index, (source, owner) in enumerate(((board, core), (other, 1 - core))):
            if mat in (1, 3):
                start = owner * (UNITS_OF[mat] * WIDTH) + piece * WIDTH
                target = outs[mat].at[:, :, :, :, pl.ds(pl.multiple_of(start, WIDTH), WIDTH)]
            else:
                target = outs[mat].at[:, :, :, owner, pl.ds(piece * ROWS, ROWS), :]
            copies.append(pltpu.make_async_copy(source.at[unit], target, sems.at[index, unit]))
    for copy in copies:
        copy.start()
    for copy in copies:
        copy.wait()


def place_weights(board, other):
    n = len(unit_list())
    cube = (SIDE, SIDE, SIDE)
    bf16 = jnp.bfloat16
    vmem_spec = pl.BlockSpec(memory_space=pltpu.VMEM)
    any_spec = pl.BlockSpec(memory_space=pl.ANY)
    outs = pl.pallas_call(
        place_kernel,
        out_shape=(
            jax.ShapeDtypeStruct(cube + (ROWS, 2 * UNITS_OF[1] * WIDTH), bf16),
            jax.ShapeDtypeStruct(cube + (2, UNITS_OF[2] * ROWS, WIDTH), bf16),
            jax.ShapeDtypeStruct(cube + (ROWS, 2 * UNITS_OF[3] * WIDTH), bf16),
            jax.ShapeDtypeStruct(cube + (2, UNITS_OF[4] * ROWS, WIDTH), bf16),
        ),
        in_specs=[vmem_spec] * 2,
        out_specs=(any_spec,) * 4,
        scratch_shapes=[pltpu.SemaphoreType.DMA((2, n))],
        compiler_params=pltpu.CompilerParams(vmem_limit_bytes=2 * 1024 * 1024),
        name='place_weights',
    )(board, other)
    rows = SIDE ** 3 * ROWS
    return (
        outs[0].reshape(rows, 2 * UNITS_OF[1] * WIDTH),
        outs[1].reshape(2 * SIDE ** 3 * UNITS_OF[2] * ROWS, WIDTH),
        outs[2].reshape(rows, 2 * UNITS_OF[3] * WIDTH),
        outs[3].reshape(2 * SIDE ** 3 * UNITS_OF[4] * ROWS, WIDTH),
    )


def sync_and_update(grads, masters, moms, variances, learn_rate, clip_max):
    shard, swapped, norm_tile = reduce_grads(*grads)
    results = adam_update(learn_rate, clip_max, norm_tile, shard, swapped, masters, moms, variances)
    new_masters, new_moms, new_vars = results[0:4], results[4:8], results[8:12]
    two_rows, four_rows, grad_norm = results[12:15]
    board, other = gather_rows(new_masters[0], new_masters[2], two_rows, four_rows)
    new_weights = place_weights(board, other)
    return tuple(new_weights) + tuple(new_masters) + tuple(new_moms) + tuple(new_vars) + (grad_norm.reshape(()),)


def solution(mesh):
    row_spec = P('dp', None)
    rep_spec = P()

    def per_device(x_rows, dy_rows, w_one, w_two, w_three, w_four, master_one, master_two, master_three, master_four, m_one, m_two, m_three, m_four, v_one, v_two, v_three, v_four, learn_rate, clip_max):
        grads = local_grads(x_rows, dy_rows, w_one, w_two, w_three, w_four)
        return sync_and_update(grads, (master_one, master_two, master_three, master_four), (m_one, m_two, m_three, m_four), (v_one, v_two, v_three, v_four), learn_rate, clip_max)

    in_specs = (row_spec, row_spec) + (rep_spec,) * 4 + (row_spec,) * 12 + (rep_spec, rep_spec)
    out_specs = (rep_spec,) * 4 + (row_spec,) * 12 + (rep_spec,)
    return jax.shard_map(per_device, mesh=mesh, in_specs=in_specs, out_specs=out_specs, check_vma=False)
```

time: 1960 us -> 306 us (0.16)
  waiting for transfers between devices: 1710 us -> 0 us
  Pallas kernels: 0 us -> 181 us
  blocking collectives: 69.3 us -> 0 us
  local copies, waits for them, and re-layouts: 30.2 us -> 4.47 us
    reduce_scatter x2 -> x0, waiting for transfers between devices: 1230 us -> none  [per_device(): lax.psum_scatter(grad_mat, 'dp', scatter_dimension=0, tiled=True) / dp_size]
    all_gather x4 -> x0, waiting for transfers between devices: 247 us -> none  [per_device(): lax.all_gather(result[0].astype(jnp.bfloat16), 'dp', axis=0, tiled=True)]
    unnamed x8 -> x0, waiting for transfers between devices: 228 us -> none
    pallas_call x0 -> x4, Pallas kernels: none -> 181 us  [the longest x1 110 us: reduce_grads(): pl.pallas_call(reduce_kernel, out_shape=(jax.ShapeDtypeStruct((n, ROWS, W...]
    psum x1 -> x0, blocking collectives: 69.3 us -> none  [per_device(): grad_norm = jnp.sqrt(lax.psum(local_sq, 'dp'))]
    unnamed x40 -> x22, local copies, waits for them, and re-layouts: 27.3 us -> 4.47 us
  transfers between devices with their start and end apart: 7 -> 0, of which waited for: 7 -> 0; matrix products, arithmetic and copies ran while one was open for 5% -> 0% of each run, Pallas kernels for 0% -> 0%
where the time goes in v1:
time: 306 us; the launch traced here: 305 us
  Pallas kernels  181 us (59%)
  matrix products  118 us (39%)
  local copies, waits for them, and re-layouts  4.47 us (1%)
    pallas_call x1, Pallas kernels, reduce_grads(): pl.pallas_call(reduce_kernel, out_shape=(jax.ShapeDtypeStruct((n, ROWS, W...  110 us
    pallas_call x1, Pallas kernels, gather_rows(): pl.pallas_call(gather_kernel, out_shape=(full, full), in_specs=[vmem_spec...  60.6 us
    dot_general x1, matrix products, local_grads(): jnp.einsum('rd,rw->dw', x_rows, dz_one, preferred_element_type=jnp.float32)  31.2 us
    dot_general x1, matrix products, local_grads(): jnp.einsum('rw,rd->wd', a_one, dh_two, preferred_element_type=jnp.float32)  24.8 us
    dot_general x1, matrix products, local_grads(): jnp.dot(a_one, w_two, preferred_element_type=jnp.float32)  21.2 us
    dot_general x1, matrix products, local_grads(): jnp.dot(x_rows, w_one, preferred_element_type=jnp.float32)  20.9 us
    pallas_call x1, Pallas kernels, place_weights(): pl.pallas_call(place_kernel, out_shape=(jax.ShapeDtypeStruct(cube + (ROWS...  7.42 us

profile of v1, /device:TPU:1, one launch (start us, length us, event | category | flops | bytes accessed | tf_op | source)
XLA Modules:
  0.0 305.3 jit_solution(7391117490630966517)
XLA Ops:
  0.7 0.0 copy-start
  0.7 1.2 copy-done
  1.9 20.9 %fusion.3 = (f32[1024,8192]{1,0:T(8,128)}, bf16[1024,8192]{1,0:T(8,128)(2,1)}) fusion(bf16[1024,512]{1,0:T(8,128)(2,1)S(1)} %copy-done, bf16[512,8192]{1,0:T(8,128)(2,1)} %param.22), kind=kOutput, calls=%fused_computation.8 | convolution fusion | flops 8623489024 | bytes 59768832 | tf_op jit(solution)/shard_map/dot_general | solution.py:48
  22.8 21.2 %convolution_convert_fusion.2 = bf16[1024,512]{1,0:T(8,128)(2,1)S(1)} fusion(bf16[8192,512]{1,0:T(8,128)(2,1)} %param.23, f32[1024,8192]{1,0:T(8,128)} %get-tuple-element.65, bf16[1024,8192]{1,0:T(8,128)(2,1)} %get-tuple-element.66), kind=kOutput, calls=%fused_computation.34 | convolution fusion | flops 8624013312 | bytes 59768832 | tf_op jit(solution)/shard_map/dot_general | solution.py:50
  44.0 0.0 copy-start.5
  44.0 0.0 copy-start.8
  44.0 2.3 convolution_convert_fusion.1
  46.4 0.0 copy-start.10
  46.4 5.3 %fusion.18 = bf16[1024,2048]{1,0:T(8,128)(2,1)S(1)} fusion(bf16[1024,2048]{1,0:T(8,128)(2,1)S(1)} %convolution_convert_fusion.1, bf16[1024,512]{1,0:T(8,128)(2,1)S(1)} %copy-done.8, bf16[2048,512]{1,0:T(8,128)(2,1)S(1)} %copy-done.5), kind=kOutput, calls=%fused_computation.27 | convolution fusion | flops 2174746624 | bytes 11534336 | tf_op jit(solution)/shard_map/rd,fd->rf/dot_general | solution.py:54
  51.7 0.0 copy-start.7
  51.7 4.4 %fusion.33 = f32[512,2048]{1,0:T(8,128)} fusion(bf16[1024,512]{1,0:T(8,128)(2,1)S(1)} %convolution_convert_fusion.2, bf16[1024,2048]{1,0:T(8,128)(2,1)S(1)} %fusion.18), kind=kOutput, calls=%fused_computation.41 | convolution fusion | flops 2147483648 | bytes 9437184 | tf_op jit(solution)/shard_map/rd,rf->df/dot_general | solution.py:56
  56.1 2.4 convolution_convert_fusion.3
  58.5 24.8 %fusion.29 = f32[8192,512]{1,0:T(8,128)} fusion(bf16[1024,512]{1,0:T(8,128)(2,1)S(1)} %convolution_convert_fusion.3, f32[1024,8192]{1,0:T(8,128)} %get-tuple-element.65, bf16[1024,8192]{1,0:T(8,128)(2,1)} %get-tuple-element.66), kind=kOutput, calls=%fused_computation.40 | convolution fusion | flops 8623489024 | bytes 68157440 | tf_op jit(solution)/shard_map/rw,rd->wd/dot_general | solution.py:58
  83.3 31.2 %fusion.9 = f32[8192,512]{0,1:T(8,128)} fusion(bf16[1024,512]{1,0:T(8,128)(2,1)S(1)} %copy-done, bf16[1024,8192]{1,0:T(8,128)(2,1)} %get-tuple-element.66, f32[1024,8192]{1,0:T(8,128)} %get-tuple-element.65, bf16[1024,512]{1,0:T(8,128)(2,1)S(1)} %convolution_convert_fusion.3, bf16[8192,512]{1,0:T(8,128)(2,1)} %param.23), kind=kOutput, calls=%fused_computation.19 | convolution fusion | flops 17272143872 | bytes 77594624 | tf_op jit(solution)/shard_map/rd,rw->dw/dot_general | solution.py:61
  114.4 5.5 %fusion.22 = f32[2048,512]{1,0:T(8,128)} fusion(bf16[1024,512]{1,0:T(8,128)(2,1)S(1)} %copy-done.9, bf16[1024,2048]{1,0:T(8,128)(2,1)} %copy-done.10), kind=kOutput, calls=%fused_computation.31 | convolution fusion | flops 2160066560 | bytes 9437184 | tf_op jit(solution)/shard_map/rf,rd->fd/dot_general | solution.py:53
  119.9 109.9 %reduce_grads.1 = (f32[20,8,512]{2,1,0:T(8,128)}, f32[10,8,512]{2,1,0:T(8,128)}, f32[8,128]{1,0:T(8,128)}) custom-call(f32[4,4,4,8,8192]{4,3,2,1,0:T(8,128)} %bitcast.33, f32[4,4,4,2,64,512]{5,4,3,2,1,0:T(8,128)} %bitcast.31, f32[4,4,4,8,2048]{4,3,2,1,0:T(8,128)} %bitcast.32, f32[4,4,4,2,16,512]{5,4,3,2,1,0:T(8,128)} %bitcast.34), custom_call_target="tpu_custom_call" | custom-call | tf_op jit(solution)/shard_map/reduce_grads/pallas_call | solution.py:307
  231.2 2.7 adam_update.1
  233.9 0.0 copy-start.1
  233.9 0.9 copy-done.1
  234.8 0.8 copy-done.2
  235.6 0.8 copy-done.3
  236.4 0.7 copy-done.4
  237.1 60.6 %gather_rows.1 = (bf16[20,4,4,4,8,512]{5,4,3,2,1,0:T(8,128)(2,1)S(1)}, bf16[20,4,4,4,8,512]{5,4,3,2,1,0:T(8,128)(2,1)S(1)}) custom-call(f32[4,8192]{1,0:T(4,128)S(1)} %copy-done.1, f32[4,2048]{1,0:T(4,128)S(1)} %copy-done.3, bf16[8,8,512]{2,1,0:T(8,128)(2,1)S(1)} %copy-done.2, bf16[2,8,512]{2,1,0:T(8,128)(2,1)S(1)} %copy-done.4), custom_call_target="tpu_custom_call" | custom-call | tf_op jit(solution)/shard_map/gather_rows/pallas_call | solution.py:486
  297.7 7.4 %place_weights.1 = (bf16[4,4,4,8,8192]{4,3,2,1,0:T(8,128)(2,1)}, bf16[4,4,4,2,64,512]{5,4,3,2,1,0:T(8,128)(2,1)}, bf16[4,4,4,8,2048]{4,3,2,1,0:T(8,128)(2,1)}, bf16[4,4,4,2,16,512]{5,4,3,2,1,0:T(8,128)(2,1)}) custom-call(bf16[20,4,4,4,8,512]{5,4,3,2,1,0:T(8,128)(2,1)S(1)} %get-tuple-element.48.board, bf16[20,4,4,4,8,512]{5,4,3,2,1,0:T(8,128)(2,1)S(1)} %get-tuple-element.49.other), custom_call_target="tpu_custom_call" | custom-call | tf_op jit(solution)/shard_map/place_weights/pallas_call | solution.py:525
  (11 shorter events, 0.0 us)
Async XLA Ops:
  0.7 1.2 copy-start
  22.8 21.2 %copy-start.6 = (bf16[512,2048]{1,0:T(8,128)(2,1)S(1)}, bf16[512,2048]{1,0:T(8,128)(2,1)}, u32[]{:S(2)}) copy-start(bf16[512,2048]{1,0:T(8,128)(2,1)} %param.24) | copy-start | bytes 6291460
  44.0 2.4 copy-start.5
  44.0 2.4 copy-start.8
  46.4 5.3 %copy-start.10 = (bf16[1024,2048]{1,0:T(8,128)(2,1)}, bf16[1024,2048]{1,0:T(8,128)(2,1)S(1)}, u32[]{:S(2)}) copy-start(bf16[1024,2048]{1,0:T(8,128)(2,1)S(1)} %convolution_convert_fusion.1) | copy-start | bytes 12582916
  51.7 4.4 %copy-start.7 = (bf16[512,2048]{1,0:T(8,128)(2,1)S(1)}, bf16[512,2048]{1,0:T(8,128)(2,1)}, u32[]{:S(2)}) copy-start(bf16[512,2048]{1,0:T(8,128)(2,1)} %param.24) | copy-start | bytes 6291460
  83.3 31.2 %copy-start.9 = (bf16[1024,512]{1,0:T(8,128)(2,1)S(1)}, bf16[1024,512]{1,0:T(8,128)(2,1)}, u32[]{:S(2)}) copy-start(bf16[1024,512]{1,0:T(8,128)(2,1)} %param.21) | copy-start | bytes 3145732
  233.9 0.9 copy-start.1
  234.8 0.8 copy-start.2
  235.6 0.8 copy-start.3
  236.4 0.7 copy-start.4

commit v2 on v1

--- a/solution.py
+++ b/solution.py
@@ -21,7 +21,6 @@
 SIDE = 4
 ROWS = 8
 UNITS_OF = {3: 2, 4: 2, 2: 8, 1: 8}
-SLOTS = 4
 MESH_ID = pl.DeviceIdType.MESH
 VMEM_BYTES = 62 * 1024 * 1024
 
@@ -44,10 +43,43 @@
     return 0.5 * (1.0 + lax.erf(pre_wide * INV_SQRT2)) + pre_wide * INV_SQRT2PI * jnp.exp(-0.5 * pre_wide * pre_wide)
 
 
+def forward_kernel(x_ref, w_one, w_two, z_out, a_out, h_out, total):
+    step = pl.program_id(0)
+
+    @pl.when(step == 0)
+    def _():
+        total[...] = jnp.zeros_like(total)
+
+    z_one = jnp.dot(x_ref[...], w_one[...], preferred_element_type=jnp.float32).astype(jnp.bfloat16)
+    z_out[...] = z_one
+    a_one = gelu_value(z_one).astype(jnp.bfloat16)
+    a_out[...] = a_one
+    total[...] += jnp.dot(a_one, w_two[...], preferred_element_type=jnp.float32)
+
+    @pl.when(step == pl.num_programs(0) - 1)
+    def _():
+        h_out[...] = total[...].astype(jnp.bfloat16)
+
+
+def forward_wide(x_rows, w_one, w_two):
+    rows, dim = x_rows.shape
+    wide = w_one.shape[1]
+    block = 512
+    bf16 = jnp.bfloat16
+    return pl.pallas_call(
+        forward_kernel,
+        grid=(wide // block,),
+        out_shape=(jax.ShapeDtypeStruct((rows, wide), bf16), jax.ShapeDtypeStruct((rows, wide), bf16), jax.ShapeDtypeStruct((rows, dim), bf16)),
+        in_specs=[pl.BlockSpec((rows, dim), lambda i: (0, 0)), pl.BlockSpec((dim, block), lambda i: (0, i)), pl.BlockSpec((block, dim), lambda i: (i, 0))],
+        out_specs=(pl.BlockSpec((rows, block), lambda i: (0, i)), pl.BlockSpec((rows, block), lambda i: (0, i)), pl.BlockSpec((rows, dim), lambda i: (0, 0))),
+        scratch_shapes=[pltpu.VMEM((rows, dim), jnp.float32)],
+        compiler_params=pltpu.CompilerParams(vmem_limit_bytes=VMEM_BYTES),
+        name='forward_wide',
+    )(x_rows, w_one, w_two)
+
+
 def local_grads(x_rows, dy_rows, w_one, w_two, w_three, w_four):
-    z_one = jnp.dot(x_rows, w_one, preferred_element_type=jnp.float32).astype(jnp.bfloat16)
-    a_one = gelu_value(z_one).astype(jnp.bfloat16)
-    h_two = jnp.dot(a_one, w_two, preferred_element_type=jnp.float32).astype(jnp.bfloat16)
+    z_one, a_one, h_two = forward_wide(x_rows, w_one, w_two)
     z_three = jnp.dot(h_two, w_three, preferred_element_type=jnp.float32).astype(jnp.bfloat16)
     a_three = gelu_value(z_three).astype(jnp.bfloat16)
     g_four = jnp.einsum('rf,rd->fd', a_three, dy_rows, preferred_element_type=jnp.float32)
@@ -56,10 +88,7 @@
     g_three = jnp.einsum('rd,rf->df', h_two, dz_three, preferred_element_type=jnp.float32)
     dh_two = jnp.einsum('rf,df->rd', dz_three, w_three, preferred_element_type=jnp.float32).astype(jnp.bfloat16)
     g_two = jnp.einsum('rw,rd->wd', a_one, dh_two, preferred_element_type=jnp.float32)
-    da_one = jnp.einsum('rd,wd->rw', dh_two, w_two, preferred_element_type=jnp.float32).astype(jnp.bfloat16)
-    dz_one = (da_one.astype(jnp.float32) * gelu_slope(z_one)).astype(jnp.bfloat16)
-    g_one = jnp.einsum('rd,rw->dw', x_rows, dz_one, preferred_element_type=jnp.float32)
-    return g_one, g_two, g_three, g_four
+    return (x_rows.T, dh_two, z_one, w_two), g_two, g_three, g_four
 
 
 class Place:
@@ -146,22 +175,50 @@
         await_bytes(self.final.at[unit], self.send_sem.at[unit])
 
 
-def reduce_kernel(g_one, g_two, g_three, g_four, shard, swapped, norm_tile, own, part, relay1, final1, relay2, final2, relay3, final3, mid, low, norm_own, norm_a, norm_b, norm_c, load_sem, part_send, part_recv, ring_sems, swap_sems, norm_sems):
+BLOCK = 256
+BLOCKS_PER_UNIT = 2 * (WIDTH // BLOCK)
+BLOCKS_PER_TURN = 6
+
+
+def reduce_kernel(x_turned, dh_two, z_one, w_two, g_two, g_three, g_four, shard, swapped, norm_tile, own, wide_own, part, relay1, final1, relay2, final2, relay3, final3, norm_own, norm_a, norm_b, norm_c, x_buf, dh_buf, z_buf, w_buf, out_buf, load_sem, part_send, part_recv, ring_sems, swap_sems, norm_sems, fetch_sems, out_sems):
     place = Place()
     units = unit_list()
     chunks = -(-len(units) // 3)
     counts = [len(range(order, len(units), 3)) for order in range(3)]
+    wide_base = first_unit(1)
+    wide_units = UNITS_OF[1]
+    wide_half = wide_units * WIDTH
+    pieces = WIDTH // BLOCK
+    blocks = wide_units * BLOCKS_PER_UNIT
     partner = place.device(other_core=True)
     group_x = [(place.device({2: by}, other_core=swap)) for by in range(SIDE) for swap in (False, True) if by or swap]
     group_y = [place.device({1: by}) for by in range(1, SIDE)]
     group_z = [place.device({0: by}) for by in range(1, SIDE)]
+
+    def block_start(block):
+        unit = lax.div(block, BLOCKS_PER_UNIT)
+        mine = lax.rem(lax.div(block, pieces), 2)
+        owner = lax.rem(place.core + 1 + mine, 2)
+        start = owner * wide_half + unit * WIDTH + lax.rem(block, pieces) * BLOCK
+        return pl.multiple_of(start, BLOCK)
+
+    def fetch(block):
+        slot = lax.rem(block, 2)
+        start = block_start(block)
+        return (
+            pltpu.make_async_copy(z_one.at[:, pl.ds(start, BLOCK)], z_buf.at[slot], fetch_sems.at[0, slot]),
+            pltpu.make_async_copy(w_two.at[pl.ds(start, BLOCK), :], w_buf.at[slot], fetch_sems.at[1, slot]),
+        )
+
+    steady = (pltpu.make_async_copy(x_turned, x_buf, fetch_sems.at[2, 0]), pltpu.make_async_copy(dh_two, dh_buf, fetch_sems.at[2, 1]))
+    for copy in steady + fetch(0):
+        copy.start()
     enter(group_x + group_y + group_z)
 
     def source(mat, piece, core):
-        if mat in (1, 3):
-            ref = g_one if mat == 1 else g_three
+        if mat == 3:
             start = core * (UNITS_OF[mat] * WIDTH) + piece * WIDTH
-            return ref.at[:, :, :, :, pl.ds(pl.multiple_of(start, WIDTH), WIDTH)]
+            return g_three.at[:, :, :, :, pl.ds(pl.multiple_of(start, WIDTH), WIDTH)]
         ref = g_two if mat == 2 else g_four
         return ref.at[:, :, :, core, pl.ds(piece * ROWS, ROWS), :]
 
@@ -177,63 +234,109 @@
     def load(chunk):
         for order in range(3):
             unit = 3 * chunk + order
-            if unit >= len(units):
+            if unit >= wide_base:
                 continue
             mat, piece = units[unit]
             send(source(mat, piece, 1 - place.core), part.at[unit], part_send.at[unit], part_recv.at[unit], partner)
-            if chunk >= SLOTS:
-                rings[order][0].drain(unit - 3 * SLOTS)
-            pltpu.make_async_copy(source(mat, piece, place.core), own.at[order, chunk % SLOTS], load_sem.at[unit]).start()
+            pltpu.make_async_copy(source(mat, piece, place.core), own.at[order], load_sem.at[unit]).start()
+
+    def wide_block(block, carry):
+        slot = lax.rem(block, 2)
+
+        @pl.when(block + 1 < blocks)
+        def _():
+            for copy in fetch(block + 1):
+                copy.start()
+
+        for copy in fetch(block):
+            copy.wait()
+        da_one = lax.dot_general(dh_buf[...], w_buf[slot], (((1,), (1,)), ((), ())), preferred_element_type=jnp.float32).astype(jnp.bfloat16)
+        dz_one = (da_one.astype(jnp.float32) * gelu_slope(z_buf[slot])).astype(jnp.bfloat16)
+        grad = jnp.dot(x_buf[...], dz_one, preferred_element_type=jnp.float32)
+        grad = grad.reshape(SIDE, SIDE, SIDE, ROWS, BLOCK)
+        unit = lax.div(block, BLOCKS_PER_UNIT)
+        piece = lax.rem(block, pieces)
+        mine = lax.rem(lax.div(block, pieces), 2)
+        cols = pl.ds(pl.multiple_of(piece * BLOCK, BLOCK), BLOCK)
+
+        @pl.when(mine == 1)
+        def _():
+            wide_own[unit, :, :, :, :, cols] = grad
+
+        @pl.when(mine == 0)
+        def _():
+            @pl.when(unit > 0)
+            def _():
+                await_bytes(out_buf.at[piece], out_sems.at[piece])
+            out_buf[piece] = grad
+            send(out_buf.at[piece], part.at[wide_base + unit, :, :, :, :, cols], out_sems.at[piece], part_recv.at[wide_base + unit], partner)
+        return carry
 
     def stage_b(order, chunk, unit):
-        lead = (order, lax.rem(chunk, SLOTS))
-        await_bytes(own.at[lead], load_sem.at[unit])
         await_bytes(part.at[unit], part_recv.at[unit])
-        own[lead] = own[lead] + part[unit]
-        rings[order][0].start(own, lead, unit)
+
+        @pl.when(unit < wide_base)
+        def _():
+            await_bytes(own.at[order], load_sem.at[unit])
+            part[unit] = part[unit] + own[order]
+
+        @pl.when(unit >= wide_base)
+        def _():
+            part[unit] = part[unit] + wide_own[unit - wide_base]
+        rings[order][0].start(part, (unit,), unit)
 
     def stage_c(order, chunk, unit):
-        rings[order][0].pass_on(own, (order, lax.rem(chunk, SLOTS)), unit)
+        rings[order][0].pass_on(part, (unit,), unit)
 
     def stage_d(order, chunk, unit):
-        mid[unit] = rings[order][0].finish(own, (order, lax.rem(chunk, SLOTS)), unit)
-        rings[order][1].start(mid, (unit,), unit)
+        final1[unit, 0] = rings[order][0].finish(part, (unit,), unit)
+        rings[order][1].start(final1, (unit, 0), unit)
 
     def stage_e(order, chunk, unit):
-        rings[order][1].pass_on(mid, (unit,), unit)
+        rings[order][1].pass_on(final1, (unit, 0), unit)
 
     def stage_f(order, chunk, unit):
-        low[unit] = rings[order][1].finish(mid, (unit,), unit)
-        rings[order][2].start(low, (unit,), unit)
+        final2[unit, 0] = rings[order][1].finish(final1, (unit, 0), unit)
+        rings[order][2].start(final2, (unit, 0), unit)
 
     def stage_g(order, chunk, unit):
-        rings[order][2].pass_on(low, (unit,), unit)
+        rings[order][2].pass_on(final2, (unit, 0), unit)
 
     def stage_h(order, chunk, unit):
-        shard[unit] = rings[order][2].finish(low, (unit,), unit) * (1.0 / (2 * SIDE ** 3))
+        shard[unit] = rings[order][2].finish(final2, (unit, 0), unit) * (1.0 / (2 * SIDE ** 3))
 
     stages = (stage_b, stage_c, stage_d, stage_e, stage_f, stage_g, stage_h)
 
+    def run(now, lag):
+        chunk = now - lag - 1
+        for order in range(3):
+            @pl.when((chunk >= 0) & (chunk < counts[order]))
+            def _(order=order):
+                stages[lag](order, chunk, 3 * chunk + order)
+
+    load(0)
+    for copy in steady:
+        copy.wait()
+
     def turn(now, carry):
-        for chunk in range(chunks):
-            @pl.when(now == chunk)
-            def _(chunk=chunk):
-                load(chunk)
-        for lag, stage in enumerate(stages):
-            chunk = now - lag - 1
-            for order in range(3):
-                @pl.when((chunk >= 0) & (chunk < counts[order]))
-                def _(stage=stage, order=order, chunk=chunk):
-                    stage(order, chunk, 3 * chunk + order)
+        run(now, 0)
+        for chunk in range(1, chunks):
+            if 3 * chunk < wide_base:
+                @pl.when(now == chunk)
+                def _(chunk=chunk):
+                    load(chunk)
+        low = lax.min(now * BLOCKS_PER_TURN, blocks)
+        high = lax.min((now + 1) * BLOCKS_PER_TURN, blocks)
+        lax.fori_loop(low, high, wide_block, 0)
+        for lag in range(1, len(stages)):
+            run(now, lag)
         return carry
 
     lax.fori_loop(0, chunks + len(stages), turn, 0)
 
     n_three = UNITS_OF[3]
-    n_one = UNITS_OF[1]
-    base_one = first_unit(1)
     send(shard.at[pl.ds(0, n_three)], swapped.at[pl.ds(0, n_three)], swap_sems.at[0], swap_sems.at[1], partner)
-    send(shard.at[pl.ds(base_one, n_one)], swapped.at[pl.ds(n_three, n_one)], swap_sems.at[0], swap_sems.at[1], partner)
+    send(shard.at[pl.ds(wide_base, wide_units)], swapped.at[pl.ds(n_three, wide_units)], swap_sems.at[0], swap_sems.at[1], partner)
 
     def fold(unit, total):
         value = shard[unit]
@@ -259,34 +362,37 @@
     await_bytes(swapped, swap_sems.at[1])
     for level, (board, group, seat) in enumerate(levels):
         await_bytes(board.at[pl.ds(0, len(group))], norm_sems.at[0, level])
+    for piece in range(pieces):
+        await_bytes(out_buf.at[piece], out_sems.at[piece])
     for order in range(3):
         def tidy(chunk, carry, order=order):
             unit = 3 * chunk + order
-            await_bytes(part.at[unit], part_send.at[unit])
-            rings[order][1].drain(unit)
-            rings[order][2].drain(unit)
-
-            @pl.when(chunk >= counts[order] - SLOTS)
+            for ring in rings[order]:
+                ring.drain(unit)
+
+            @pl.when(unit < wide_base)
             def _():
-                rings[order][0].drain(unit)
+                await_bytes(part.at[unit], part_send.at[unit])
             return carry
 
         lax.fori_loop(0, counts[order], tidy, 0)
 
 
-def reduce_grads(g_one, g_two, g_three, g_four):
+def reduce_grads(wide_parts, g_two, g_three, g_four):
     n = len(unit_list())
     cube = (SIDE, SIDE, SIDE)
-    args = (
-        g_one.reshape(cube + (ROWS, 2 * UNITS_OF[1] * WIDTH)),
+    args = tuple(wide_parts) + (
         g_two.reshape(cube + (2, UNITS_OF[2] * ROWS, WIDTH)),
         g_three.reshape(cube + (ROWS, 2 * UNITS_OF[3] * WIDTH)),
         g_four.reshape(cube + (2, UNITS_OF[4] * ROWS, WIDTH)),
     )
-    f32 = jnp.float32
+    f32, bf16 = jnp.float32, jnp.bfloat16
     dma = pltpu.SemaphoreType.DMA
+    dim, rows = wide_parts[0].shape
+    model = wide_parts[1].shape[1]
     scratch = [
-        pltpu.VMEM((3, SLOTS) + cube + (ROWS, WIDTH), f32),
+        pltpu.VMEM((3,) + cube + (ROWS, WIDTH), f32),
+        pltpu.VMEM((UNITS_OF[1],) + cube + (ROWS, WIDTH), f32),
         pltpu.VMEM((n,) + cube + (ROWS, WIDTH), f32),
         pltpu.VMEM((n, 2, SIDE, SIDE, ROWS, WIDTH // 2), f32),
         pltpu.VMEM((n, 2, SIDE, SIDE, ROWS, WIDTH), f32),
@@ -294,13 +400,16 @@
         pltpu.VMEM((n, 2, SIDE, ROWS, WIDTH), f32),
         pltpu.VMEM((n, 2, ROWS, WIDTH // 2), f32),
         pltpu.VMEM((n, 2, ROWS, WIDTH), f32),
-        pltpu.VMEM((n, SIDE, SIDE, ROWS, WIDTH), f32),
-        pltpu.VMEM((n, SIDE, ROWS, WIDTH), f32),
         pltpu.VMEM((3, ROWS, 128), f32),
         pltpu.VMEM((2 * SIDE, ROWS, 128), f32),
         pltpu.VMEM((SIDE, ROWS, 128), f32),
         pltpu.VMEM((SIDE, ROWS, 128), f32),
-        dma((n,)), dma((n,)), dma((n,)), dma((3, 3, n)), dma((2,)), dma((2, 3)),
+        pltpu.VMEM((dim, rows), bf16),
+        pltpu.VMEM((rows, model), bf16),
+        pltpu.VMEM((2, rows, BLOCK), bf16),
+        pltpu.VMEM((2, BLOCK, model), bf16),
+        pltpu.VMEM((WIDTH // BLOCK,) + cube + (ROWS, BLOCK), f32),
+        dma((n,)), dma((n,)), dma((n,)), dma((3, 3, n)), dma((2,)), dma((2, 3)), dma((3, 2)), dma((WIDTH // BLOCK,)),
     ]
     any_spec = pl.BlockSpec(memory_space=pl.ANY)
     vmem_spec = pl.BlockSpec(memory_space=pltpu.VMEM)
@@ -311,7 +420,7 @@
             jax.ShapeDtypeStruct((UNITS_OF[3] + UNITS_OF[1], ROWS, WIDTH), f32),
             jax.ShapeDtypeStruct((ROWS, 128), f32),
         ),
-        in_specs=[any_spec] * 4,
+        in_specs=[any_spec] * len(args),
         out_specs=(vmem_spec,) * 3,
         scratch_shapes=scratch,
         compiler_params=pltpu.CompilerParams(collective_id=0, has_side_effects=True, vmem_limit_bytes=VMEM_BYTES),

time: 306 us -> 266 us (0.87)
  matrix products: 118 us -> 33.9 us
  Pallas kernels: 181 us -> 224 us
    dot_general x3 -> x0, matrix products: 73.2 us -> none  [the longest x1 31.2 us: local_grads(): jnp.einsum('rd,rw->dw', x_rows, dz_one, preferred_element_type=jnp.float32)]
    pallas_call x0 -> x1, Pallas kernels: none -> 29.8 us  [forward_wide(): pl.pallas_call(forward_kernel, grid=(wide // block,), out_shape=(jax.Shap...]
    pallas_call x1, Pallas kernels: 110 us -> 124 us  [reduce_grads(): pl.pallas_call(reduce_kernel, out_shape=(jax.ShapeDtypeStruct((n, ROWS, W...]
    dot_general x1, matrix products: 24.8 us -> 11.8 us  [local_grads(): jnp.einsum('rw,rd->wd', a_one, dh_two, preferred_element_type=jnp.float32)]
where the time goes in v2:
time: 266 us; the launch traced here: 265 us
  Pallas kernels  224 us (84%)
  matrix products  33.9 us (13%)
  local copies, waits for them, and re-layouts  4.58 us (2%)
    pallas_call x1, Pallas kernels, reduce_grads(): pl.pallas_call(reduce_kernel, out_shape=(jax.ShapeDtypeStruct((n, ROWS, W...  124 us
    pallas_call x1, Pallas kernels, gather_rows(): pl.pallas_call(gather_kernel, out_shape=(full, full), in_specs=[vmem_spec...  60.7 us
    pallas_call x1, Pallas kernels, forward_wide(): pl.pallas_call(forward_kernel, grid=(wide // block,), out_shape=(jax.Shap...  29.8 us
    dot_general x1, matrix products, local_grads(): jnp.einsum('rw,rd->wd', a_one, dh_two, preferred_element_type=jnp.float32)  11.8 us
    pallas_call x1, Pallas kernels, place_weights(): pl.pallas_call(place_kernel, out_shape=(jax.ShapeDtypeStruct(cube + (ROWS...  7.42 us
    dot_general x1, matrix products, local_grads(): jnp.einsum('rf,rd->fd', a_three, dy_rows, preferred_element_type=jnp.floa...  5.68 us

profile of v2, /device:TPU:1, one launch (start us, length us, event | category | flops | bytes accessed | tf_op | source)
XLA Modules:
  0.0 265.0 jit_solution(1733360810845633889)
XLA Ops:
  0.7 0.0 copy-start
  0.7 29.8 %forward_wide.1 = (bf16[1024,8192]{1,0:T(8,128)(2,1)}, bf16[1024,8192]{1,0:T(8,128)(2,1)}, bf16[1024,512]{1,0:T(8,128)(2,1)}) custom-call(bf16[1024,512]{1,0:T(8,128)(2,1)} %x_ref.1, bf16[512,8192]{1,0:T(8,128)(2,1)} %w_one.1, bf16[8192,512]{1,0:T(8,128)(2,1)} %w_two.3), custom_call_target="tpu_custom_call" | custom-call | tf_op jit(solution)/shard_map/forward_wide/pallas_call | solution.py:69
  30.4 0.0 copy-start.8
  30.4 4.4 %convolution_convert_fusion = bf16[1024,2048]{1,0:T(8,128)(2,1)S(1)} fusion(bf16[1024,512]{1,0:T(8,128)(2,1)} %get-tuple-element.44, bf16[512,2048]{1,0:T(8,128)(2,1)} %param.24), kind=kOutput, calls=%fused_computation.16 | convolution fusion | flops 2149580800 | bytes 7340032 | tf_op jit(solution)/shard_map/dot_general | solution.py:83
  34.9 0.0 copy-start.10
  34.9 0.0 copy-start.6
  34.9 0.0 slice-start.1
  34.9 5.3 %fusion.5 = bf16[1024,2048]{1,0:T(8,128)(2,1)S(1)} fusion(bf16[1024,2048]{1,0:T(8,128)(2,1)S(1)} %convolution_convert_fusion, bf16[1024,512]{1,0:T(8,128)(2,1)S(1)} %copy-done, bf16[2048,512]{1,0:T(8,128)(2,1)S(1)} %copy-done.8), kind=kOutput, calls=%fused_computation.10 | convolution fusion | flops 2174746624 | bytes 11534336 | tf_op jit(solution)/shard_map/rd,fd->rf/dot_general | solution.py:86
  40.2 0.0 copy-start.9
  40.3 4.4 %fusion.15 = f32[512,2048]{1,0:T(8,128)} fusion(bf16[1024,512]{1,0:T(8,128)(2,1)S(1)} %copy-done.6, bf16[1024,2048]{1,0:T(8,128)(2,1)S(1)} %fusion.5), kind=kOutput, calls=%fused_computation.20 | convolution fusion | flops 2147483648 | bytes 9437184 | tf_op jit(solution)/shard_map/rd,rf->df/dot_general | solution.py:88
  44.7 2.4 convolution_convert_fusion.1.dh_two
  47.0 0.0 copy-start.7
  47.1 11.8 %fusion.14 = f32[8192,512]{1,0:T(8,128)} fusion(bf16[1024,8192]{1,0:T(8,128)(2,1)S(1)} %bitcast.29, bf16[1024,512]{1,0:T(8,128)(2,1)S(1)} %convolution_convert_fusion.1.dh_two), kind=kOutput, calls=%fused_computation.19 | convolution fusion | flops 8589934592 | bytes 34603008 | tf_op jit(solution)/shard_map/rw,rd->wd/dot_general | solution.py:90
  58.9 5.7 %fusion.9 = f32[2048,512]{1,0:T(8,128)} fusion(bf16[1024,512]{1,0:T(8,128)(2,1)S(1)} %copy-done, bf16[1024,2048]{1,0:T(8,128)(2,1)} %copy-done.10), kind=kOutput, calls=%fused_computation.14 | convolution fusion | flops 2160066560 | bytes 9437184 | tf_op jit(solution)/shard_map/rf,rd->fd/dot_general | solution.py:85
  64.6 1.3 copy.37
  65.9 123.7 %reduce_grads.1 = (f32[20,8,512]{2,1,0:T(8,128)}, f32[10,8,512]{2,1,0:T(8,128)}, f32[8,128]{1,0:T(8,128)}) custom-call(bf16[512,1024]{1,0:T(8,128)(2,1)} %bitcast.27, bf16[1024,512]{1,0:T(8,128)(2,1)} %copy-done.7, bf16[1024,8192]{1,0:T(8,128)(2,1)} %get-tuple-element.45.z_one, bf16[8192,512]{1,0:T(8,128)(2,1)} %w_two.3, f32[4,4,4,2,64,512]{5,4,3,2,1,0:T(8,128)} %bitcast.24, ...), custom_call_target="tpu_custom_call" | custom-call | tf_op jit(solution)/shard_map/reduce_grads/pallas_call | solution.py:416
  190.8 2.7 %adam_update.1 = (f32[4,8192]{1,0:T(4,128)}, f32[64,512]{1,0:T(8,128)}, f32[4,2048]{1,0:T(4,128)}, f32[16,512]{1,0:T(8,128)}, f32[4,8192]{1,0:T(4,128)}, /*index...) custom-call(f32[1,1]{1,0:T(1,128)} %bitcast.22.lr_ref, ...), custom_call_target="tpu_custom_call" | custom-call | tf_op jit(solution)/shard_map/adam_update/pallas_call | solution.py:475
  193.5 0.0 copy-start.1
  193.5 0.9 copy-done.1
  194.4 0.8 copy-done.2
  195.3 0.8 copy-done.3
  196.0 0.7 copy-done.4
  196.8 60.7 %gather_rows.1 = (bf16[20,4,4,4,8,512]{5,4,3,2,1,0:T(8,128)(2,1)S(1)}, bf16[20,4,4,4,8,512]{5,4,3,2,1,0:T(8,128)(2,1)S(1)}) custom-call(f32[4,8192]{1,0:T(4,128)S(1)} %copy-done.1, f32[4,2048]{1,0:T(4,128)S(1)} %copy-done.3, bf16[8,8,512]{2,1,0:T(8,128)(2,1)S(1)} %copy-done.2, bf16[2,8,512]{2,1,0:T(8,128)(2,1)S(1)} %copy-done.4), custom_call_target="tpu_custom_call" | custom-call | tf_op jit(solution)/shard_map/gather_rows/pallas_call | solution.py:595
  257.4 7.4 %place_weights.1 = (bf16[4,4,4,8,8192]{4,3,2,1,0:T(8,128)(2,1)}, bf16[4,4,4,2,64,512]{5,4,3,2,1,0:T(8,128)(2,1)}, bf16[4,4,4,8,2048]{4,3,2,1,0:T(8,128)(2,1)}, bf16[4,4,4,2,16,512]{5,4,3,2,1,0:T(8,128)(2,1)}) custom-call(bf16[20,4,4,4,8,512]{5,4,3,2,1,0:T(8,128)(2,1)S(1)} %get-tuple-element.54.board, bf16[20,4,4,4,8,512]{5,4,3,2,1,0:T(8,128)(2,1)S(1)} %get-tuple-element.55.other), custom_call_target="tpu_custom_call" | custom-call | tf_op jit(solution)/shard_map/place_weights/pallas_call | solution.py:634
  (19 shorter events, 0.0 us)
Async XLA Ops:
  0.7 34.2 %copy-start = (bf16[1024,512]{1,0:T(8,128)(2,1)S(1)}, bf16[1024,512]{1,0:T(8,128)(2,1)}, u32[]{:S(2)}) copy-start(bf16[1024,512]{1,0:T(8,128)(2,1)} %param.21) | copy-start | bytes 3145732
  30.4 4.4 %copy-start.8 = (bf16[2048,512]{1,0:T(8,128)(2,1)S(1)}, bf16[2048,512]{1,0:T(8,128)(2,1)}, u32[]{:S(2)}) copy-start(bf16[2048,512]{1,0:T(8,128)(2,1)} %param.25) | copy-start | bytes 6291460
  34.9 5.4 %copy-start.10 = (bf16[1024,2048]{1,0:T(8,128)(2,1)}, bf16[1024,2048]{1,0:T(8,128)(2,1)S(1)}, u32[]{:S(2)}) copy-start(bf16[1024,2048]{1,0:T(8,128)(2,1)S(1)} %convolution_convert_fusion) | copy-start | bytes 12582916
  34.9 5.4 %copy-start.6 = (bf16[1024,512]{1,0:T(8,128)(2,1)S(1)}, bf16[1024,512]{1,0:T(8,128)(2,1)}, u32[]{:S(2)}) copy-start(bf16[1024,512]{1,0:T(8,128)(2,1)} %get-tuple-element.44) | copy-start | bytes 3145732
  34.9 12.2 %slice-start = ((s8[16777216]{0:T(1024)(128)(4,1)}), s8[4194304]{0:T(1024)(128)(4,1)S(1)}, s32[]{:S(2)}) async-start(s8[16777216]{0:T(1024)(128)(4,1)} %bitcast.28), calls=%async_computation | async-start | bytes 8388608
  34.9 12.2 %slice-start.1 = ((s8[16777216]{0:T(1024)(128)(4,1)}), s8[4194304]{0:T(1024)(128)(4,1)S(1)}, s32[]{:S(2)}) async-start(s8[16777216]{0:T(1024)(128)(4,1)} %bitcast.28), calls=%async_computation.1 | async-start | bytes 8388608
  34.9 12.2 %slice-start.2 = ((s8[16777216]{0:T(1024)(128)(4,1)}), s8[4194304]{0:T(1024)(128)(4,1)S(1)}, s32[]{:S(2)}) async-start(s8[16777216]{0:T(1024)(128)(4,1)} %bitcast.28), calls=%async_computation.2 | async-start | bytes 8388608
  40.2 4.4 %copy-start.9 = (bf16[512,2048]{1,0:T(8,128)(2,1)S(1)}, bf16[512,2048]{1,0:T(8,128)(2,1)}, u32[]{:S(2)}) copy-start(bf16[512,2048]{1,0:T(8,128)(2,1)} %param.24) | copy-start | bytes 6291460
  40.3 6.8 %slice-start.3 = ((s8[16777216]{0:T(1024)(128)(4,1)}), s8[4194304]{0:T(1024)(128)(4,1)S(1)}, s32[]{:S(2)}) async-start(s8[16777216]{0:T(1024)(128)(4,1)} %bitcast.28), calls=%async_computation.3 | async-start | bytes 8388608
  47.0 11.8 %copy-start.7 = (bf16[1024,512]{1,0:T(8,128)(2,1)}, bf16[1024,512]{1,0:T(8,128)(2,1)S(1)}, u32[]{:S(2)}) copy-start(bf16[1024,512]{1,0:T(8,128)(2,1)S(1)} %convolution_convert_fusion.1.dh_two) | copy-start | bytes 3145732
  58.9 5.7 %copy-start.5 = (bf16[1024,512]{1,0:T(8,128)(2,1)S(1)}, bf16[1024,512]{1,0:T(8,128)(2,1)}, u32[]{:S(2)}) copy-start(bf16[1024,512]{1,0:T(8,128)(2,1)} %x_ref.1) | copy-start | bytes 3145732
  193.5 0.9 copy-start.1
  194.4 0.8 copy-start.2
  195.3 0.8 copy-start.3
  196.0 0.7 copy-start.4

commit v3 on v2

--- a/solution.py
+++ b/solution.py
@@ -43,12 +43,13 @@
     return 0.5 * (1.0 + lax.erf(pre_wide * INV_SQRT2)) + pre_wide * INV_SQRT2PI * jnp.exp(-0.5 * pre_wide * pre_wide)
 
 
-def forward_kernel(x_ref, w_one, w_two, z_out, a_out, h_out, total):
+def forward_kernel(x_ref, w_one, w_two, z_out, a_out, h_out, x_turned, total):
     step = pl.program_id(0)
 
     @pl.when(step == 0)
     def _():
         total[...] = jnp.zeros_like(total)
+        x_turned[...] = x_ref[...].T
 
     z_one = jnp.dot(x_ref[...], w_one[...], preferred_element_type=jnp.float32).astype(jnp.bfloat16)
     z_out[...] = z_one
@@ -69,26 +70,61 @@
     return pl.pallas_call(
         forward_kernel,
         grid=(wide // block,),
-        out_shape=(jax.ShapeDtypeStruct((rows, wide), bf16), jax.ShapeDtypeStruct((rows, wide), bf16), jax.ShapeDtypeStruct((rows, dim), bf16)),
+        out_shape=(jax.ShapeDtypeStruct((rows, wide), bf16), jax.ShapeDtypeStruct((rows, wide), bf16), jax.ShapeDtypeStruct((rows, dim), bf16), jax.ShapeDtypeStruct((dim, rows), bf16)),
         in_specs=[pl.BlockSpec((rows, dim), lambda i: (0, 0)), pl.BlockSpec((dim, block), lambda i: (0, i)), pl.BlockSpec((block, dim), lambda i: (i, 0))],
-        out_specs=(pl.BlockSpec((rows, block), lambda i: (0, i)), pl.BlockSpec((rows, block), lambda i: (0, i)), pl.BlockSpec((rows, dim), lambda i: (0, 0))),
+        out_specs=(pl.BlockSpec((rows, block), lambda i: (0, i)), pl.BlockSpec((rows, block), lambda i: (0, i)), pl.BlockSpec((rows, dim), lambda i: (0, 0)), pl.BlockSpec((dim, rows), lambda i: (0, 0))),
         scratch_shapes=[pltpu.VMEM((rows, dim), jnp.float32)],
         compiler_params=pltpu.CompilerParams(vmem_limit_bytes=VMEM_BYTES),
         name='forward_wide',
     )(x_rows, w_one, w_two)
 
 
+def middle_kernel(h_ref, dy_ref, w_three, w_four, g_three, g_four, dh_out, total, h_turned):
+    step = pl.program_id(0)
+    f32, bf16 = jnp.float32, jnp.bfloat16
+
+    @pl.when(step == 0)
+    def _():
+        total[...] = jnp.zeros_like(total)
+        h_turned[...] = h_ref[...].T
+
+    z_three = jnp.dot(h_ref[...], w_three[...], preferred_element_type=f32).astype(bf16)
+    a_three = gelu_value(z_three).astype(bf16)
+    da_three = lax.dot_general(dy_ref[...], w_four[...], (((1,), (1,)), ((), ())), preferred_element_type=f32).astype(bf16)
+    dz_three = (da_three.astype(f32) * gelu_slope(z_three)).astype(bf16)
+    g_four[...] = lax.dot_general(a_three, dy_ref[...], (((0,), (0,)), ((), ())), preferred_element_type=f32)
+    g_three[...] = jnp.dot(h_turned[...], dz_three, preferred_element_type=f32)
+    total[...] += lax.dot_general(dz_three, w_three[...], (((1,), (1,)), ((), ())), preferred_element_type=f32)
+
+    @pl.when(step == pl.num_programs(0) - 1)
+    def _():
+        dh_out[...] = total[...].astype(bf16)
+
+
+def middle(h_two, dy_rows, w_three, w_four):
+    rows, dim = h_two.shape
+    wide = w_three.shape[1]
+    block = 512
+    f32, bf16 = jnp.float32, jnp.bfloat16
+    whole = pl.BlockSpec((rows, dim), lambda i: (0, 0))
+    across, down = pl.BlockSpec((dim, block), lambda i: (0, i)), pl.BlockSpec((block, dim), lambda i: (i, 0))
+    return pl.pallas_call(
+        middle_kernel,
+        grid=(wide // block,),
+        out_shape=(jax.ShapeDtypeStruct((dim, wide), f32), jax.ShapeDtypeStruct((wide, dim), f32), jax.ShapeDtypeStruct((rows, dim), bf16)),
+        in_specs=[whole, whole, across, down],
+        out_specs=(across, down, whole),
+        scratch_shapes=[pltpu.VMEM((rows, dim), f32), pltpu.VMEM((dim, rows), bf16)],
+        compiler_params=pltpu.CompilerParams(vmem_limit_bytes=VMEM_BYTES),
+        name='middle',
+    )(h_two, dy_rows, w_three, w_four)
+
+
 def local_grads(x_rows, dy_rows, w_one, w_two, w_three, w_four):
-    z_one, a_one, h_two = forward_wide(x_rows, w_one, w_two)
-    z_three = jnp.dot(h_two, w_three, preferred_element_type=jnp.float32).astype(jnp.bfloat16)
-    a_three = gelu_value(z_three).astype(jnp.bfloat16)
-    g_four = jnp.einsum('rf,rd->fd', a_three, dy_rows, preferred_element_type=jnp.float32)
-    da_three = jnp.einsum('rd,fd->rf', dy_rows, w_four, preferred_element_type=jnp.float32).astype(jnp.bfloat16)
-    dz_three = (da_three.astype(jnp.float32) * gelu_slope(z_three)).astype(jnp.bfloat16)
-    g_three = jnp.einsum('rd,rf->df', h_two, dz_three, preferred_element_type=jnp.float32)
-    dh_two = jnp.einsum('rf,df->rd', dz_three, w_three, preferred_element_type=jnp.float32).astype(jnp.bfloat16)
+    z_one, a_one, h_two, x_turned = forward_wide(x_rows, w_one, w_two)
+    g_three, g_four, dh_two = middle(h_two, dy_rows, w_three, w_four)
     g_two = jnp.einsum('rw,rd->wd', a_one, dh_two, preferred_element_type=jnp.float32)
-    return (x_rows.T, dh_two, z_one, w_two), g_two, g_three, g_four
+    return (x_turned, dh_two, z_one, w_two), g_two, g_three, g_four
 
 
 class Place:
@@ -177,7 +213,7 @@
 
 BLOCK = 256
 BLOCKS_PER_UNIT = 2 * (WIDTH // BLOCK)
-BLOCKS_PER_TURN = 6
+BLOCKS_AFTER = (2, 2, 1)
 
 
 def reduce_kernel(x_turned, dh_two, z_one, w_two, g_two, g_three, g_four, shard, swapped, norm_tile, own, wide_own, part, relay1, final1, relay2, final2, relay3, final3, norm_own, norm_a, norm_b, norm_c, x_buf, dh_buf, z_buf, w_buf, out_buf, load_sem, part_send, part_recv, ring_sems, swap_sems, norm_sems, fetch_sems, out_sems):
@@ -314,9 +350,14 @@
             def _(order=order):
                 stages[lag](order, chunk, 3 * chunk + order)
 
+    def wide_blocks(low, count):
+        lax.fori_loop(lax.min(low, blocks), lax.min(low + count, blocks), wide_block, 0)
+
     load(0)
     for copy in steady:
         copy.wait()
+    first_blocks = 6
+    wide_blocks(0, first_blocks)
 
     def turn(now, carry):
         run(now, 0)
@@ -325,14 +366,15 @@
                 @pl.when(now == chunk)
                 def _(chunk=chunk):
                     load(chunk)
-        low = lax.min(now * BLOCKS_PER_TURN, blocks)
-        high = lax.min((now + 1) * BLOCKS_PER_TURN, blocks)
-        lax.fori_loop(low, high, wide_block, 0)
+        done = first_blocks + (now - 1) * sum(BLOCKS_AFTER)
         for lag in range(1, len(stages)):
+            if lag <= len(BLOCKS_AFTER):
+                wide_blocks(done, BLOCKS_AFTER[lag - 1])
+                done = done + BLOCKS_AFTER[lag - 1]
             run(now, lag)
         return carry
 
-    lax.fori_loop(0, chunks + len(stages), turn, 0)
+    lax.fori_loop(1, chunks + len(stages), turn, 0)
 
     n_three = UNITS_OF[3]
     send(shard.at[pl.ds(0, n_three)], swapped.at[pl.ds(0, n_three)], swap_sems.at[0], swap_sems.at[1], partner)
@@ -515,30 +557,35 @@
         await_bytes(self.blocks(unit, 3), self.send_sem.at[unit])
 
 
-def gather_kernel(one_rows, three_rows, two_rows, four_rows, board, other, swap_one, swap_three, ring_sems, pair_sems, swap_sems):
+def gather_kernel(one_rows, three_rows, two_rows, four_rows, board, other, own_one, own_three, swap_one, swap_three, ring_sems, pair_sems, swap_sems, load_sems):
     place = Place()
     units = unit_list()
     chunks = -(-len(units) // 3)
     counts = [len(range(order, len(units), 3)) for order in range(3)]
     partner = place.device(other_core=True)
     here = tuple(place.coords)
+    splits = ((1, one_rows, own_one, swap_one), (3, three_rows, own_three, swap_three))
+    loads = []
+    for index, (mat, rows, mine, landing) in enumerate(splits):
+        span = UNITS_OF[mat] * WIDTH
+        loads.append(pltpu.make_async_copy(rows.at[:, pl.ds(pl.multiple_of(place.core * span, WIDTH), span)], mine, load_sems.at[index]))
+    for index, (mat, rows) in enumerate(((2, two_rows), (4, four_rows))):
+        loads.append(pltpu.make_async_copy(rows, board.at[(pl.ds(first_unit(mat), UNITS_OF[mat]),) + here], load_sems.at[2 + index]))
+    for copy in loads:
+        copy.start()
     enter(place.neighbours())
-    splits = ((1, one_rows, swap_one), (3, three_rows, swap_three))
-    for index, (mat, rows, landing) in enumerate(splits):
+    for index, (mat, rows, mine, landing) in enumerate(splits):
         span = UNITS_OF[mat] * WIDTH
         theirs = rows.at[:, pl.ds(pl.multiple_of((1 - place.core) * span, WIDTH), span)]
         send(theirs, landing, swap_sems.at[0, index], swap_sems.at[1, index], partner)
-    for mat, rows in ((2, two_rows), (4, four_rows)):
-        for piece in range(UNITS_OF[mat]):
-            board[(first_unit(mat) + piece,) + here] = rows[piece]
-    for index, (mat, rows, landing) in enumerate(splits):
+    for copy in loads:
+        copy.wait()
+    for index, (mat, rows, mine, landing) in enumerate(splits):
         await_bytes(landing, swap_sems.at[1, index])
         for piece in range(UNITS_OF[mat]):
-            start = place.core * (UNITS_OF[mat] * WIDTH) + piece * WIDTH
-            mine = rows[:, pl.ds(pl.multiple_of(start, WIDTH), WIDTH)]
-            theirs = landing[:, piece * WIDTH:(piece + 1) * WIDTH]
-            top = jnp.where(place.core == 0, mine, theirs)
-            bottom = jnp.where(place.core == 0, theirs, mine)
+            cols = slice(piece * WIDTH, (piece + 1) * WIDTH)
+            top = jnp.where(place.core == 0, mine[:, cols], landing[:, cols])
+            bottom = jnp.where(place.core == 0, landing[:, cols], mine[:, cols])
             board[(first_unit(mat) + piece,) + here] = jnp.concatenate([top, bottom], axis=0).astype(board.dtype)
 
     rings = []
@@ -546,42 +593,37 @@
         axes = (order + 2) % 3, (order + 1) % 3, order
         rings.append([RingSpread(place, axis, axes[:level], board, ring_sems.at[level, 0], ring_sems.at[level, 1], ring_sems.at[level, 2]) for level, axis in enumerate(axes)])
 
-    def every(action):
-        def turn(chunk, carry):
-            for order in range(3):
-                @pl.when(chunk < counts[order])
-                def _(order=order):
-                    action(order, 3 * chunk + order)
-            return carry
-
-        lax.fori_loop(0, chunks, turn, 0)
-
-    def begin(order, unit):
-        rings[order][0].start(unit)
-
-    every(begin)
-    for level in range(3):
-        def pass_on(order, unit, level=level):
-            rings[order][level].pass_on(unit)
-
-        def onward(order, unit, level=level):
-            rings[order][level].finish(unit)
-            if level < 2:
-                rings[order][level + 1].start(unit)
-            else:
-                send(board.at[unit], other.at[unit], pair_sems.at[0, unit], pair_sems.at[1, unit], partner)
-
-        every(pass_on)
-        every(onward)
-
-    def tidy(order, unit):
+    def begin(order, unit, level):
+        if level:
+            rings[order][level - 1].finish(unit)
+        rings[order][level].start(unit)
+
+    def pass_on(order, unit, level):
+        rings[order][level].pass_on(unit)
+
+    def hand_over(order, unit, level):
+        rings[order][level].finish(unit)
+        send(board.at[unit], other.at[unit], pair_sems.at[0, unit], pair_sems.at[1, unit], partner)
+
+    def tidy(order, unit, level):
         await_bytes(other.at[unit], pair_sems.at[1, unit])
         await_bytes(board.at[unit], pair_sems.at[0, unit])
-        for level in range(3):
-            rings[order][level].drain(unit)
-
-    every(tidy)
-    for index, (mat, rows, landing) in enumerate(splits):
+        for ring in rings[order]:
+            ring.drain(unit)
+
+    stages = ((begin, 0), (pass_on, 0), (begin, 1), (pass_on, 1), (begin, 2), (pass_on, 2), (hand_over, 2), (tidy, 2))
+
+    def turn(now, carry):
+        for lag, (stage, level) in enumerate(stages):
+            chunk = now - lag
+            for order in range(3):
+                @pl.when((chunk >= 0) & (chunk < counts[order]))
+                def _(stage=stage, level=level, chunk=chunk, order=order):
+                    stage(order, 3 * chunk + order, level)
+        return carry
+
+    lax.fori_loop(0, chunks + len(stages) - 1, turn, 0)
+    for index, (mat, rows, mine, landing) in enumerate(splits):
         await_bytes(landing, swap_sems.at[0, index])
 
 
@@ -595,12 +637,14 @@
     return pl.pallas_call(
         gather_kernel,
         out_shape=(full, full),
-        in_specs=[vmem_spec] * 4,
+        in_specs=[pl.BlockSpec(memory_space=pltpu.HBM)] * 4,
         out_specs=(vmem_spec, vmem_spec),
         scratch_shapes=[
             pltpu.VMEM((ROWS // 2, UNITS_OF[1] * WIDTH), f32),
             pltpu.VMEM((ROWS // 2, UNITS_OF[3] * WIDTH), f32),
-            dma((3, 3, n)), dma((2, n)), dma((2, 2)),
+            pltpu.VMEM((ROWS // 2, UNITS_OF[1] * WIDTH), f32),
+            pltpu.VMEM((ROWS // 2, UNITS_OF[3] * WIDTH), f32),
+            dma((3, 3, n)), dma((2, n)), dma((2, 2)), dma((4,)),
         ],
         compiler_params=pltpu.CompilerParams(collective_id=1, has_side_effects=True, vmem_limit_bytes=32 * 1024 * 1024),
         name='gather_rows',

time: 266 us -> 256 us (0.962)
  matrix products: 33.9 us -> 16 us
  Pallas kernels: 224 us -> 234 us
    dot_general x5 -> x0, matrix products: 22.1 us -> none  [the longest x1 5.68 us: local_grads(): jnp.einsum('rf,rd->fd', a_three, dy_rows, preferred_element_type=jnp.floa...]
    pallas_call x1 -> x2, Pallas kernels: 60.7 us -> 75.5 us  [the longest x1 57.6 us: gather_rows(): pl.pallas_call(gather_kernel, out_shape=(full, full), in_specs=[pl.BlockS...]
    pallas_call x1, Pallas kernels: 124 us -> 118 us  [reduce_grads(): pl.pallas_call(reduce_kernel, out_shape=(jax.ShapeDtypeStruct((n, ROWS, W...]
    dot_general x1, matrix products: 11.8 us -> 16 us  [local_grads(): jnp.einsum('rw,rd->wd', a_one, dh_two, preferred_element_type=jnp.float32)]
where the time goes in v3:
time: 256 us; the launch traced here: 255 us
  Pallas kernels  234 us (91%)
  matrix products  16 us (6%)
  local copies, waits for them, and re-layouts  3.21 us (1%)
    pallas_call x1, Pallas kernels, reduce_grads(): pl.pallas_call(reduce_kernel, out_shape=(jax.ShapeDtypeStruct((n, ROWS, W...  118 us
    pallas_call x1, Pallas kernels, gather_rows(): pl.pallas_call(gather_kernel, out_shape=(full, full), in_specs=[pl.BlockS...  57.6 us
    pallas_call x1, Pallas kernels, forward_wide(): pl.pallas_call(forward_kernel, grid=(wide // block,), out_shape=(jax.Shap...  30.3 us
    pallas_call x1, Pallas kernels, middle(): pl.pallas_call(middle_kernel, grid=(wide // block,), out_shape=(jax.Shape...  17.9 us
    dot_general x1, matrix products, local_grads(): jnp.einsum('rw,rd->wd', a_one, dh_two, preferred_element_type=jnp.float32)  16 us
    pallas_call x1, Pallas kernels, place_weights(): pl.pallas_call(place_kernel, out_shape=(jax.ShapeDtypeStruct(cube + (ROWS...  7.42 us

profile of v3, /device:TPU:1, one launch (start us, length us, event | category | flops | bytes accessed | tf_op | source)
XLA Modules:
  0.0 255.1 jit_solution(12740029532984566876)
XLA Ops:
  0.7 30.3 %forward_wide.1 = (bf16[1024,8192]{1,0:T(8,128)(2,1)}, bf16[1024,8192]{1,0:T(8,128)(2,1)}, bf16[1024,512]{1,0:T(8,128)(2,1)}, bf16[512,1024]{1,0:T(8,128)(2,1)}) custom-call(bf16[1024,512]{1,0:T(8,128)(2,1)} %x_ref.1, bf16[512,8192]{1,0:T(8,128)(2,1)} %w_one.1, bf16[8192,512]{1,0:T(8,128)(2,1)} %w_two.3), custom_call_target="tpu_custom_call" | custom-call | tf_op jit(solution)/shard_map/forward_wide/pallas_call | solution.py:70
  31.0 17.9 %middle.1 = (f32[512,2048]{1,0:T(8,128)}, f32[2048,512]{1,0:T(8,128)}, bf16[1024,512]{1,0:T(8,128)(2,1)}) custom-call(bf16[1024,512]{1,0:T(8,128)(2,1)} %get-tuple-element.49.h_ref, bf16[1024,512]{1,0:T(8,128)(2,1)} %dy_ref.1, bf16[512,2048]{1,0:T(8,128)(2,1)} %w_three.1, bf16[2048,512]{1,0:T(8,128)(2,1)} %w_four.1), custom_call_target="tpu_custom_call" | custom-call | tf_op jit(solution)/shard_map/middle/pallas_call | solution.py:111
  48.9 16.0 %fusion = f32[8192,512]{1,0:T(8,128)} fusion(bf16[1024,8192]{1,0:T(8,128)(2,1)} %get-tuple-element.52, bf16[1024,512]{1,0:T(8,128)(2,1)} %get-tuple-element.50.dh_two), kind=kOutput, calls=%fused_computation | convolution fusion | flops 8589934592 | bytes 34603008 | tf_op jit(solution)/shard_map/rw,rd->wd/dot_general | solution.py:126
  64.9 117.7 %reduce_grads.1 = (f32[20,8,512]{2,1,0:T(8,128)}, f32[10,8,512]{2,1,0:T(8,128)}, f32[8,128]{1,0:T(8,128)}) custom-call(bf16[512,1024]{1,0:T(8,128)(2,1)} %get-tuple-element.48.x_turned, bf16[1024,512]{1,0:T(8,128)(2,1)} %get-tuple-element.50.dh_two, bf16[1024,8192]{1,0:T(8,128)(2,1)} %get-tuple-element.51.z_one, bf16[8192,512]{1,0:T(8,128)(2,1)} %w_two.3, ...), custom_call_target="tpu_custom_call" | custom-call | tf_op jit(solution)/shard_map/reduce_grads/pallas_call | solution.py:458
  183.9 2.7 %adam_update.1 = (f32[4,8192]{1,0:T(4,128)}, f32[64,512]{1,0:T(8,128)}, f32[4,2048]{1,0:T(4,128)}, f32[16,512]{1,0:T(8,128)}, f32[4,8192]{1,0:T(4,128)}, /*index...) custom-call(f32[1,1]{1,0:T(1,128)} %bitcast.12.lr_ref, ...), custom_call_target="tpu_custom_call" | custom-call | tf_op jit(solution)/shard_map/adam_update/pallas_call | solution.py:517
  186.6 0.0 copy-start
  186.6 0.9 copy-done
  187.5 0.0 copy-start.1
  187.5 0.8 copy-done.1
  188.4 0.0 copy-start.2
  188.4 0.8 copy-done.2
  189.1 0.0 copy-start.3
  189.1 0.7 copy-done.3
  189.9 57.6 %gather_rows.1 = (bf16[20,4,4,4,8,512]{5,4,3,2,1,0:T(8,128)(2,1)S(1)}, bf16[20,4,4,4,8,512]{5,4,3,2,1,0:T(8,128)(2,1)S(1)}) custom-call(f32[4,8192]{1,0:T(4,128)S(1)} %copy-done, f32[4,2048]{1,0:T(4,128)S(1)} %copy-done.2, bf16[8,8,512]{2,1,0:T(8,128)(2,1)S(1)} %copy-done.1, bf16[2,8,512]{2,1,0:T(8,128)(2,1)S(1)} %copy-done.3), custom_call_target="tpu_custom_call" | custom-call | tf_op jit(solution)/shard_map/gather_rows/pallas_call | solution.py:637
  247.5 7.4 %place_weights.1 = (bf16[4,4,4,8,8192]{4,3,2,1,0:T(8,128)(2,1)}, bf16[4,4,4,2,64,512]{5,4,3,2,1,0:T(8,128)(2,1)}, bf16[4,4,4,8,2048]{4,3,2,1,0:T(8,128)(2,1)}, bf16[4,4,4,2,16,512]{5,4,3,2,1,0:T(8,128)(2,1)}) custom-call(bf16[20,4,4,4,8,512]{5,4,3,2,1,0:T(8,128)(2,1)S(1)} %get-tuple-element.62.board, bf16[20,4,4,4,8,512]{5,4,3,2,1,0:T(8,128)(2,1)S(1)} %get-tuple-element.63.other), custom_call_target="tpu_custom_call" | custom-call | tf_op jit(solution)/shard_map/place_weights/pallas_call | solution.py:678
Async XLA Ops:
  186.6 0.9 copy-start
  187.5 0.8 copy-start.1
  188.4 0.8 copy-start.2
  189.1 0.7 copy-start.3

commit v4 on v3

--- a/solution.py
+++ b/solution.py
@@ -22,11 +22,14 @@
 ROWS = 8
 UNITS_OF = {3: 2, 4: 2, 2: 8, 1: 8}
 MESH_ID = pl.DeviceIdType.MESH
+BY_COLUMNS = (((1,), (1,)), ((), ()))
+BY_ROWS = (((0,), (0,)), ((), ()))
 VMEM_BYTES = 62 * 1024 * 1024
+ADAM_VMEM = 8 * 1024 * 1024
 
 
 def unit_list():
-    return [(mat, piece) for mat in (3, 4, 2, 1) for piece in range(UNITS_OF[mat])]
+    return [(mat, piece) for mat in (3, 4, 1, 2) for piece in range(UNITS_OF[mat])]
 
 
 def first_unit(mat):
@@ -43,7 +46,7 @@
     return 0.5 * (1.0 + lax.erf(pre_wide * INV_SQRT2)) + pre_wide * INV_SQRT2PI * jnp.exp(-0.5 * pre_wide * pre_wide)
 
 
-def forward_kernel(x_ref, w_one, w_two, z_out, a_out, h_out, x_turned, total):
+def forward_kernel(x_ref, w_one, w_two, z_out, a_turned, h_out, x_turned, total):
     step = pl.program_id(0)
 
     @pl.when(step == 0)
@@ -54,7 +57,7 @@
     z_one = jnp.dot(x_ref[...], w_one[...], preferred_element_type=jnp.float32).astype(jnp.bfloat16)
     z_out[...] = z_one
     a_one = gelu_value(z_one).astype(jnp.bfloat16)
-    a_out[...] = a_one
+    a_turned[...] = a_one.T
     total[...] += jnp.dot(a_one, w_two[...], preferred_element_type=jnp.float32)
 
     @pl.when(step == pl.num_programs(0) - 1)
@@ -70,9 +73,9 @@
     return pl.pallas_call(
         forward_kernel,
         grid=(wide // block,),
-        out_shape=(jax.ShapeDtypeStruct((rows, wide), bf16), jax.ShapeDtypeStruct((rows, wide), bf16), jax.ShapeDtypeStruct((rows, dim), bf16), jax.ShapeDtypeStruct((dim, rows), bf16)),
-        in_specs=[pl.BlockSpec((rows, dim), lambda i: (0, 0)), pl.BlockSpec((dim, block), lambda i: (0, i)), pl.BlockSpec((block, dim), lambda i: (i, 0))],
-        out_specs=(pl.BlockSpec((rows, block), lambda i: (0, i)), pl.BlockSpec((rows, block), lambda i: (0, i)), pl.BlockSpec((rows, dim), lambda i: (0, 0)), pl.BlockSpec((dim, rows), lambda i: (0, 0))),
+        out_shape=(jax.ShapeDtypeStruct((rows, wide), bf16), jax.ShapeDtypeStruct((wide, rows), bf16), jax.ShapeDtypeStruct((rows, dim), bf16), jax.ShapeDtypeStruct((dim, rows), bf16)),
+        in_specs=[pl.BlockSpec((rows, dim), whole_at), pl.BlockSpec((dim, block), across_at), pl.BlockSpec((block, dim), down_at)],
+        out_specs=(pl.BlockSpec((rows, block), across_at), pl.BlockSpec((block, rows), down_at), pl.BlockSpec((rows, dim), whole_at), pl.BlockSpec((dim, rows), whole_at)),
         scratch_shapes=[pltpu.VMEM((rows, dim), jnp.float32)],
         compiler_params=pltpu.CompilerParams(vmem_limit_bytes=VMEM_BYTES),
         name='forward_wide',
@@ -90,11 +93,11 @@
 
     z_three = jnp.dot(h_ref[...], w_three[...], preferred_element_type=f32).astype(bf16)
     a_three = gelu_value(z_three).astype(bf16)
-    da_three = lax.dot_general(dy_ref[...], w_four[...], (((1,), (1,)), ((), ())), preferred_element_type=f32).astype(bf16)
+    da_three = lax.dot_general(dy_ref[...], w_four[...], BY_COLUMNS, preferred_element_type=f32).astype(bf16)
     dz_three = (da_three.astype(f32) * gelu_slope(z_three)).astype(bf16)
-    g_four[...] = lax.dot_general(a_three, dy_ref[...], (((0,), (0,)), ((), ())), preferred_element_type=f32)
+    g_four[...] = lax.dot_general(a_three, dy_ref[...], BY_ROWS, preferred_element_type=f32)
     g_three[...] = jnp.dot(h_turned[...], dz_three, preferred_element_type=f32)
-    total[...] += lax.dot_general(dz_three, w_three[...], (((1,), (1,)), ((), ())), preferred_element_type=f32)
+    total[...] += lax.dot_general(dz_three, w_three[...], BY_COLUMNS, preferred_element_type=f32)
 
     @pl.when(step == pl.num_programs(0) - 1)
     def _():
@@ -106,8 +109,8 @@
     wide = w_three.shape[1]
     block = 512
     f32, bf16 = jnp.float32, jnp.bfloat16
-    whole = pl.BlockSpec((rows, dim), lambda i: (0, 0))
-    across, down = pl.BlockSpec((dim, block), lambda i: (0, i)), pl.BlockSpec((block, dim), lambda i: (i, 0))
+    whole = pl.BlockSpec((rows, dim), whole_at)
+    across, down = pl.BlockSpec((dim, block), across_at), pl.BlockSpec((block, dim), down_at)
     return pl.pallas_call(
         middle_kernel,
         grid=(wide // block,),
@@ -121,10 +124,21 @@
 
 
 def local_grads(x_rows, dy_rows, w_one, w_two, w_three, w_four):
-    z_one, a_one, h_two, x_turned = forward_wide(x_rows, w_one, w_two)
+    z_one, a_turned, h_two, x_turned = forward_wide(x_rows, w_one, w_two)
     g_three, g_four, dh_two = middle(h_two, dy_rows, w_three, w_four)
-    g_two = jnp.einsum('rw,rd->wd', a_one, dh_two, preferred_element_type=jnp.float32)
-    return (x_turned, dh_two, z_one, w_two), g_two, g_three, g_four
+    return x_turned, dh_two, z_one, w_two, a_turned, g_three, g_four
+
+
+def whole_at(step):
+    return 0, 0
+
+
+def across_at(step):
+    return 0, step
+
+
+def down_at(step):
+    return step, 0
 
 
 class Place:
@@ -213,10 +227,14 @@
 
 BLOCK = 256
 BLOCKS_PER_UNIT = 2 * (WIDTH // BLOCK)
-BLOCKS_AFTER = (2, 2, 1)
-
-
-def reduce_kernel(x_turned, dh_two, z_one, w_two, g_two, g_three, g_four, shard, swapped, norm_tile, own, wide_own, part, relay1, final1, relay2, final2, relay3, final3, norm_own, norm_a, norm_b, norm_c, x_buf, dh_buf, z_buf, w_buf, out_buf, load_sem, part_send, part_recv, ring_sems, swap_sems, norm_sems, fetch_sems, out_sems):
+BLOCKS_AFTER = (3, 3, 2)
+TALL_AFTER = (4, 4, 4)
+WIDE_DEEP = 3
+TALL_DEEP = 6
+STORE_DEEP = 3
+
+
+def reduce_kernel(x_turned, dh_two, z_one, w_two, a_turned, g_three, g_four, shard, swapped, norm_tile, g_two, own, part, relay1, final1, relay2, final2, relay3, final3, norm_own, norm_a, norm_b, norm_c, x_buf, dh_buf, z_buf, w_buf, out_buf, a_buf, tall_buf, load_sem, part_send, part_recv, ring_sems, swap_sems, norm_sems, fetch_sems, out_sems, tall_sems):
     place = Place()
     units = unit_list()
     chunks = -(-len(units) // 3)
@@ -239,7 +257,7 @@
         return pl.multiple_of(start, BLOCK)
 
     def fetch(block):
-        slot = lax.rem(block, 2)
+        slot = lax.rem(block, WIDE_DEEP)
         start = block_start(block)
         return (
             pltpu.make_async_copy(z_one.at[:, pl.ds(start, BLOCK)], z_buf.at[slot], fetch_sems.at[0, slot]),
@@ -247,8 +265,26 @@
         )
 
     steady = (pltpu.make_async_copy(x_turned, x_buf, fetch_sems.at[2, 0]), pltpu.make_async_copy(dh_two, dh_buf, fetch_sems.at[2, 1]))
-    for copy in steady + fetch(0):
+    tall_blocks_all = 2 * UNITS_OF[2] * ROWS * SIDE ** 3 // BLOCK
+    tall_chips = BLOCK // (2 * UNITS_OF[2] * ROWS)
+
+    def tall_fetch(block):
+        slot = lax.rem(block, TALL_DEEP)
+        return pltpu.make_async_copy(a_turned.at[pl.ds(pl.multiple_of(block * BLOCK, BLOCK), BLOCK), :], a_buf.at[slot], tall_sems.at[0, slot])
+
+    def tall_store(block):
+        slot = lax.rem(block, STORE_DEEP)
+        chip = block * tall_chips
+        spot_of = (lax.div(chip, SIDE * SIDE), lax.rem(lax.div(chip, SIDE), SIDE), pl.ds(lax.rem(chip, SIDE), tall_chips))
+        return pltpu.make_async_copy(tall_buf.at[slot], g_two.at[spot_of], tall_sems.at[1, slot])
+
+    for copy in steady:
         copy.start()
+    for block in range(WIDE_DEEP - 1):
+        for copy in fetch(block):
+            copy.start()
+    for block in range(TALL_DEEP - 1):
+        tall_fetch(block).start()
     enter(group_x + group_y + group_z)
 
     def source(mat, piece, core):
@@ -258,35 +294,41 @@
         ref = g_two if mat == 2 else g_four
         return ref.at[:, :, :, core, pl.ds(piece * ROWS, ROWS), :]
 
+    def sems_of(level):
+        return [ring_sems.at[level, kind] for kind in range(3)]
+
     rings = []
     for order in range(3):
         a, b = order, (order + 1) % 3
         c = (order + 2) % 3
-        first = RingSum(place, [0, 1, 2], a, relay1, final1, ring_sems.at[0, 0], ring_sems.at[0, 1], ring_sems.at[0, 2])
-        second = RingSum(place, first.rest, b, relay2, final2, ring_sems.at[1, 0], ring_sems.at[1, 1], ring_sems.at[1, 2])
-        third = RingSum(place, second.rest, c, relay3, final3, ring_sems.at[2, 0], ring_sems.at[2, 1], ring_sems.at[2, 2])
+        first = RingSum(place, [0, 1, 2], a, relay1, final1, *sems_of(0))
+        second = RingSum(place, first.rest, b, relay2, final2, *sems_of(1))
+        third = RingSum(place, second.rest, c, relay3, final3, *sems_of(2))
         rings.append((first, second, third))
+
+    def own_slot(unit):
+        return lax.rem(unit + wide_base, wide_units) if not isinstance(unit, int) else (unit + wide_base) % wide_units
 
     def load(chunk):
         for order in range(3):
             unit = 3 * chunk + order
-            if unit >= wide_base:
+            if unit >= len(units) or units[unit][0] == 1:
                 continue
             mat, piece = units[unit]
             send(source(mat, piece, 1 - place.core), part.at[unit], part_send.at[unit], part_recv.at[unit], partner)
-            pltpu.make_async_copy(source(mat, piece, place.core), own.at[order], load_sem.at[unit]).start()
+            pltpu.make_async_copy(source(mat, piece, place.core), own.at[own_slot(unit)], load_sem.at[unit]).start()
 
     def wide_block(block, carry):
-        slot = lax.rem(block, 2)
-
-        @pl.when(block + 1 < blocks)
+        slot = lax.rem(block, WIDE_DEEP)
+
+        @pl.when(block + WIDE_DEEP - 1 < blocks)
         def _():
-            for copy in fetch(block + 1):
+            for copy in fetch(block + WIDE_DEEP - 1):
                 copy.start()
 
         for copy in fetch(block):
             copy.wait()
-        da_one = lax.dot_general(dh_buf[...], w_buf[slot], (((1,), (1,)), ((), ())), preferred_element_type=jnp.float32).astype(jnp.bfloat16)
+        da_one = lax.dot_general(dh_buf[...], w_buf[slot], BY_COLUMNS, preferred_element_type=jnp.float32).astype(jnp.bfloat16)
         dz_one = (da_one.astype(jnp.float32) * gelu_slope(z_buf[slot])).astype(jnp.bfloat16)
         grad = jnp.dot(x_buf[...], dz_one, preferred_element_type=jnp.float32)
         grad = grad.reshape(SIDE, SIDE, SIDE, ROWS, BLOCK)
@@ -294,10 +336,11 @@
         piece = lax.rem(block, pieces)
         mine = lax.rem(lax.div(block, pieces), 2)
         cols = pl.ds(pl.multiple_of(piece * BLOCK, BLOCK), BLOCK)
+        cube_all = (ALL,) * 4
 
         @pl.when(mine == 1)
         def _():
-            wide_own[unit, :, :, :, :, cols] = grad
+            own[(unit,) + cube_all + (cols,)] = grad
 
         @pl.when(mine == 0)
         def _():
@@ -305,20 +348,40 @@
             def _():
                 await_bytes(out_buf.at[piece], out_sems.at[piece])
             out_buf[piece] = grad
-            send(out_buf.at[piece], part.at[wide_base + unit, :, :, :, :, cols], out_sems.at[piece], part_recv.at[wide_base + unit], partner)
+            send(out_buf.at[piece], part.at[(wide_base + unit,) + cube_all + (cols,)], out_sems.at[piece], part_recv.at[wide_base + unit], partner)
+        return carry
+
+    def tall_block(block, carry):
+        slot = lax.rem(block, STORE_DEEP)
+
+        @pl.when(block + TALL_DEEP - 1 < tall_blocks_all)
+        def _():
+            tall_fetch(block + TALL_DEEP - 1).start()
+
+        tall_fetch(block).wait()
+        grad = jnp.dot(a_buf[lax.rem(block, TALL_DEEP)], dh_buf[...], preferred_element_type=jnp.float32)
+
+        @pl.when(block >= STORE_DEEP)
+        def _():
+            tall_store(block - STORE_DEEP).wait()
+        tall_buf[slot] = grad.reshape(tall_buf.shape[1:])
+        tall_store(block).start()
+
+        @pl.when(block == tall_blocks_all - 1)
+        def _():
+            for back in range(STORE_DEEP):
+                tall_store(block - back).wait()
         return carry
 
     def stage_b(order, chunk, unit):
         await_bytes(part.at[unit], part_recv.at[unit])
 
-        @pl.when(unit < wide_base)
+        slot = own_slot(unit)
+
+        @pl.when((unit < wide_base) | (unit >= wide_base + wide_units))
         def _():
-            await_bytes(own.at[order], load_sem.at[unit])
-            part[unit] = part[unit] + own[order]
-
-        @pl.when(unit >= wide_base)
-        def _():
-            part[unit] = part[unit] + wide_own[unit - wide_base]
+            await_bytes(own.at[slot], load_sem.at[unit])
+        part[unit] = part[unit] + own[slot]
         rings[order][0].start(part, (unit,), unit)
 
     def stage_c(order, chunk, unit):
@@ -353,24 +416,34 @@
     def wide_blocks(low, count):
         lax.fori_loop(lax.min(low, blocks), lax.min(low + count, blocks), wide_block, 0)
 
+    def wide_blocks(low, count):
+        lax.fori_loop(lax.min(low, blocks), lax.min(low + count, blocks), wide_block, 0)
+
+    def tall_blocks(low, count):
+        lax.fori_loop(lax.min(low, tall_blocks_all), lax.min(low + count, tall_blocks_all), tall_block, 0)
+
     load(0)
     for copy in steady:
         copy.wait()
-    first_blocks = 6
-    wide_blocks(0, first_blocks)
+    first_wide = 8
+    wide_blocks(0, first_wide)
 
     def turn(now, carry):
         run(now, 0)
         for chunk in range(1, chunks):
-            if 3 * chunk < wide_base:
+            if any(mat != 1 for mat, _ in units[3 * chunk:3 * chunk + 3]):
                 @pl.when(now == chunk)
                 def _(chunk=chunk):
                     load(chunk)
-        done = first_blocks + (now - 1) * sum(BLOCKS_AFTER)
+
+        wide_done = first_wide + (now - 1) * sum(BLOCKS_AFTER)
+        tall_done = (now - 1) * sum(TALL_AFTER)
         for lag in range(1, len(stages)):
             if lag <= len(BLOCKS_AFTER):
-                wide_blocks(done, BLOCKS_AFTER[lag - 1])
-                done = done + BLOCKS_AFTER[lag - 1]
+                wide_blocks(wide_done, BLOCKS_AFTER[lag - 1])
+                tall_blocks(tall_done, TALL_AFTER[lag - 1])
+                wide_done = wide_done + BLOCKS_AFTER[lag - 1]
+                tall_done = tall_done + TALL_AFTER[lag - 1]
             run(now, lag)
         return carry
 
@@ -412,7 +485,7 @@
             for ring in rings[order]:
                 ring.drain(unit)
 
-            @pl.when(unit < wide_base)
+            @pl.when((unit < wide_base) | (unit >= wide_base + wide_units))
             def _():
                 await_bytes(part.at[unit], part_send.at[unit])
             return carry
@@ -420,20 +493,19 @@
         lax.fori_loop(0, counts[order], tidy, 0)
 
 
-def reduce_grads(wide_parts, g_two, g_three, g_four):
+def reduce_grads(x_turned, dh_two, z_one, w_two, a_turned, g_three, g_four):
     n = len(unit_list())
     cube = (SIDE, SIDE, SIDE)
-    args = tuple(wide_parts) + (
-        g_two.reshape(cube + (2, UNITS_OF[2] * ROWS, WIDTH)),
+    args = (
+        x_turned, dh_two, z_one, w_two, a_turned,
         g_three.reshape(cube + (ROWS, 2 * UNITS_OF[3] * WIDTH)),
         g_four.reshape(cube + (2, UNITS_OF[4] * ROWS, WIDTH)),
     )
     f32, bf16 = jnp.float32, jnp.bfloat16
     dma = pltpu.SemaphoreType.DMA
-    dim, rows = wide_parts[0].shape
-    model = wide_parts[1].shape[1]
+    dim, rows = x_turned.shape
+    model = dh_two.shape[1]
     scratch = [
-        pltpu.VMEM((3,) + cube + (ROWS, WIDTH), f32),
         pltpu.VMEM((UNITS_OF[1],) + cube + (ROWS, WIDTH), f32),
         pltpu.VMEM((n,) + cube + (ROWS, WIDTH), f32),
         pltpu.VMEM((n, 2, SIDE, SIDE, ROWS, WIDTH // 2), f32),
@@ -448,10 +520,12 @@
         pltpu.VMEM((SIDE, ROWS, 128), f32),
         pltpu.VMEM((dim, rows), bf16),
         pltpu.VMEM((rows, model), bf16),
-        pltpu.VMEM((2, rows, BLOCK), bf16),
-        pltpu.VMEM((2, BLOCK, model), bf16),
+        pltpu.VMEM((WIDE_DEEP, rows, BLOCK), bf16),
+        pltpu.VMEM((WIDE_DEEP, BLOCK, model), bf16),
         pltpu.VMEM((WIDTH // BLOCK,) + cube + (ROWS, BLOCK), f32),
-        dma((n,)), dma((n,)), dma((n,)), dma((3, 3, n)), dma((2,)), dma((2, 3)), dma((3, 2)), dma((WIDTH // BLOCK,)),
+        pltpu.VMEM((TALL_DEEP, BLOCK, rows), bf16),
+        pltpu.VMEM((STORE_DEEP, BLOCK // (2 * UNITS_OF[2] * ROWS), 2, UNITS_OF[2] * ROWS, WIDTH), f32),
+        dma((n,)), dma((n,)), dma((n,)), dma((3, 3, n)), dma((2,)), dma((2, 3)), dma((3, WIDE_DEEP)), dma((WIDTH // BLOCK,)), dma((2, TALL_DEEP)),
     ]
     any_spec = pl.BlockSpec(memory_space=pl.ANY)
     vmem_spec = pl.BlockSpec(memory_space=pltpu.VMEM)
@@ -461,9 +535,10 @@
             jax.ShapeDtypeStruct((n, ROWS, WIDTH), f32),
             jax.ShapeDtypeStruct((UNITS_OF[3] + UNITS_OF[1], ROWS, WIDTH), f32),
             jax.ShapeDtypeStruct((ROWS, 128), f32),
+            jax.ShapeDtypeStruct(cube + (2, UNITS_OF[2] * ROWS, WIDTH), f32),
         ),
         in_specs=[any_spec] * len(args),
-        out_specs=(vmem_spec,) * 3,
+        out_specs=(vmem_spec,) * 3 + (any_spec,),
         scratch_shapes=scratch,
         compiler_params=pltpu.CompilerParams(collective_id=0, has_side_effects=True, vmem_limit_bytes=VMEM_BYTES),
         name='reduce_grads',
@@ -519,6 +594,7 @@
         out_shape=out_shape,
         in_specs=[vmem_spec] * len(args),
         out_specs=[vmem_spec] * len(out_shape),
+        compiler_params=pltpu.CompilerParams(vmem_limit_bytes=ADAM_VMEM),
         name='adam_update',
     )(*args)
 
@@ -591,7 +667,7 @@
     rings = []
     for order in range(3):
         axes = (order + 2) % 3, (order + 1) % 3, order
-        rings.append([RingSpread(place, axis, axes[:level], board, ring_sems.at[level, 0], ring_sems.at[level, 1], ring_sems.at[level, 2]) for level, axis in enumerate(axes)])
+        rings.append([RingSpread(place, axis, axes[:level], board, *[ring_sems.at[level, kind] for kind in range(3)]) for level, axis in enumerate(axes)])
 
     def begin(order, unit, level):
         if level:
@@ -699,7 +775,7 @@
 
 
 def sync_and_update(grads, masters, moms, variances, learn_rate, clip_max):
-    shard, swapped, norm_tile = reduce_grads(*grads)
+    shard, swapped, norm_tile, _ = reduce_grads(*grads)
     results = adam_update(learn_rate, clip_max, norm_tile, shard, swapped, masters, moms, variances)
     new_masters, new_moms, new_vars = results[0:4], results[4:8], results[8:12]
     two_rows, four_rows, grad_norm = results[12:15]

time: 256 us -> 269 us (1.051)
  Pallas kernels: 234 us -> 261 us
  matrix products: 16 us -> 0 us
    pallas_call x1, Pallas kernels: 118 us -> 146 us  [reduce_grads(): pl.pallas_call(reduce_kernel, out_shape=(jax.ShapeDtypeStruct((n, ROWS, W...]
    dot_general x1 -> x0, matrix products: 16 us -> none  [local_grads(): jnp.einsum('rw,rd->wd', a_one, dh_two, preferred_element_type=jnp.float32)]
where the time goes in v4:
time: 269 us; the launch traced here: 268 us
  Pallas kernels  261 us (97%)
  local copies, waits for them, and re-layouts  4.3 us (2%)
    pallas_call x1, Pallas kernels, reduce_grads(): pl.pallas_call(reduce_kernel, out_shape=(jax.ShapeDtypeStruct((n, ROWS, W...  146 us
    pallas_call x1, Pallas kernels, gather_rows(): pl.pallas_call(gather_kernel, out_shape=(full, full), in_specs=[pl.BlockS...  57.3 us
    pallas_call x1, Pallas kernels, forward_wide(): pl.pallas_call(forward_kernel, grid=(wide // block,), out_shape=(jax.Shap...  31.4 us
    pallas_call x1, Pallas kernels, middle(): pl.pallas_call(middle_kernel, grid=(wide // block,), out_shape=(jax.Shape...  17.9 us
    pallas_call x1, Pallas kernels, place_weights(): pl.pallas_call(place_kernel, out_shape=(jax.ShapeDtypeStruct(cube + (ROWS...  7.42 us

profile of v4, /device:TPU:1, one launch (start us, length us, event | category | flops | bytes accessed | tf_op | source)
XLA Modules:
  0.0 267.6 jit_solution(15696980696913867221)
XLA Ops:
  0.7 31.4 %forward_wide.1 = (bf16[1024,8192]{1,0:T(8,128)(2,1)}, bf16[8192,1024]{1,0:T(8,128)(2,1)}, bf16[1024,512]{1,0:T(8,128)(2,1)}, bf16[512,1024]{1,0:T(8,128)(2,1)}) custom-call(bf16[1024,512]{1,0:T(8,128)(2,1)} %x_ref.1, bf16[512,8192]{1,0:T(8,128)(2,1)} %w_one.1, bf16[8192,512]{1,0:T(8,128)(2,1)} %w_two.3), custom_call_target="tpu_custom_call" | custom-call | tf_op jit(solution)/shard_map/forward_wide/pallas_call | solution.py:73
  32.1 17.9 %middle.1 = (f32[512,2048]{1,0:T(8,128)}, f32[2048,512]{1,0:T(8,128)}, bf16[1024,512]{1,0:T(8,128)(2,1)}) custom-call(bf16[1024,512]{1,0:T(8,128)(2,1)} %get-tuple-element.49.h_ref, bf16[1024,512]{1,0:T(8,128)(2,1)} %dy_ref.1, bf16[512,2048]{1,0:T(8,128)(2,1)} %w_three.1, bf16[2048,512]{1,0:T(8,128)(2,1)} %w_four.1), custom_call_target="tpu_custom_call" | custom-call | tf_op jit(solution)/shard_map/middle/pallas_call | solution.py:114
  50.0 0.0 copy-start.2
  50.0 0.0 copy-start.3
  50.0 0.0 copy-start.4
  50.0 0.0 copy-start.5
  50.1 0.0 copy-start.6
  50.1 0.0 copy-start.7
  50.1 0.0 copy-start.9
  50.1 0.0 copy-start.10
  50.1 0.0 copy-start.11
  50.1 0.0 copy-start.12
  50.1 0.0 copy-start.13
  50.1 0.0 copy-start.14
  50.2 145.8 %reduce_grads.1 = (f32[20,8,512]{2,1,0:T(8,128)}, f32[10,8,512]{2,1,0:T(8,128)}, f32[8,128]{1,0:T(8,128)}, f32[4,4,4,2,64,512]{5,4,3,2,1,0:T(8,128)}) custom-call(bf16[512,1024]{1,0:T(8,128)(2,1)} %get-tuple-element.48.x_turned, bf16[1024,512]{1,0:T(8,128)(2,1)} %get-tuple-element.50.dh_two, bf16[1024,8192]{1,0:T(8,128)(2,1)} %get-tuple-element.51.z_one, ...), custom_call_target="tpu_custom_call" | custom-call | tf_op jit(solution)/shard_map/reduce_grads/pallas_call | solution.py:532
  197.4 1.0 copy-done
  198.4 0.9 copy-done.1
  199.3 0.7 copy-done.16
  200.0 1.2 adam_update.1
  201.2 0.0 copy-start.8
  201.2 0.9 copy-done.8
  202.1 0.8 copy-done.15
  202.9 57.3 %gather_rows.1 = (bf16[20,4,4,4,8,512]{5,4,3,2,1,0:T(8,128)(2,1)S(1)}, bf16[20,4,4,4,8,512]{5,4,3,2,1,0:T(8,128)(2,1)S(1)}) custom-call(f32[4,8192]{1,0:T(4,128)S(1)} %copy-done.8, f32[4,2048]{1,0:T(4,128)S(1)} %copy-done.15, bf16[8,8,512]{2,1,0:T(8,128)(2,1)S(1)} %get-tuple-element.60.two_rows, bf16[2,8,512]{2,1,0:T(8,128)(2,1)S(1)} %get-tuple-element.61.four_rows), custom_call_target="tpu_custom_call" | custom-call | tf_op jit(solution)/shard_map/gather_rows/pallas_call | solution.py:713
  260.1 7.4 %place_weights.1 = (bf16[4,4,4,8,8192]{4,3,2,1,0:T(8,128)(2,1)}, bf16[4,4,4,2,64,512]{5,4,3,2,1,0:T(8,128)(2,1)}, bf16[4,4,4,8,2048]{4,3,2,1,0:T(8,128)(2,1)}, bf16[4,4,4,2,16,512]{5,4,3,2,1,0:T(8,128)(2,1)}) custom-call(bf16[20,4,4,4,8,512]{5,4,3,2,1,0:T(8,128)(2,1)S(1)} %get-tuple-element.62.board, bf16[20,4,4,4,8,512]{5,4,3,2,1,0:T(8,128)(2,1)S(1)} %get-tuple-element.63.other), custom_call_target="tpu_custom_call" | custom-call | tf_op jit(solution)/shard_map/place_weights/pallas_call | solution.py:754
  (16 shorter events, 0.0 us)
Async XLA Ops:
  50.0 147.3 %copy-start.2 = (f32[4,8192]{1,0:T(4,128)S(1)}, f32[4,8192]{1,0:T(4,128)}, u32[]{:S(2)}) copy-start(f32[4,8192]{1,0:T(4,128)} %refs_0_.1) | copy-start | bytes 393220
  50.0 147.3 %copy-start.3 = (f32[64,512]{1,0:T(8,128)S(1)}, f32[64,512]{1,0:T(8,128)}, u32[]{:S(2)}) copy-start(f32[64,512]{1,0:T(8,128)} %refs_1_.1) | copy-start | bytes 393220
  50.0 147.3 %copy-start.4 = (f32[4,8192]{1,0:T(4,128)S(1)}, f32[4,8192]{1,0:T(4,128)}, u32[]{:S(2)}) copy-start(f32[4,8192]{1,0:T(4,128)} %refs_4_.1) | copy-start | bytes 393220
  50.0 147.3 %copy-start.5 = (f32[64,512]{1,0:T(8,128)S(1)}, f32[64,512]{1,0:T(8,128)}, u32[]{:S(2)}) copy-start(f32[64,512]{1,0:T(8,128)} %refs_5_.1) | copy-start | bytes 393220
  50.1 147.3 %copy-start.6 = (f32[4,8192]{1,0:T(4,128)S(1)}, f32[4,8192]{1,0:T(4,128)}, u32[]{:S(2)}) copy-start(f32[4,8192]{1,0:T(4,128)} %refs_8_.1) | copy-start | bytes 393220
  50.1 147.3 %copy-start.7 = (f32[64,512]{1,0:T(8,128)S(1)}, f32[64,512]{1,0:T(8,128)}, u32[]{:S(2)}) copy-start(f32[64,512]{1,0:T(8,128)} %refs_9_.1) | copy-start | bytes 393220
  50.1 147.3 %copy-start.9 = (f32[4,2048]{1,0:T(4,128)S(1)}, f32[4,2048]{1,0:T(4,128)}, u32[]{:S(2)}) copy-start(f32[4,2048]{1,0:T(4,128)} %refs_2_.1) | copy-start | bytes 98308
  50.1 147.3 %copy-start.10 = (f32[16,512]{1,0:T(8,128)S(1)}, f32[16,512]{1,0:T(8,128)}, u32[]{:S(2)}) copy-start(f32[16,512]{1,0:T(8,128)} %refs_3_.1) | copy-start | bytes 98308
  50.1 147.3 %copy-start.11 = (f32[4,2048]{1,0:T(4,128)S(1)}, f32[4,2048]{1,0:T(4,128)}, u32[]{:S(2)}) copy-start(f32[4,2048]{1,0:T(4,128)} %refs_6_.1) | copy-start | bytes 98308
  50.1 147.3 %copy-start.12 = (f32[16,512]{1,0:T(8,128)S(1)}, f32[16,512]{1,0:T(8,128)}, u32[]{:S(2)}) copy-start(f32[16,512]{1,0:T(8,128)} %refs_7_.1) | copy-start | bytes 98308
  50.1 147.3 %copy-start.13 = (f32[4,2048]{1,0:T(4,128)S(1)}, f32[4,2048]{1,0:T(4,128)}, u32[]{:S(2)}) copy-start(f32[4,2048]{1,0:T(4,128)} %refs_10_.1) | copy-start | bytes 98308
  50.1 147.3 %copy-start.14 = (f32[16,512]{1,0:T(8,128)S(1)}, f32[16,512]{1,0:T(8,128)}, u32[]{:S(2)}) copy-start(f32[16,512]{1,0:T(8,128)} %refs_11_.1) | copy-start | bytes 98308
  197.4 1.0 copy-start
  198.4 0.9 copy-start.1
  199.3 0.7 copy-start.16
  201.2 0.9 copy-start.8
  202.1 0.8 copy-start.15

commit v5 on v3

--- a/solution.py
+++ b/solution.py
@@ -22,7 +22,11 @@
 ROWS = 8
 UNITS_OF = {3: 2, 4: 2, 2: 8, 1: 8}
 MESH_ID = pl.DeviceIdType.MESH
+BY_COLUMNS = (((1,), (1,)), ((), ()))
+BY_ROWS = (((0,), (0,)), ((), ()))
 VMEM_BYTES = 62 * 1024 * 1024
+ADAM_VMEM = 8 * 1024 * 1024
+WIDE_DEEP = 4
 
 
 def unit_list():
@@ -43,7 +47,7 @@
     return 0.5 * (1.0 + lax.erf(pre_wide * INV_SQRT2)) + pre_wide * INV_SQRT2PI * jnp.exp(-0.5 * pre_wide * pre_wide)
 
 
-def forward_kernel(x_ref, w_one, w_two, z_out, a_out, h_out, x_turned, total):
+def forward_kernel(x_ref, w_one, w_two, z_out, a_turned, h_out, x_turned, total):
     step = pl.program_id(0)
 
     @pl.when(step == 0)
@@ -54,7 +58,7 @@
     z_one = jnp.dot(x_ref[...], w_one[...], preferred_element_type=jnp.float32).astype(jnp.bfloat16)
     z_out[...] = z_one
     a_one = gelu_value(z_one).astype(jnp.bfloat16)
-    a_out[...] = a_one
+    a_turned[...] = a_one.T
     total[...] += jnp.dot(a_one, w_two[...], preferred_element_type=jnp.float32)
 
     @pl.when(step == pl.num_programs(0) - 1)
@@ -65,14 +69,14 @@
 def forward_wide(x_rows, w_one, w_two):
     rows, dim = x_rows.shape
     wide = w_one.shape[1]
-    block = 512
+    block = 1024
     bf16 = jnp.bfloat16
     return pl.pallas_call(
         forward_kernel,
         grid=(wide // block,),
-        out_shape=(jax.ShapeDtypeStruct((rows, wide), bf16), jax.ShapeDtypeStruct((rows, wide), bf16), jax.ShapeDtypeStruct((rows, dim), bf16), jax.ShapeDtypeStruct((dim, rows), bf16)),
-        in_specs=[pl.BlockSpec((rows, dim), lambda i: (0, 0)), pl.BlockSpec((dim, block), lambda i: (0, i)), pl.BlockSpec((block, dim), lambda i: (i, 0))],
-        out_specs=(pl.BlockSpec((rows, block), lambda i: (0, i)), pl.BlockSpec((rows, block), lambda i: (0, i)), pl.BlockSpec((rows, dim), lambda i: (0, 0)), pl.BlockSpec((dim, rows), lambda i: (0, 0))),
+        out_shape=(jax.ShapeDtypeStruct((rows, wide), bf16), jax.ShapeDtypeStruct((wide, rows), bf16), jax.ShapeDtypeStruct((rows, dim), bf16), jax.ShapeDtypeStruct((dim, rows), bf16)),
+        in_specs=[pl.BlockSpec((rows, dim), whole_at), pl.BlockSpec((dim, block), across_at), pl.BlockSpec((block, dim), down_at)],
+        out_specs=(pl.BlockSpec((rows, block), across_at), pl.BlockSpec((block, rows), down_at), pl.BlockSpec((rows, dim), whole_at), pl.BlockSpec((dim, rows), whole_at)),
         scratch_shapes=[pltpu.VMEM((rows, dim), jnp.float32)],
         compiler_params=pltpu.CompilerParams(vmem_limit_bytes=VMEM_BYTES),
         name='forward_wide',
@@ -90,11 +94,11 @@
 
     z_three = jnp.dot(h_ref[...], w_three[...], preferred_element_type=f32).astype(bf16)
     a_three = gelu_value(z_three).astype(bf16)
-    da_three = lax.dot_general(dy_ref[...], w_four[...], (((1,), (1,)), ((), ())), preferred_element_type=f32).astype(bf16)
+    da_three = lax.dot_general(dy_ref[...], w_four[...], BY_COLUMNS, preferred_element_type=f32).astype(bf16)
     dz_three = (da_three.astype(f32) * gelu_slope(z_three)).astype(bf16)
-    g_four[...] = lax.dot_general(a_three, dy_ref[...], (((0,), (0,)), ((), ())), preferred_element_type=f32)
+    g_four[...] = lax.dot_general(a_three, dy_ref[...], BY_ROWS, preferred_element_type=f32)
     g_three[...] = jnp.dot(h_turned[...], dz_three, preferred_element_type=f32)
-    total[...] += lax.dot_general(dz_three, w_three[...], (((1,), (1,)), ((), ())), preferred_element_type=f32)
+    total[...] += lax.dot_general(dz_three, w_three[...], BY_COLUMNS, preferred_element_type=f32)
 
     @pl.when(step == pl.num_programs(0) - 1)
     def _():
@@ -106,8 +110,8 @@
     wide = w_three.shape[1]
     block = 512
     f32, bf16 = jnp.float32, jnp.bfloat16
-    whole = pl.BlockSpec((rows, dim), lambda i: (0, 0))
-    across, down = pl.BlockSpec((dim, block), lambda i: (0, i)), pl.BlockSpec((block, dim), lambda i: (i, 0))
+    whole = pl.BlockSpec((rows, dim), whole_at)
+    across, down = pl.BlockSpec((dim, block), across_at), pl.BlockSpec((block, dim), down_at)
     return pl.pallas_call(
         middle_kernel,
         grid=(wide // block,),
@@ -121,10 +125,22 @@
 
 
 def local_grads(x_rows, dy_rows, w_one, w_two, w_three, w_four):
-    z_one, a_one, h_two, x_turned = forward_wide(x_rows, w_one, w_two)
+    z_one, a_turned, h_two, x_turned = forward_wide(x_rows, w_one, w_two)
     g_three, g_four, dh_two = middle(h_two, dy_rows, w_three, w_four)
-    g_two = jnp.einsum('rw,rd->wd', a_one, dh_two, preferred_element_type=jnp.float32)
+    g_two = jnp.dot(a_turned, dh_two, preferred_element_type=jnp.float32)
     return (x_turned, dh_two, z_one, w_two), g_two, g_three, g_four
+
+
+def whole_at(step):
+    return 0, 0
+
+
+def across_at(step):
+    return 0, step
+
+
+def down_at(step):
+    return step, 0
 
 
 class Place:
@@ -239,7 +255,7 @@
         return pl.multiple_of(start, BLOCK)
 
     def fetch(block):
-        slot = lax.rem(block, 2)
+        slot = lax.rem(block, WIDE_DEEP)
         start = block_start(block)
         return (
             pltpu.make_async_copy(z_one.at[:, pl.ds(start, BLOCK)], z_buf.at[slot], fetch_sems.at[0, slot]),
@@ -247,8 +263,11 @@
         )
 
     steady = (pltpu.make_async_copy(x_turned, x_buf, fetch_sems.at[2, 0]), pltpu.make_async_copy(dh_two, dh_buf, fetch_sems.at[2, 1]))
-    for copy in steady + fetch(0):
+    for copy in steady:
         copy.start()
+    for block in range(WIDE_DEEP - 1):
+        for copy in fetch(block):
+            copy.start()
     enter(group_x + group_y + group_z)
 
     def source(mat, piece, core):
@@ -258,13 +277,16 @@
         ref = g_two if mat == 2 else g_four
         return ref.at[:, :, :, core, pl.ds(piece * ROWS, ROWS), :]
 
+    def sems_of(level):
+        return [ring_sems.at[level, kind] for kind in range(3)]
+
     rings = []
     for order in range(3):
         a, b = order, (order + 1) % 3
         c = (order + 2) % 3
-        first = RingSum(place, [0, 1, 2], a, relay1, final1, ring_sems.at[0, 0], ring_sems.at[0, 1], ring_sems.at[0, 2])
-        second = RingSum(place, first.rest, b, relay2, final2, ring_sems.at[1, 0], ring_sems.at[1, 1], ring_sems.at[1, 2])
-        third = RingSum(place, second.rest, c, relay3, final3, ring_sems.at[2, 0], ring_sems.at[2, 1], ring_sems.at[2, 2])
+        first = RingSum(place, [0, 1, 2], a, relay1, final1, *sems_of(0))
+        second = RingSum(place, first.rest, b, relay2, final2, *sems_of(1))
+        third = RingSum(place, second.rest, c, relay3, final3, *sems_of(2))
         rings.append((first, second, third))
 
     def load(chunk):
@@ -277,16 +299,16 @@
             pltpu.make_async_copy(source(mat, piece, place.core), own.at[order], load_sem.at[unit]).start()
 
     def wide_block(block, carry):
-        slot = lax.rem(block, 2)
-
-        @pl.when(block + 1 < blocks)
+        slot = lax.rem(block, WIDE_DEEP)
+
+        @pl.when(block + WIDE_DEEP - 1 < blocks)
         def _():
-            for copy in fetch(block + 1):
+            for copy in fetch(block + WIDE_DEEP - 1):
                 copy.start()
 
         for copy in fetch(block):
             copy.wait()
-        da_one = lax.dot_general(dh_buf[...], w_buf[slot], (((1,), (1,)), ((), ())), preferred_element_type=jnp.float32).astype(jnp.bfloat16)
+        da_one = lax.dot_general(dh_buf[...], w_buf[slot], BY_COLUMNS, preferred_element_type=jnp.float32).astype(jnp.bfloat16)
         dz_one = (da_one.astype(jnp.float32) * gelu_slope(z_buf[slot])).astype(jnp.bfloat16)
         grad = jnp.dot(x_buf[...], dz_one, preferred_element_type=jnp.float32)
         grad = grad.reshape(SIDE, SIDE, SIDE, ROWS, BLOCK)
@@ -448,10 +470,10 @@
         pltpu.VMEM((SIDE, ROWS, 128), f32),
         pltpu.VMEM((dim, rows), bf16),
         pltpu.VMEM((rows, model), bf16),
-        pltpu.VMEM((2, rows, BLOCK), bf16),
-        pltpu.VMEM((2, BLOCK, model), bf16),
+        pltpu.VMEM((WIDE_DEEP, rows, BLOCK), bf16),
+        pltpu.VMEM((WIDE_DEEP, BLOCK, model), bf16),
         pltpu.VMEM((WIDTH // BLOCK,) + cube + (ROWS, BLOCK), f32),
-        dma((n,)), dma((n,)), dma((n,)), dma((3, 3, n)), dma((2,)), dma((2, 3)), dma((3, 2)), dma((WIDTH // BLOCK,)),
+        dma((n,)), dma((n,)), dma((n,)), dma((3, 3, n)), dma((2,)), dma((2, 3)), dma((3, WIDE_DEEP)), dma((WIDTH // BLOCK,)),
     ]
     any_spec = pl.BlockSpec(memory_space=pl.ANY)
     vmem_spec = pl.BlockSpec(memory_space=pltpu.VMEM)
@@ -519,6 +541,7 @@
         out_shape=out_shape,
         in_specs=[vmem_spec] * len(args),
         out_specs=[vmem_spec] * len(out_shape),
+        compiler_params=pltpu.CompilerParams(vmem_limit_bytes=ADAM_VMEM),
         name='adam_update',
     )(*args)
 
@@ -591,7 +614,7 @@
     rings = []
     for order in range(3):
         axes = (order + 2) % 3, (order + 1) % 3, order
-        rings.append([RingSpread(place, axis, axes[:level], board, ring_sems.at[level, 0], ring_sems.at[level, 1], ring_sems.at[level, 2]) for level, axis in enumerate(axes)])
+        rings.append([RingSpread(place, axis, axes[:level], board, *[ring_sems.at[level, kind] for kind in range(3)]) for level, axis in enumerate(axes)])
 
     def begin(order, unit, level):
         if level:

time: 256 us -> 252 us (0.984)
  Pallas kernels: 234 us -> 229 us
where the time goes in v5:
time: 252 us
  Pallas kernels  229 us (91%)
  matrix products  15.9 us (6%)
  local copies, waits for them, and re-layouts  4.29 us (2%)
    pallas_call x1, Pallas kernels, reduce_grads(): pl.pallas_call(reduce_kernel, out_shape=(jax.ShapeDtypeStruct((n, ROWS, W...  117 us
    pallas_call x1, Pallas kernels, gather_rows(): pl.pallas_call(gather_kernel, out_shape=(full, full), in_specs=[pl.BlockS...  57.2 us
    pallas_call x1, Pallas kernels, forward_wide(): pl.pallas_call(forward_kernel, grid=(wide // block,), out_shape=(jax.Shap...  28.2 us
    pallas_call x1, Pallas kernels, middle(): pl.pallas_call(middle_kernel, grid=(wide // block,), out_shape=(jax.Shape...  17.9 us
    dot_general x1, matrix products, local_grads(): g_two = jnp.dot(a_turned, dh_two, preferred_element_type=jnp.float32)  15.9 us
    pallas_call x1, Pallas kernels, place_weights(): pl.pallas_call(place_kernel, out_shape=(jax.ShapeDtypeStruct(cube + (ROWS...  7.42 us

profile of v5, /device:TPU:1, one launch (start us, length us, event | category | flops | bytes accessed | tf_op | source)
XLA Modules:
  0.0 251.6 jit_solution(8743684397118318446)
XLA Ops:
  0.7 28.2 %forward_wide.1 = (bf16[1024,8192]{1,0:T(8,128)(2,1)}, bf16[8192,1024]{1,0:T(8,128)(2,1)}, bf16[1024,512]{1,0:T(8,128)(2,1)}, bf16[512,1024]{1,0:T(8,128)(2,1)}) custom-call(bf16[1024,512]{1,0:T(8,128)(2,1)} %x_ref.1, bf16[512,8192]{1,0:T(8,128)(2,1)} %w_one.1, bf16[8192,512]{1,0:T(8,128)(2,1)} %w_two.3), custom_call_target="tpu_custom_call" | custom-call | tf_op jit(solution)/shard_map/forward_wide/pallas_call | solution.py:74
  28.9 17.9 %middle.1 = (f32[512,2048]{1,0:T(8,128)}, f32[2048,512]{1,0:T(8,128)}, bf16[1024,512]{1,0:T(8,128)(2,1)}) custom-call(bf16[1024,512]{1,0:T(8,128)(2,1)} %get-tuple-element.49.h_ref, bf16[1024,512]{1,0:T(8,128)(2,1)} %dy_ref.1, bf16[512,2048]{1,0:T(8,128)(2,1)} %w_three.1, bf16[2048,512]{1,0:T(8,128)(2,1)} %w_four.1), custom_call_target="tpu_custom_call" | custom-call | tf_op jit(solution)/shard_map/middle/pallas_call | solution.py:115
  46.8 15.9 %fusion = f32[8192,512]{1,0:T(8,128)} fusion(bf16[8192,1024]{1,0:T(8,128)(2,1)} %get-tuple-element.52, bf16[1024,512]{1,0:T(8,128)(2,1)} %get-tuple-element.50.dh_two), kind=kOutput, calls=%fused_computation | convolution fusion | flops 8589934592 | bytes 34603008 | tf_op jit(solution)/shard_map/dot_general | solution.py:130
  62.8 0.0 copy-start.5
  62.8 0.0 copy-start.6
  62.8 0.0 copy-start.7
  62.8 0.0 copy-start.9
  62.8 0.0 copy-start.10
  62.8 0.0 copy-start.11
  62.8 0.0 copy-start.12
  62.8 0.0 copy-start.13
  62.8 0.0 copy-start.14
  62.9 117.1 %reduce_grads.1 = (f32[20,8,512]{2,1,0:T(8,128)}, f32[10,8,512]{2,1,0:T(8,128)}, f32[8,128]{1,0:T(8,128)}) custom-call(bf16[512,1024]{1,0:T(8,128)(2,1)} %get-tuple-element.48.x_turned, bf16[1024,512]{1,0:T(8,128)(2,1)} %get-tuple-element.50.dh_two, bf16[1024,8192]{1,0:T(8,128)(2,1)} %get-tuple-element.51.z_one, bf16[8192,512]{1,0:T(8,128)(2,1)} %w_two.3, ...), custom_call_target="tpu_custom_call" | custom-call | tf_op jit(solution)/shard_map/reduce_grads/pallas_call | solution.py:480
  181.2 0.0 copy-done.2
  181.3 0.0 copy-done.3
  181.4 1.0 copy-done
  182.3 0.9 copy-done.1
  183.3 0.7 copy-done.16
  183.9 1.2 adam_update.1
  185.2 0.0 copy-start.8
  185.2 0.9 copy-done.8
  186.1 0.8 copy-done.15
  186.8 57.2 %gather_rows.1 = (bf16[20,4,4,4,8,512]{5,4,3,2,1,0:T(8,128)(2,1)S(1)}, bf16[20,4,4,4,8,512]{5,4,3,2,1,0:T(8,128)(2,1)S(1)}) custom-call(f32[4,8192]{1,0:T(4,128)S(1)} %copy-done.8, f32[4,2048]{1,0:T(4,128)S(1)} %copy-done.15, bf16[8,8,512]{2,1,0:T(8,128)(2,1)S(1)} %get-tuple-element.60.two_rows, bf16[2,8,512]{2,1,0:T(8,128)(2,1)S(1)} %get-tuple-element.61.four_rows), custom_call_target="tpu_custom_call" | custom-call | tf_op jit(solution)/shard_map/gather_rows/pallas_call | solution.py:660
  244.0 7.4 %place_weights.1 = (bf16[4,4,4,8,8192]{4,3,2,1,0:T(8,128)(2,1)}, bf16[4,4,4,2,64,512]{5,4,3,2,1,0:T(8,128)(2,1)}, bf16[4,4,4,8,2048]{4,3,2,1,0:T(8,128)(2,1)}, bf16[4,4,4,2,16,512]{5,4,3,2,1,0:T(8,128)(2,1)}) custom-call(bf16[20,4,4,4,8,512]{5,4,3,2,1,0:T(8,128)(2,1)S(1)} %get-tuple-element.62.board, bf16[20,4,4,4,8,512]{5,4,3,2,1,0:T(8,128)(2,1)S(1)} %get-tuple-element.63.other), custom_call_target="tpu_custom_call" | custom-call | tf_op jit(solution)/shard_map/place_weights/pallas_call | solution.py:701
  (17 shorter events, 0.0 us)
Async XLA Ops:
  62.7 118.5 %copy-start.2 = (f32[4,8192]{1,0:T(4,128)S(1)}, f32[4,8192]{1,0:T(4,128)}, u32[]{:S(2)}) copy-start(f32[4,8192]{1,0:T(4,128)} %refs_0_.1) | copy-start | bytes 393220
  62.7 118.5 %copy-start.3 = (f32[64,512]{1,0:T(8,128)S(1)}, f32[64,512]{1,0:T(8,128)}, u32[]{:S(2)}) copy-start(f32[64,512]{1,0:T(8,128)} %refs_1_.1) | copy-start | bytes 393220
  62.7 118.5 %copy-start.4 = (f32[4,8192]{1,0:T(4,128)S(1)}, f32[4,8192]{1,0:T(4,128)}, u32[]{:S(2)}) copy-start(f32[4,8192]{1,0:T(4,128)} %refs_4_.1) | copy-start | bytes 393220
  62.8 118.5 %copy-start.5 = (f32[64,512]{1,0:T(8,128)S(1)}, f32[64,512]{1,0:T(8,128)}, u32[]{:S(2)}) copy-start(f32[64,512]{1,0:T(8,128)} %refs_5_.1) | copy-start | bytes 393220
  62.8 118.5 %copy-start.6 = (f32[4,8192]{1,0:T(4,128)S(1)}, f32[4,8192]{1,0:T(4,128)}, u32[]{:S(2)}) copy-start(f32[4,8192]{1,0:T(4,128)} %refs_8_.1) | copy-start | bytes 393220
  62.8 118.5 %copy-start.7 = (f32[64,512]{1,0:T(8,128)S(1)}, f32[64,512]{1,0:T(8,128)}, u32[]{:S(2)}) copy-start(f32[64,512]{1,0:T(8,128)} %refs_9_.1) | copy-start | bytes 393220
  62.8 118.5 %copy-start.9 = (f32[4,2048]{1,0:T(4,128)S(1)}, f32[4,2048]{1,0:T(4,128)}, u32[]{:S(2)}) copy-start(f32[4,2048]{1,0:T(4,128)} %refs_2_.1) | copy-start | bytes 98308
  62.8 118.5 %copy-start.10 = (f32[16,512]{1,0:T(8,128)S(1)}, f32[16,512]{1,0:T(8,128)}, u32[]{:S(2)}) copy-start(f32[16,512]{1,0:T(8,128)} %refs_3_.1) | copy-start | bytes 98308
  62.8 118.5 %copy-start.11 = (f32[4,2048]{1,0:T(4,128)S(1)}, f32[4,2048]{1,0:T(4,128)}, u32[]{:S(2)}) copy-start(f32[4,2048]{1,0:T(4,128)} %refs_6_.1) | copy-start | bytes 98308
  62.8 118.5 %copy-start.12 = (f32[16,512]{1,0:T(8,128)S(1)}, f32[16,512]{1,0:T(8,128)}, u32[]{:S(2)}) copy-start(f32[16,512]{1,0:T(8,128)} %refs_7_.1) | copy-start | bytes 98308
  62.8 118.5 %copy-start.13 = (f32[4,2048]{1,0:T(4,128)S(1)}, f32[4,2048]{1,0:T(4,128)}, u32[]{:S(2)}) copy-start(f32[4,2048]{1,0:T(4,128)} %refs_10_.1) | copy-start | bytes 98308
  62.8 118.5 %copy-start.14 = (f32[16,512]{1,0:T(8,128)S(1)}, f32[16,512]{1,0:T(8,128)}, u32[]{:S(2)}) copy-start(f32[16,512]{1,0:T(8,128)} %refs_11_.1) | copy-start | bytes 98308
  181.4 1.0 copy-start
  182.3 0.9 copy-start.1
  183.3 0.7 copy-start.16
  185.2 0.9 copy-start.8
  186.1 0.8 copy-start.15

commit v6 on v5

--- a/solution.py
+++ b/solution.py
@@ -30,7 +30,7 @@
 
 
 def unit_list():
-    return [(mat, piece) for mat in (3, 4, 2, 1) for piece in range(UNITS_OF[mat])]
+    return [(mat, piece) for mat in (4, 2, 3, 1) for piece in range(UNITS_OF[mat])]
 
 
 def first_unit(mat):
@@ -83,7 +83,11 @@
     )(x_rows, w_one, w_two)
 
 
-def middle_kernel(h_ref, dy_ref, w_three, w_four, g_three, g_four, dh_out, total, h_turned):
+NARROW_STEPS = 4
+TALL_STEPS = 8
+
+
+def middle_kernel(h_ref, dy_ref, w_three, w_four, a_turned, g_three, g_four, g_two, dh_out, total, h_turned):
     step = pl.program_id(0)
     f32, bf16 = jnp.float32, jnp.bfloat16
 
@@ -92,42 +96,59 @@
         total[...] = jnp.zeros_like(total)
         h_turned[...] = h_ref[...].T
 
-    z_three = jnp.dot(h_ref[...], w_three[...], preferred_element_type=f32).astype(bf16)
-    a_three = gelu_value(z_three).astype(bf16)
-    da_three = lax.dot_general(dy_ref[...], w_four[...], BY_COLUMNS, preferred_element_type=f32).astype(bf16)
-    dz_three = (da_three.astype(f32) * gelu_slope(z_three)).astype(bf16)
-    g_four[...] = lax.dot_general(a_three, dy_ref[...], BY_ROWS, preferred_element_type=f32)
-    g_three[...] = jnp.dot(h_turned[...], dz_three, preferred_element_type=f32)
-    total[...] += lax.dot_general(dz_three, w_three[...], BY_COLUMNS, preferred_element_type=f32)
-
-    @pl.when(step == pl.num_programs(0) - 1)
+    @pl.when(step < NARROW_STEPS)
+    def _():
+        z_three = jnp.dot(h_ref[...], w_three[...], preferred_element_type=f32).astype(bf16)
+        a_three = gelu_value(z_three).astype(bf16)
+        da_three = lax.dot_general(dy_ref[...], w_four[...], BY_COLUMNS, preferred_element_type=f32).astype(bf16)
+        dz_three = (da_three.astype(f32) * gelu_slope(z_three)).astype(bf16)
+        g_four[...] = lax.dot_general(a_three, dy_ref[...], BY_ROWS, preferred_element_type=f32)
+        g_three[...] = jnp.dot(h_turned[...], dz_three, preferred_element_type=f32)
+        total[...] += lax.dot_general(dz_three, w_three[...], BY_COLUMNS, preferred_element_type=f32)
+
+    @pl.when(step == NARROW_STEPS - 1)
     def _():
         dh_out[...] = total[...].astype(bf16)
 
-
-def middle(h_two, dy_rows, w_three, w_four):
+    @pl.when(step >= NARROW_STEPS)
+    def _():
+        g_two[...] = jnp.dot(a_turned[...], dh_out[...], preferred_element_type=f32)
+
+
+def narrow_across(step):
+    return across_at(jnp.minimum(step, NARROW_STEPS - 1))
+
+
+def narrow_down(step):
+    return down_at(jnp.minimum(step, NARROW_STEPS - 1))
+
+
+def tall_down(step):
+    return down_at(jnp.maximum(step - NARROW_STEPS, 0))
+
+
+def middle(h_two, dy_rows, w_three, w_four, a_turned):
     rows, dim = h_two.shape
-    wide = w_three.shape[1]
-    block = 512
+    wide, tall = w_three.shape[1], a_turned.shape[0]
+    block, tall_block = wide // NARROW_STEPS, tall // TALL_STEPS
     f32, bf16 = jnp.float32, jnp.bfloat16
     whole = pl.BlockSpec((rows, dim), whole_at)
-    across, down = pl.BlockSpec((dim, block), across_at), pl.BlockSpec((block, dim), down_at)
+    across, down = pl.BlockSpec((dim, block), narrow_across), pl.BlockSpec((block, dim), narrow_down)
     return pl.pallas_call(
         middle_kernel,
-        grid=(wide // block,),
-        out_shape=(jax.ShapeDtypeStruct((dim, wide), f32), jax.ShapeDtypeStruct((wide, dim), f32), jax.ShapeDtypeStruct((rows, dim), bf16)),
-        in_specs=[whole, whole, across, down],
-        out_specs=(across, down, whole),
+        grid=(NARROW_STEPS + TALL_STEPS,),
+        out_shape=(jax.ShapeDtypeStruct((dim, wide), f32), jax.ShapeDtypeStruct((wide, dim), f32), jax.ShapeDtypeStruct((tall, dim), f32), jax.ShapeDtypeStruct((rows, dim), bf16)),
+        in_specs=[whole, whole, across, down, pl.BlockSpec((tall_block, rows), tall_down)],
+        out_specs=(across, down, pl.BlockSpec((tall_block, dim), tall_down), whole),
         scratch_shapes=[pltpu.VMEM((rows, dim), f32), pltpu.VMEM((dim, rows), bf16)],
         compiler_params=pltpu.CompilerParams(vmem_limit_bytes=VMEM_BYTES),
         name='middle',
-    )(h_two, dy_rows, w_three, w_four)
+    )(h_two, dy_rows, w_three, w_four, a_turned)
 
 
 def local_grads(x_rows, dy_rows, w_one, w_two, w_three, w_four):
     z_one, a_turned, h_two, x_turned = forward_wide(x_rows, w_one, w_two)
-    g_three, g_four, dh_two = middle(h_two, dy_rows, w_three, w_four)
-    g_two = jnp.dot(a_turned, dh_two, preferred_element_type=jnp.float32)
+    g_three, g_four, g_two, dh_two = middle(h_two, dy_rows, w_three, w_four, a_turned)
     return (x_turned, dh_two, z_one, w_two), g_two, g_three, g_four
 
 
@@ -232,7 +253,7 @@
 BLOCKS_AFTER = (2, 2, 1)
 
 
-def reduce_kernel(x_turned, dh_two, z_one, w_two, g_two, g_three, g_four, shard, swapped, norm_tile, own, wide_own, part, relay1, final1, relay2, final2, relay3, final3, norm_own, norm_a, norm_b, norm_c, x_buf, dh_buf, z_buf, w_buf, out_buf, load_sem, part_send, part_recv, ring_sems, swap_sems, norm_sems, fetch_sems, out_sems):
+def reduce_kernel(x_turned, dh_two, z_one, w_two, g_two, g_three, g_four, shard, own, wide_own, part, relay1, final1, relay2, final2, relay3, final3, norm_own, norm_a, norm_b, norm_c, x_buf, dh_buf, z_buf, w_buf, out_buf, load_sem, part_send, part_recv, ring_sems, swap_sems, norm_sems, fetch_sems, out_sems):
     place = Place()
     units = unit_list()
     chunks = -(-len(units) // 3)
@@ -378,7 +399,7 @@
     load(0)
     for copy in steady:
         copy.wait()
-    first_blocks = 6
+    first_blocks = 2
     wide_blocks(0, first_blocks)
 
     def turn(now, carry):
@@ -398,9 +419,9 @@
 
     lax.fori_loop(1, chunks + len(stages), turn, 0)
 
-    n_three = UNITS_OF[3]
-    send(shard.at[pl.ds(0, n_three)], swapped.at[pl.ds(0, n_three)], swap_sems.at[0], swap_sems.at[1], partner)
-    send(shard.at[pl.ds(wide_base, wide_units)], swapped.at[pl.ds(n_three, wide_units)], swap_sems.at[0], swap_sems.at[1], partner)
+    swap_count = UNITS_OF[3] + wide_units
+    swapped = shard.at[pl.ds(len(units), swap_count)]
+    send(shard.at[pl.ds(first_unit(3), swap_count)], swapped, swap_sems.at[0], swap_sems.at[1], partner)
 
     def fold(unit, total):
         value = shard[unit]
@@ -420,7 +441,7 @@
         total = board[0]
         for row in range(1, len(group) + 1):
             total = total + board[row]
-    norm_tile[...] = total
+    shard[len(units) + swap_count] = jnp.concatenate([total] * (WIDTH // 128), axis=1)
 
     await_bytes(swapped, swap_sems.at[0])
     await_bytes(swapped, swap_sems.at[1])
@@ -479,25 +500,24 @@
     vmem_spec = pl.BlockSpec(memory_space=pltpu.VMEM)
     return pl.pallas_call(
         reduce_kernel,
-        out_shape=(
-            jax.ShapeDtypeStruct((n, ROWS, WIDTH), f32),
-            jax.ShapeDtypeStruct((UNITS_OF[3] + UNITS_OF[1], ROWS, WIDTH), f32),
-            jax.ShapeDtypeStruct((ROWS, 128), f32),
-        ),
+        out_shape=jax.ShapeDtypeStruct((n + UNITS_OF[3] + UNITS_OF[1] + 1, ROWS, WIDTH), f32),
         in_specs=[any_spec] * len(args),
-        out_specs=(vmem_spec,) * 3,
+        out_specs=vmem_spec,
         scratch_shapes=scratch,
         compiler_params=pltpu.CompilerParams(collective_id=0, has_side_effects=True, vmem_limit_bytes=VMEM_BYTES),
         name='reduce_grads',
     )(*args)
 
 
-def adam_kernel(lr_ref, clip_ref, norm_tile, shard, swapped, *refs):
+def adam_kernel(lr_ref, clip_ref, shard, *refs):
     masters, moms, variances = refs[0:4], refs[4:8], refs[8:12]
     new_masters, new_moms, new_vars = refs[12:16], refs[16:20], refs[20:24]
-    two_rows, four_rows, norm_ref = refs[24:27]
+    two_rows, four_rows, norm_ref, one_rows, three_rows = refs[24:29]
+    spread = {1: one_rows, 3: three_rows}
+    units = len(unit_list())
+    norm_tile = shard[units + UNITS_OF[3] + UNITS_OF[1]][:, 0:128]
     core = lax.rem(lax.axis_index('dp'), 2)
-    grad_norm = jnp.sqrt(jnp.sum(jnp.sum(norm_tile[...], axis=1, keepdims=True), axis=0, keepdims=True))
+    grad_norm = jnp.sqrt(jnp.sum(jnp.sum(norm_tile, axis=1, keepdims=True), axis=0, keepdims=True))
     norm_ref[...] = grad_norm
     clip_scale = jnp.minimum(1.0, clip_ref[...] / (grad_norm + NORM_EPS))
     learn_rate = lr_ref[...]
@@ -521,11 +541,11 @@
             for piece in range(UNITS_OF[mat]):
                 col = (half * UNITS_OF[mat] + piece) * WIDTH
                 where = (slice(None), slice(col, col + WIDTH))
-                block = jnp.where(core == half, shard[first_unit(mat) + piece], swapped[base + piece])
-                update(mat - 1, where, jnp.where(core == 0, block[0:ROWS // 2], block[ROWS // 2:ROWS]))
-
-
-def adam_update(learn_rate, clip_max, norm_tile, shard, swapped, masters, moms, variances):
+                block = jnp.where(core == half, shard[first_unit(mat) + piece], shard[units + base + piece])
+                spread[mat][where] = update(mat - 1, where, jnp.where(core == 0, block[0:ROWS // 2], block[ROWS // 2:ROWS]))
+
+
+def adam_update(learn_rate, clip_max, shard, masters, moms, variances):
     state = list(masters) + list(moms) + list(variances)
     f32, bf16 = jnp.float32, jnp.bfloat16
     vmem_spec = pl.BlockSpec(memory_space=pltpu.VMEM)
@@ -534,8 +554,10 @@
         jax.ShapeDtypeStruct((UNITS_OF[2], ROWS, WIDTH), bf16),
         jax.ShapeDtypeStruct((UNITS_OF[4], ROWS, WIDTH), bf16),
         jax.ShapeDtypeStruct((1, 1), f32),
+        jax.ShapeDtypeStruct(masters[0].shape, f32),
+        jax.ShapeDtypeStruct(masters[2].shape, f32),
     ]
-    args = [learn_rate.reshape(1, 1), clip_max.reshape(1, 1), norm_tile, shard, swapped] + state
+    args = [learn_rate.reshape(1, 1), clip_max.reshape(1, 1), shard] + state
     return pl.pallas_call(
         adam_kernel,
         out_shape=out_shape,
@@ -603,13 +625,15 @@
         send(theirs, landing, swap_sems.at[0, index], swap_sems.at[1, index], partner)
     for copy in loads:
         copy.wait()
-    for index, (mat, rows, mine, landing) in enumerate(splits):
-        await_bytes(landing, swap_sems.at[1, index])
-        for piece in range(UNITS_OF[mat]):
-            cols = slice(piece * WIDTH, (piece + 1) * WIDTH)
-            top = jnp.where(place.core == 0, mine[:, cols], landing[:, cols])
-            bottom = jnp.where(place.core == 0, landing[:, cols], mine[:, cols])
-            board[(first_unit(mat) + piece,) + here] = jnp.concatenate([top, bottom], axis=0).astype(board.dtype)
+
+    def assemble():
+        for index, (mat, rows, mine, landing) in enumerate(splits):
+            await_bytes(landing, swap_sems.at[1, index])
+            for piece in range(UNITS_OF[mat]):
+                cols = slice(piece * WIDTH, (piece + 1) * WIDTH)
+                top = jnp.where(place.core == 0, mine[:, cols], landing[:, cols])
+                bottom = jnp.where(place.core == 0, landing[:, cols], mine[:, cols])
+                board[(first_unit(mat) + piece,) + here] = jnp.concatenate([top, bottom], axis=0).astype(board.dtype)
 
     rings = []
     for order in range(3):
@@ -636,7 +660,12 @@
 
     stages = ((begin, 0), (pass_on, 0), (begin, 1), (pass_on, 1), (begin, 2), (pass_on, 2), (hand_over, 2), (tidy, 2))
 
+    ready = first_unit(3) // 3
+
     def turn(now, carry):
+        @pl.when(now == ready)
+        def _():
+            assemble()
         for lag, (stage, level) in enumerate(stages):
             chunk = now - lag
             for order in range(3):
@@ -722,11 +751,11 @@
 
 
 def sync_and_update(grads, masters, moms, variances, learn_rate, clip_max):
-    shard, swapped, norm_tile = reduce_grads(*grads)
-    results = adam_update(learn_rate, clip_max, norm_tile, shard, swapped, masters, moms, variances)
+    shard = reduce_grads(*grads)
+    results = adam_update(learn_rate, clip_max, shard, masters, moms, variances)
     new_masters, new_moms, new_vars = results[0:4], results[4:8], results[8:12]
-    two_rows, four_rows, grad_norm = results[12:15]
-    board, other = gather_rows(new_masters[0], new_masters[2], two_rows, four_rows)
+    two_rows, four_rows, grad_norm, one_rows, three_rows = results[12:17]
+    board, other = gather_rows(one_rows, three_rows, two_rows, four_rows)
     new_weights = place_weights(board, other)
     return tuple(new_weights) + tuple(new_masters) + tuple(new_moms) + tuple(new_vars) + (grad_norm.reshape(()),)
 

time: 252 us -> 245 us (0.972)
  matrix products: 15.9 us -> 0 us
  Pallas kernels: 229 us -> 241 us
  local copies, waits for them, and re-layouts: 4.29 us -> 1.1 us
    dot_general x1 -> x0, matrix products: 15.9 us -> none  [local_grads(): g_two = jnp.dot(a_turned, dh_two, preferred_element_type=jnp.float32)]
    pallas_call x2, Pallas kernels: 135 us -> 148 us  [the longest x1 114 us: reduce_grads(): pl.pallas_call(reduce_kernel, out_shape=jax.ShapeDtypeStruct((n + UNITS_O...]
    unnamed x34 -> x26, local copies, waits for them, and re-layouts: 4.29 us -> 1.1 us
where the time goes in v6:
time: 245 us; the launch traced here: 244 us
  Pallas kernels  241 us (98%)
    pallas_call x1, Pallas kernels, reduce_grads(): pl.pallas_call(reduce_kernel, out_shape=jax.ShapeDtypeStruct((n + UNITS_O...  114 us
    pallas_call x1, Pallas kernels, gather_rows(): pl.pallas_call(gather_kernel, out_shape=(full, full), in_specs=[pl.BlockS...  56.1 us
    pallas_call x1, Pallas kernels, middle(): pl.pallas_call(middle_kernel, grid=(NARROW_STEPS + TALL_STEPS,), out_shap...  33.8 us
    pallas_call x1, Pallas kernels, forward_wide(): pl.pallas_call(forward_kernel, grid=(wide // block,), out_shape=(jax.Shap...  28.2 us
    pallas_call x1, Pallas kernels, place_weights(): pl.pallas_call(place_kernel, out_shape=(jax.ShapeDtypeStruct(cube + (ROWS...  7.42 us

profile of v6, /device:TPU:1, one launch (start us, length us, event | category | flops | bytes accessed | tf_op | source)
XLA Modules:
  0.0 244.0 jit_solution(18151159503629309335)
XLA Ops:
  0.7 28.2 %forward_wide.1 = (bf16[1024,8192]{1,0:T(8,128)(2,1)}, bf16[8192,1024]{1,0:T(8,128)(2,1)}, bf16[1024,512]{1,0:T(8,128)(2,1)}, bf16[512,1024]{1,0:T(8,128)(2,1)}) custom-call(bf16[1024,512]{1,0:T(8,128)(2,1)} %x_ref.1, bf16[512,8192]{1,0:T(8,128)(2,1)} %w_one.1, bf16[8192,512]{1,0:T(8,128)(2,1)} %w_two.3), custom_call_target="tpu_custom_call" | custom-call | tf_op jit(solution)/shard_map/forward_wide/pallas_call | solution.py:74
  28.9 33.8 %middle.1 = (f32[512,2048]{1,0:T(8,128)}, f32[2048,512]{1,0:T(8,128)}, f32[8192,512]{1,0:T(8,128)}, bf16[1024,512]{1,0:T(8,128)(2,1)}) custom-call(bf16[1024,512]{1,0:T(8,128)(2,1)} %get-tuple-element.49.h_ref, bf16[1024,512]{1,0:T(8,128)(2,1)} %dy_ref.1, bf16[512,2048]{1,0:T(8,128)(2,1)} %w_three.1, bf16[2048,512]{1,0:T(8,128)(2,1)} %w_four.1, ...), custom_call_target="tpu_custom_call" | custom-call | tf_op jit(solution)/shard_map/middle/pallas_call | solution.py:137
  62.7 0.0 copy-start.1
  62.8 0.0 copy-start.2
  62.8 0.0 copy-start.3
  62.8 0.0 copy-start.4
  62.8 0.0 copy-start.5
  62.8 0.0 copy-start.6
  62.8 0.0 copy-start.7
  62.8 0.0 copy-start.8
  62.8 0.0 copy-start.9
  62.9 0.0 copy-start.10
  62.9 0.0 copy-start.11
  62.9 0.0 copy-start.12
  62.9 113.7 %reduce_grads.1.shard = f32[31,8,512]{2,1,0:T(8,128)} custom-call(bf16[512,1024]{1,0:T(8,128)(2,1)} %get-tuple-element.48.x_turned, bf16[1024,512]{1,0:T(8,128)(2,1)} %get-tuple-element.51.dh_two, bf16[1024,8192]{1,0:T(8,128)(2,1)} %get-tuple-element.52.z_one, bf16[8192,512]{1,0:T(8,128)(2,1)} %w_two.3, f32[4,4,4,2,64,512]{5,4,3,2,1,0:T(8,128)} %bitcast.12, ...), custom_call_target="tpu_custom_call" | custom-call | tf_op jit(solution)/shard_map/reduce_grads/pallas_call | solution.py:501
  177.9 0.0 copy-done.1
  177.9 0.0 copy-done.2
  177.9 0.0 copy-done.3
  178.0 0.0 copy-done.4
  178.0 0.0 copy-done.5
  178.1 1.0 copy-done
  179.1 1.2 adam_update.1
  180.3 56.1 %gather_rows.1 = (bf16[20,4,4,4,8,512]{5,4,3,2,1,0:T(8,128)(2,1)S(1)}, bf16[20,4,4,4,8,512]{5,4,3,2,1,0:T(8,128)(2,1)S(1)}) custom-call(f32[4,8192]{1,0:T(4,128)S(1)} %get-tuple-element.56.one_rows, f32[4,2048]{1,0:T(4,128)S(1)} %get-tuple-element.57.three_rows, bf16[8,8,512]{2,1,0:T(8,128)(2,1)S(1)} %get-tuple-element.58.two_rows, ...), custom_call_target="tpu_custom_call" | custom-call | tf_op jit(solution)/shard_map/gather_rows/pallas_call | solution.py:689
  236.5 7.4 %place_weights.1 = (bf16[4,4,4,8,8192]{4,3,2,1,0:T(8,128)(2,1)}, bf16[4,4,4,2,64,512]{5,4,3,2,1,0:T(8,128)(2,1)}, bf16[4,4,4,8,2048]{4,3,2,1,0:T(8,128)(2,1)}, bf16[4,4,4,2,16,512]{5,4,3,2,1,0:T(8,128)(2,1)}) custom-call(bf16[20,4,4,4,8,512]{5,4,3,2,1,0:T(8,128)(2,1)S(1)} %get-tuple-element.60.board, bf16[20,4,4,4,8,512]{5,4,3,2,1,0:T(8,128)(2,1)S(1)} %get-tuple-element.61.other), custom_call_target="tpu_custom_call" | custom-call | tf_op jit(solution)/shard_map/place_weights/pallas_call | solution.py:730
  (8 shorter events, 0.0 us)
Async XLA Ops:
  62.7 115.2 %copy-start.1 = (f32[4,8192]{1,0:T(4,128)S(1)}, f32[4,8192]{1,0:T(4,128)}, u32[]{:S(2)}) copy-start(f32[4,8192]{1,0:T(4,128)} %refs_0_.1) | copy-start | bytes 393220
  62.8 115.2 %copy-start.2 = (f32[64,512]{1,0:T(8,128)S(1)}, f32[64,512]{1,0:T(8,128)}, u32[]{:S(2)}) copy-start(f32[64,512]{1,0:T(8,128)} %refs_1_.1) | copy-start | bytes 393220
  62.8 115.2 %copy-start.3 = (f32[4,8192]{1,0:T(4,128)S(1)}, f32[4,8192]{1,0:T(4,128)}, u32[]{:S(2)}) copy-start(f32[4,8192]{1,0:T(4,128)} %refs_4_.1) | copy-start | bytes 393220
  62.8 115.2 %copy-start.4 = (f32[64,512]{1,0:T(8,128)S(1)}, f32[64,512]{1,0:T(8,128)}, u32[]{:S(2)}) copy-start(f32[64,512]{1,0:T(8,128)} %refs_5_.1) | copy-start | bytes 393220
  62.8 115.2 %copy-start.5 = (f32[4,8192]{1,0:T(4,128)S(1)}, f32[4,8192]{1,0:T(4,128)}, u32[]{:S(2)}) copy-start(f32[4,8192]{1,0:T(4,128)} %refs_8_.1) | copy-start | bytes 393220
  62.8 115.2 %copy-start.6 = (f32[64,512]{1,0:T(8,128)S(1)}, f32[64,512]{1,0:T(8,128)}, u32[]{:S(2)}) copy-start(f32[64,512]{1,0:T(8,128)} %refs_9_.1) | copy-start | bytes 393220
  62.8 115.2 %copy-start.7 = (f32[4,2048]{1,0:T(4,128)S(1)}, f32[4,2048]{1,0:T(4,128)}, u32[]{:S(2)}) copy-start(f32[4,2048]{1,0:T(4,128)} %refs_2_.1) | copy-start | bytes 98308
  62.8 115.2 %copy-start.8 = (f32[16,512]{1,0:T(8,128)S(1)}, f32[16,512]{1,0:T(8,128)}, u32[]{:S(2)}) copy-start(f32[16,512]{1,0:T(8,128)} %refs_3_.1) | copy-start | bytes 98308
  62.8 115.2 %copy-start.9 = (f32[4,2048]{1,0:T(4,128)S(1)}, f32[4,2048]{1,0:T(4,128)}, u32[]{:S(2)}) copy-start(f32[4,2048]{1,0:T(4,128)} %refs_6_.1) | copy-start | bytes 98308
  62.9 115.2 %copy-start.10 = (f32[16,512]{1,0:T(8,128)S(1)}, f32[16,512]{1,0:T(8,128)}, u32[]{:S(2)}) copy-start(f32[16,512]{1,0:T(8,128)} %refs_7_.1) | copy-start | bytes 98308
  62.9 115.2 %copy-start.11 = (f32[4,2048]{1,0:T(4,128)S(1)}, f32[4,2048]{1,0:T(4,128)}, u32[]{:S(2)}) copy-start(f32[4,2048]{1,0:T(4,128)} %refs_10_.1) | copy-start | bytes 98308
  62.9 115.2 %copy-start.12 = (f32[16,512]{1,0:T(8,128)S(1)}, f32[16,512]{1,0:T(8,128)}, u32[]{:S(2)}) copy-start(f32[16,512]{1,0:T(8,128)} %refs_11_.1) | copy-start | bytes 98308
  178.0 1.0 copy-start

commit v7 on v6

--- a/solution.py
+++ b/solution.py
@@ -47,58 +47,40 @@
     return 0.5 * (1.0 + lax.erf(pre_wide * INV_SQRT2)) + pre_wide * INV_SQRT2PI * jnp.exp(-0.5 * pre_wide * pre_wide)
 
 
-def forward_kernel(x_ref, w_one, w_two, z_out, a_turned, h_out, x_turned, total):
+WIDE_STEPS = 8
+NARROW_STEPS = 4
+TALL_STEPS = 8
+NARROW_FROM = WIDE_STEPS
+TALL_FROM = WIDE_STEPS + NARROW_STEPS
+
+
+def local_kernel(x_ref, dy_ref, w_one, w_two, w_three, w_four, z_out, x_turned, g_three, g_four, g_two, dh_out, total, held, h_turned, a_turned):
     step = pl.program_id(0)
+    f32, bf16 = jnp.float32, jnp.bfloat16
 
     @pl.when(step == 0)
     def _():
         total[...] = jnp.zeros_like(total)
         x_turned[...] = x_ref[...].T
 
-    z_one = jnp.dot(x_ref[...], w_one[...], preferred_element_type=jnp.float32).astype(jnp.bfloat16)
-    z_out[...] = z_one
-    a_one = gelu_value(z_one).astype(jnp.bfloat16)
-    a_turned[...] = a_one.T
-    total[...] += jnp.dot(a_one, w_two[...], preferred_element_type=jnp.float32)
-
-    @pl.when(step == pl.num_programs(0) - 1)
+    @pl.when(step < NARROW_FROM)
     def _():
-        h_out[...] = total[...].astype(jnp.bfloat16)
-
-
-def forward_wide(x_rows, w_one, w_two):
-    rows, dim = x_rows.shape
-    wide = w_one.shape[1]
-    block = 1024
-    bf16 = jnp.bfloat16
-    return pl.pallas_call(
-        forward_kernel,
-        grid=(wide // block,),
-        out_shape=(jax.ShapeDtypeStruct((rows, wide), bf16), jax.ShapeDtypeStruct((wide, rows), bf16), jax.ShapeDtypeStruct((rows, dim), bf16), jax.ShapeDtypeStruct((dim, rows), bf16)),
-        in_specs=[pl.BlockSpec((rows, dim), whole_at), pl.BlockSpec((dim, block), across_at), pl.BlockSpec((block, dim), down_at)],
-        out_specs=(pl.BlockSpec((rows, block), across_at), pl.BlockSpec((block, rows), down_at), pl.BlockSpec((rows, dim), whole_at), pl.BlockSpec((dim, rows), whole_at)),
-        scratch_shapes=[pltpu.VMEM((rows, dim), jnp.float32)],
-        compiler_params=pltpu.CompilerParams(vmem_limit_bytes=VMEM_BYTES),
-        name='forward_wide',
-    )(x_rows, w_one, w_two)
-
-
-NARROW_STEPS = 4
-TALL_STEPS = 8
-
-
-def middle_kernel(h_ref, dy_ref, w_three, w_four, a_turned, g_three, g_four, g_two, dh_out, total, h_turned):
-    step = pl.program_id(0)
-    f32, bf16 = jnp.float32, jnp.bfloat16
-
-    @pl.when(step == 0)
+        z_one = jnp.dot(x_ref[...], w_one[...], preferred_element_type=f32).astype(bf16)
+        z_out[...] = z_one
+        a_one = gelu_value(z_one).astype(bf16)
+        a_turned[step] = a_one.T
+        total[...] += jnp.dot(a_one, w_two[...], preferred_element_type=f32)
+
+    @pl.when(step == NARROW_FROM - 1)
     def _():
+        h_two = total[...].astype(bf16)
+        held[...] = h_two
+        h_turned[...] = h_two.T
         total[...] = jnp.zeros_like(total)
-        h_turned[...] = h_ref[...].T
-
-    @pl.when(step < NARROW_STEPS)
+
+    @pl.when((step >= NARROW_FROM) & (step < TALL_FROM))
     def _():
-        z_three = jnp.dot(h_ref[...], w_three[...], preferred_element_type=f32).astype(bf16)
+        z_three = jnp.dot(held[...], w_three[...], preferred_element_type=f32).astype(bf16)
         a_three = gelu_value(z_three).astype(bf16)
         da_three = lax.dot_general(dy_ref[...], w_four[...], BY_COLUMNS, preferred_element_type=f32).astype(bf16)
         dz_three = (da_three.astype(f32) * gelu_slope(z_three)).astype(bf16)
@@ -106,62 +88,78 @@
         g_three[...] = jnp.dot(h_turned[...], dz_three, preferred_element_type=f32)
         total[...] += lax.dot_general(dz_three, w_three[...], BY_COLUMNS, preferred_element_type=f32)
 
-    @pl.when(step == NARROW_STEPS - 1)
+    @pl.when(step == TALL_FROM - 1)
     def _():
         dh_out[...] = total[...].astype(bf16)
 
-    @pl.when(step >= NARROW_STEPS)
+    @pl.when(step >= TALL_FROM)
     def _():
-        g_two[...] = jnp.dot(a_turned[...], dh_out[...], preferred_element_type=f32)
+        g_two[...] = jnp.dot(a_turned[step - TALL_FROM], dh_out[...], preferred_element_type=f32)
+
+
+def whole_at(step):
+    return 0, 0
+
+
+def held_step(step, first, count):
+    return jnp.clip(step - first, 0, count - 1)
+
+
+def wide_across(step):
+    return 0, held_step(step, 0, WIDE_STEPS)
+
+
+def wide_down(step):
+    return held_step(step, 0, WIDE_STEPS), 0
 
 
 def narrow_across(step):
-    return across_at(jnp.minimum(step, NARROW_STEPS - 1))
+    return 0, held_step(step, NARROW_FROM, NARROW_STEPS)
 
 
 def narrow_down(step):
-    return down_at(jnp.minimum(step, NARROW_STEPS - 1))
+    return held_step(step, NARROW_FROM, NARROW_STEPS), 0
 
 
 def tall_down(step):
-    return down_at(jnp.maximum(step - NARROW_STEPS, 0))
-
-
-def middle(h_two, dy_rows, w_three, w_four, a_turned):
-    rows, dim = h_two.shape
-    wide, tall = w_three.shape[1], a_turned.shape[0]
-    block, tall_block = wide // NARROW_STEPS, tall // TALL_STEPS
+    return held_step(step, TALL_FROM, TALL_STEPS), 0
+
+
+def local_grads(x_rows, dy_rows, w_one, w_two, w_three, w_four):
+    rows, dim = x_rows.shape
+    wide, narrow = w_one.shape[1], w_three.shape[1]
     f32, bf16 = jnp.float32, jnp.bfloat16
     whole = pl.BlockSpec((rows, dim), whole_at)
-    across, down = pl.BlockSpec((dim, block), narrow_across), pl.BlockSpec((block, dim), narrow_down)
-    return pl.pallas_call(
-        middle_kernel,
-        grid=(NARROW_STEPS + TALL_STEPS,),
-        out_shape=(jax.ShapeDtypeStruct((dim, wide), f32), jax.ShapeDtypeStruct((wide, dim), f32), jax.ShapeDtypeStruct((tall, dim), f32), jax.ShapeDtypeStruct((rows, dim), bf16)),
-        in_specs=[whole, whole, across, down, pl.BlockSpec((tall_block, rows), tall_down)],
-        out_specs=(across, down, pl.BlockSpec((tall_block, dim), tall_down), whole),
-        scratch_shapes=[pltpu.VMEM((rows, dim), f32), pltpu.VMEM((dim, rows), bf16)],
+    slab, thin, tall = wide // WIDE_STEPS, narrow // NARROW_STEPS, wide // TALL_STEPS
+    z_one, x_turned, g_three, g_four, g_two, dh_two = pl.pallas_call(
+        local_kernel,
+        grid=(TALL_FROM + TALL_STEPS,),
+        out_shape=(
+            jax.ShapeDtypeStruct((rows, wide), bf16),
+            jax.ShapeDtypeStruct((dim, rows), bf16),
+            jax.ShapeDtypeStruct((dim, narrow), f32),
+            jax.ShapeDtypeStruct((narrow, dim), f32),
+            jax.ShapeDtypeStruct((wide, dim), f32),
+            jax.ShapeDtypeStruct((rows, dim), bf16),
+        ),
+        in_specs=[
+            whole, whole,
+            pl.BlockSpec((dim, slab), wide_across), pl.BlockSpec((slab, dim), wide_down),
+            pl.BlockSpec((dim, thin), narrow_across), pl.BlockSpec((thin, dim), narrow_down),
+        ],
+        out_specs=(
+            pl.BlockSpec((rows, slab), wide_across),
+            pl.BlockSpec((dim, rows), whole_at),
+            pl.BlockSpec((dim, thin), narrow_across),
+            pl.BlockSpec((thin, dim), narrow_down),
+            pl.BlockSpec((tall, dim), tall_down),
+            whole,
+        ),
+        scratch_shapes=[pltpu.VMEM((rows, dim), f32), pltpu.VMEM((rows, dim), bf16), pltpu.VMEM((dim, rows), bf16), pltpu.VMEM((WIDE_STEPS, slab, rows), bf16)],
         compiler_params=pltpu.CompilerParams(vmem_limit_bytes=VMEM_BYTES),
-        name='middle',
-    )(h_two, dy_rows, w_three, w_four, a_turned)
-
-
-def local_grads(x_rows, dy_rows, w_one, w_two, w_three, w_four):
-    z_one, a_turned, h_two, x_turned = forward_wide(x_rows, w_one, w_two)
-    g_three, g_four, g_two, dh_two = middle(h_two, dy_rows, w_three, w_four, a_turned)
+        name='local_grads',
+    )(x_rows, dy_rows, w_one, w_two, w_three, w_four)
     return (x_turned, dh_two, z_one, w_two), g_two, g_three, g_four
-
-
-def whole_at(step):
-    return 0, 0
-
-
-def across_at(step):
-    return 0, step
-
-
-def down_at(step):
-    return step, 0
 
 
 class Place:

time: 245 us -> 238 us (0.971)
  Pallas kernels: 241 us -> 234 us
    pallas_call x2 -> x1, Pallas kernels: 62.1 us -> 55.5 us  [local_grads(): pl.pallas_call(local_kernel, grid=(TALL_FROM + TALL_STEPS,), out_shape=(j...]
where the time goes in v7:
time: 238 us; the launch traced here: 237 us
  Pallas kernels  234 us (98%)
    pallas_call x1, Pallas kernels, reduce_grads(): pl.pallas_call(reduce_kernel, out_shape=jax.ShapeDtypeStruct((n + UNITS_O...  114 us
    pallas_call x1, Pallas kernels, gather_rows(): pl.pallas_call(gather_kernel, out_shape=(full, full), in_specs=[pl.BlockS...  56.1 us
    pallas_call x1, Pallas kernels, local_grads(): pl.pallas_call(local_kernel, grid=(TALL_FROM + TALL_STEPS,), out_shape=(j...  55.5 us
    pallas_call x1, Pallas kernels, place_weights(): pl.pallas_call(place_kernel, out_shape=(jax.ShapeDtypeStruct(cube + (ROWS...  7.42 us

profile of v7, /device:TPU:1, one launch (start us, length us, event | category | flops | bytes accessed | tf_op | source)
XLA Modules:
  0.0 237.4 jit_solution(16565821099381739146)
XLA Ops:
  0.7 55.5 %local_grads.1 = (bf16[1024,8192]{1,0:T(8,128)(2,1)}, bf16[512,1024]{1,0:T(8,128)(2,1)}, f32[512,2048]{1,0:T(8,128)}, f32[2048,512]{1,0:T(8,128)}, f32[8192,512]{1,0:T(8,128)}, /*index=5*/bf16[1024,512]{1,0:T(8,128)(2,1)}) custom-call(bf16[1024,512]{1,0:T(8,128)(2,1)} %x_ref.1, bf16[1024,512]{1,0:T(8,128)(2,1)} %dy_ref.1, bf16[512,8192]{1,0:T(8,128)(2,1)} %w_one.1, ...), custom_call_target="tpu_custom_call" | custom-call | tf_op jit(solution)/shard_map/local_grads/pallas_call | solution.py:134
  56.1 0.0 copy-start.1
  56.1 0.0 copy-start.2
  56.2 0.0 copy-start.3
  56.2 0.0 copy-start.4
  56.2 0.0 copy-start.5
  56.2 0.0 copy-start.6
  56.2 0.0 copy-start.7
  56.2 0.0 copy-start.8
  56.2 0.0 copy-start.9
  56.2 0.0 copy-start.10
  56.3 0.0 copy-start.11
  56.3 0.0 copy-start.12
  56.3 113.7 %reduce_grads.1.shard = f32[31,8,512]{2,1,0:T(8,128)} custom-call(bf16[512,1024]{1,0:T(8,128)(2,1)} %get-tuple-element.46.x_turned, bf16[1024,512]{1,0:T(8,128)(2,1)} %get-tuple-element.47.dh_two, bf16[1024,8192]{1,0:T(8,128)(2,1)} %get-tuple-element.48.z_one, bf16[8192,512]{1,0:T(8,128)(2,1)} %w_two.3, f32[4,4,4,2,64,512]{5,4,3,2,1,0:T(8,128)} %bitcast.12, ...), custom_call_target="tpu_custom_call" | custom-call | tf_op jit(solution)/shard_map/reduce_grads/pallas_call | solution.py:499
  171.3 0.0 copy-done.1
  171.3 0.0 copy-done.2
  171.3 0.0 copy-done.3
  171.3 0.0 copy-done.4
  171.3 0.0 copy-done.5
  171.3 0.0 copy-done.6
  171.4 1.0 copy-done
  172.5 1.2 adam_update.1
  173.7 56.1 %gather_rows.1 = (bf16[20,4,4,4,8,512]{5,4,3,2,1,0:T(8,128)(2,1)S(1)}, bf16[20,4,4,4,8,512]{5,4,3,2,1,0:T(8,128)(2,1)S(1)}) custom-call(f32[4,8192]{1,0:T(4,128)S(1)} %get-tuple-element.52.one_rows, f32[4,2048]{1,0:T(4,128)S(1)} %get-tuple-element.53.three_rows, bf16[8,8,512]{2,1,0:T(8,128)(2,1)S(1)} %get-tuple-element.54.two_rows, ...), custom_call_target="tpu_custom_call" | custom-call | tf_op jit(solution)/shard_map/gather_rows/pallas_call | solution.py:687
  229.8 7.4 %place_weights.1 = (bf16[4,4,4,8,8192]{4,3,2,1,0:T(8,128)(2,1)}, bf16[4,4,4,2,64,512]{5,4,3,2,1,0:T(8,128)(2,1)}, bf16[4,4,4,8,2048]{4,3,2,1,0:T(8,128)(2,1)}, bf16[4,4,4,2,16,512]{5,4,3,2,1,0:T(8,128)(2,1)}) custom-call(bf16[20,4,4,4,8,512]{5,4,3,2,1,0:T(8,128)(2,1)S(1)} %get-tuple-element.56.board, bf16[20,4,4,4,8,512]{5,4,3,2,1,0:T(8,128)(2,1)S(1)} %get-tuple-element.57.other), custom_call_target="tpu_custom_call" | custom-call | tf_op jit(solution)/shard_map/place_weights/pallas_call | solution.py:728
  (7 shorter events, 0.0 us)
Async XLA Ops:
  56.1 115.2 %copy-start.1 = (f32[4,8192]{1,0:T(4,128)S(1)}, f32[4,8192]{1,0:T(4,128)}, u32[]{:S(2)}) copy-start(f32[4,8192]{1,0:T(4,128)} %refs_0_.1) | copy-start | bytes 393220
  56.1 115.2 %copy-start.2 = (f32[64,512]{1,0:T(8,128)S(1)}, f32[64,512]{1,0:T(8,128)}, u32[]{:S(2)}) copy-start(f32[64,512]{1,0:T(8,128)} %refs_1_.1) | copy-start | bytes 393220
  56.2 115.2 %copy-start.3 = (f32[4,8192]{1,0:T(4,128)S(1)}, f32[4,8192]{1,0:T(4,128)}, u32[]{:S(2)}) copy-start(f32[4,8192]{1,0:T(4,128)} %refs_4_.1) | copy-start | bytes 393220
  56.2 115.2 %copy-start.4 = (f32[64,512]{1,0:T(8,128)S(1)}, f32[64,512]{1,0:T(8,128)}, u32[]{:S(2)}) copy-start(f32[64,512]{1,0:T(8,128)} %refs_5_.1) | copy-start | bytes 393220
  56.2 115.2 %copy-start.5 = (f32[4,8192]{1,0:T(4,128)S(1)}, f32[4,8192]{1,0:T(4,128)}, u32[]{:S(2)}) copy-start(f32[4,8192]{1,0:T(4,128)} %refs_8_.1) | copy-start | bytes 393220
  56.2 115.2 %copy-start.6 = (f32[64,512]{1,0:T(8,128)S(1)}, f32[64,512]{1,0:T(8,128)}, u32[]{:S(2)}) copy-start(f32[64,512]{1,0:T(8,128)} %refs_9_.1) | copy-start | bytes 393220
  56.2 115.2 %copy-start.7 = (f32[4,2048]{1,0:T(4,128)S(1)}, f32[4,2048]{1,0:T(4,128)}, u32[]{:S(2)}) copy-start(f32[4,2048]{1,0:T(4,128)} %refs_2_.1) | copy-start | bytes 98308
  56.2 115.2 %copy-start.8 = (f32[16,512]{1,0:T(8,128)S(1)}, f32[16,512]{1,0:T(8,128)}, u32[]{:S(2)}) copy-start(f32[16,512]{1,0:T(8,128)} %refs_3_.1) | copy-start | bytes 98308
  56.2 115.1 %copy-start.9 = (f32[4,2048]{1,0:T(4,128)S(1)}, f32[4,2048]{1,0:T(4,128)}, u32[]{:S(2)}) copy-start(f32[4,2048]{1,0:T(4,128)} %refs_6_.1) | copy-start | bytes 98308
  56.2 115.1 %copy-start.10 = (f32[16,512]{1,0:T(8,128)S(1)}, f32[16,512]{1,0:T(8,128)}, u32[]{:S(2)}) copy-start(f32[16,512]{1,0:T(8,128)} %refs_7_.1) | copy-start | bytes 98308
  56.3 115.1 %copy-start.11 = (f32[4,2048]{1,0:T(4,128)S(1)}, f32[4,2048]{1,0:T(4,128)}, u32[]{:S(2)}) copy-start(f32[4,2048]{1,0:T(4,128)} %refs_10_.1) | copy-start | bytes 98308
  56.3 115.1 %copy-start.12 = (f32[16,512]{1,0:T(8,128)S(1)}, f32[16,512]{1,0:T(8,128)}, u32[]{:S(2)}) copy-start(f32[16,512]{1,0:T(8,128)} %refs_11_.1) | copy-start | bytes 98308
  171.4 1.0 copy-start

commit v8 on v7

--- a/solution.py
+++ b/solution.py
@@ -658,18 +658,20 @@
 
     stages = ((begin, 0), (pass_on, 0), (begin, 1), (pass_on, 1), (begin, 2), (pass_on, 2), (hand_over, 2), (tidy, 2))
 
-    ready = first_unit(3) // 3
+    early = 4
+    ready = -(-(first_unit(3) // 3) // 2)
 
     def turn(now, carry):
         @pl.when(now == ready)
         def _():
             assemble()
         for lag, (stage, level) in enumerate(stages):
-            chunk = now - lag
-            for order in range(3):
-                @pl.when((chunk >= 0) & (chunk < counts[order]))
-                def _(stage=stage, level=level, chunk=chunk, order=order):
-                    stage(order, 3 * chunk + order, level)
+            entered = now - lag
+            for chunk in (2 * entered - 1, 2 * entered) if lag < early else (entered,):
+                for order in range(3):
+                    @pl.when((chunk >= 0) & (chunk < counts[order]))
+                    def _(stage=stage, level=level, chunk=chunk, order=order):
+                        stage(order, 3 * chunk + order, level)
         return carry
 
     lax.fori_loop(0, chunks + len(stages) - 1, turn, 0)

time: 238 us -> 237 us (level)
  no operation moved by 1% of the time
where the time goes in v8:
time: 237 us; the launch traced here: 236 us
  Pallas kernels  233 us (98%)
    pallas_call x1, Pallas kernels, reduce_grads(): pl.pallas_call(reduce_kernel, out_shape=jax.ShapeDtypeStruct((n + UNITS_O...  114 us
    pallas_call x1, Pallas kernels, local_grads(): pl.pallas_call(local_kernel, grid=(TALL_FROM + TALL_STEPS,), out_shape=(j...  55.5 us
    pallas_call x1, Pallas kernels, gather_rows(): pl.pallas_call(gather_kernel, out_shape=(full, full), in_specs=[pl.BlockS...  55.1 us
    pallas_call x1, Pallas kernels, place_weights(): pl.pallas_call(place_kernel, out_shape=(jax.ShapeDtypeStruct(cube + (ROWS...  7.42 us

profile of v8, /device:TPU:1, one launch (start us, length us, event | category | flops | bytes accessed | tf_op | source)
XLA Modules:
  0.0 236.4 jit_solution(17686852907087627956)
XLA Ops:
  0.7 55.5 %local_grads.1 = (bf16[1024,8192]{1,0:T(8,128)(2,1)}, bf16[512,1024]{1,0:T(8,128)(2,1)}, f32[512,2048]{1,0:T(8,128)}, f32[2048,512]{1,0:T(8,128)}, f32[8192,512]{1,0:T(8,128)}, /*index=5*/bf16[1024,512]{1,0:T(8,128)(2,1)}) custom-call(bf16[1024,512]{1,0:T(8,128)(2,1)} %x_ref.1, bf16[1024,512]{1,0:T(8,128)(2,1)} %dy_ref.1, bf16[512,8192]{1,0:T(8,128)(2,1)} %w_one.1, ...), custom_call_target="tpu_custom_call" | custom-call | tf_op jit(solution)/shard_map/local_grads/pallas_call | solution.py:134
  56.1 0.0 copy-start.1
  56.1 0.0 copy-start.2
  56.2 0.0 copy-start.3
  56.2 0.0 copy-start.4
  56.2 0.0 copy-start.5
  56.2 0.0 copy-start.6
  56.2 0.0 copy-start.7
  56.2 0.0 copy-start.8
  56.2 0.0 copy-start.9
  56.2 0.0 copy-start.10
  56.3 0.0 copy-start.11
  56.3 0.0 copy-start.12
  56.3 113.7 %reduce_grads.1.shard = f32[31,8,512]{2,1,0:T(8,128)} custom-call(bf16[512,1024]{1,0:T(8,128)(2,1)} %get-tuple-element.46.x_turned, bf16[1024,512]{1,0:T(8,128)(2,1)} %get-tuple-element.47.dh_two, bf16[1024,8192]{1,0:T(8,128)(2,1)} %get-tuple-element.48.z_one, bf16[8192,512]{1,0:T(8,128)(2,1)} %w_two.3, f32[4,4,4,2,64,512]{5,4,3,2,1,0:T(8,128)} %bitcast.12, ...), custom_call_target="tpu_custom_call" | custom-call | tf_op jit(solution)/shard_map/reduce_grads/pallas_call | solution.py:499
  171.3 0.0 copy-done.1
  171.3 0.0 copy-done.2
  171.3 0.0 copy-done.3
  171.3 0.0 copy-done.4
  171.3 0.0 copy-done.5
  171.3 0.0 copy-done.6
  171.4 1.0 copy-done
  172.5 1.2 adam_update.1
  173.7 55.1 %gather_rows.1 = (bf16[20,4,4,4,8,512]{5,4,3,2,1,0:T(8,128)(2,1)S(1)}, bf16[20,4,4,4,8,512]{5,4,3,2,1,0:T(8,128)(2,1)S(1)}) custom-call(f32[4,8192]{1,0:T(4,128)S(1)} %get-tuple-element.52.one_rows, f32[4,2048]{1,0:T(4,128)S(1)} %get-tuple-element.53.three_rows, bf16[8,8,512]{2,1,0:T(8,128)(2,1)S(1)} %get-tuple-element.54.two_rows, ...), custom_call_target="tpu_custom_call" | custom-call | tf_op jit(solution)/shard_map/gather_rows/pallas_call | solution.py:689
  228.8 7.4 %place_weights.1 = (bf16[4,4,4,8,8192]{4,3,2,1,0:T(8,128)(2,1)}, bf16[4,4,4,2,64,512]{5,4,3,2,1,0:T(8,128)(2,1)}, bf16[4,4,4,8,2048]{4,3,2,1,0:T(8,128)(2,1)}, bf16[4,4,4,2,16,512]{5,4,3,2,1,0:T(8,128)(2,1)}) custom-call(bf16[20,4,4,4,8,512]{5,4,3,2,1,0:T(8,128)(2,1)S(1)} %get-tuple-element.56.board, bf16[20,4,4,4,8,512]{5,4,3,2,1,0:T(8,128)(2,1)S(1)} %get-tuple-element.57.other), custom_call_target="tpu_custom_call" | custom-call | tf_op jit(solution)/shard_map/place_weights/pallas_call | solution.py:730
  (7 shorter events, 0.0 us)
Async XLA Ops:
  56.1 115.2 %copy-start.1 = (f32[4,8192]{1,0:T(4,128)S(1)}, f32[4,8192]{1,0:T(4,128)}, u32[]{:S(2)}) copy-start(f32[4,8192]{1,0:T(4,128)} %refs_0_.1) | copy-start | bytes 393220
  56.1 115.2 %copy-start.2 = (f32[64,512]{1,0:T(8,128)S(1)}, f32[64,512]{1,0:T(8,128)}, u32[]{:S(2)}) copy-start(f32[64,512]{1,0:T(8,128)} %refs_1_.1) | copy-start | bytes 393220
  56.2 115.2 %copy-start.3 = (f32[4,8192]{1,0:T(4,128)S(1)}, f32[4,8192]{1,0:T(4,128)}, u32[]{:S(2)}) copy-start(f32[4,8192]{1,0:T(4,128)} %refs_4_.1) | copy-start | bytes 393220
  56.2 115.2 %copy-start.4 = (f32[64,512]{1,0:T(8,128)S(1)}, f32[64,512]{1,0:T(8,128)}, u32[]{:S(2)}) copy-start(f32[64,512]{1,0:T(8,128)} %refs_5_.1) | copy-start | bytes 393220
  56.2 115.2 %copy-start.5 = (f32[4,8192]{1,0:T(4,128)S(1)}, f32[4,8192]{1,0:T(4,128)}, u32[]{:S(2)}) copy-start(f32[4,8192]{1,0:T(4,128)} %refs_8_.1) | copy-start | bytes 393220
  56.2 115.2 %copy-start.6 = (f32[64,512]{1,0:T(8,128)S(1)}, f32[64,512]{1,0:T(8,128)}, u32[]{:S(2)}) copy-start(f32[64,512]{1,0:T(8,128)} %refs_9_.1) | copy-start | bytes 393220
  56.2 115.2 %copy-start.7 = (f32[4,2048]{1,0:T(4,128)S(1)}, f32[4,2048]{1,0:T(4,128)}, u32[]{:S(2)}) copy-start(f32[4,2048]{1,0:T(4,128)} %refs_2_.1) | copy-start | bytes 98308
  56.2 115.2 %copy-start.8 = (f32[16,512]{1,0:T(8,128)S(1)}, f32[16,512]{1,0:T(8,128)}, u32[]{:S(2)}) copy-start(f32[16,512]{1,0:T(8,128)} %refs_3_.1) | copy-start | bytes 98308
  56.2 115.1 %copy-start.9 = (f32[4,2048]{1,0:T(4,128)S(1)}, f32[4,2048]{1,0:T(4,128)}, u32[]{:S(2)}) copy-start(f32[4,2048]{1,0:T(4,128)} %refs_6_.1) | copy-start | bytes 98308
  56.2 115.1 %copy-start.10 = (f32[16,512]{1,0:T(8,128)S(1)}, f32[16,512]{1,0:T(8,128)}, u32[]{:S(2)}) copy-start(f32[16,512]{1,0:T(8,128)} %refs_7_.1) | copy-start | bytes 98308
  56.3 115.1 %copy-start.11 = (f32[4,2048]{1,0:T(4,128)S(1)}, f32[4,2048]{1,0:T(4,128)}, u32[]{:S(2)}) copy-start(f32[4,2048]{1,0:T(4,128)} %refs_10_.1) | copy-start | bytes 98308
  56.3 115.1 %copy-start.12 = (f32[16,512]{1,0:T(8,128)S(1)}, f32[16,512]{1,0:T(8,128)}, u32[]{:S(2)}) copy-start(f32[16,512]{1,0:T(8,128)} %refs_11_.1) | copy-start | bytes 98308
  171.4 1.0 copy-start
